TPU v7x, 32 devices: a whole 2x2x4 slice. The times are simulated.
32 devices in a mesh: dp: 8 (over y, x, core), tensor: 4 (over z).
Axes of the slice: x: 2, y: 2, z: 4, core: 2. Of those that a mesh axis runs over, the one named last changes fastest.
Arguments:
- inputs: bfloat16 [12288, 768], P(('dp', 'tensor')), may hold values from -6 to 6
- segments: int32 [24, 512], P('dp'), may hold values from 0 to 3, never falling along the last dimension, each value on 1 to 256 neighbouring positions
- labels: int32 [24], P('dp'), may hold values from 0 to 2
- qkv_weight: bfloat16 [3, 768, 768], P(None, None, 'tensor'), may hold values from -0.21875 to 0.21875
- qv_bias: float32 [2, 768], P(None, 'tensor'), may hold values from -3 to 3
- out_weight: bfloat16 [768, 768], P('tensor'), may hold values from -0.875 to 0.875
- out_bias: float32 [768], replicated, may hold values from -3 to 3
- norm1_gain: float32 [768], replicated, may hold values from 0.5 to 1.5
- norm1_bias: float32 [768], replicated, may hold values from -3 to 3
- up_weight: bfloat16 [768, 3072], P(None, 'tensor'), may hold values from -0.21875 to 0.21875
- up_bias: float32 [3072], P('tensor'), may hold values from -3 to 3
- down_weight: bfloat16 [3072, 768], P('tensor'), may hold values from -0.109375 to 0.109375
- down_bias: float32 [768], replicated, may hold values from -3 to 3
- norm2_gain: float32 [768], replicated, may hold values from 0.5 to 1.5
- norm2_bias: float32 [768], replicated, may hold values from -3 to 3
- pool_weight: bfloat16 [768, 768], replicated, may hold values from -0.21875 to 0.21875
- pool_bias: float32 [768], replicated, may hold values from -3 to 3
- class_weight: bfloat16 [768, 3], replicated, may hold values from -0.4375 to 0.4375
- class_bias: float32 [3], replicated, may hold values from -4 to 4
- cotangent: bfloat16 [12288, 768], P(('dp', 'tensor')), may hold values from -6 to 6
Outputs:
- hidden: bfloat16 [12288, 768], P(('dp', 'tensor'))
- input_grad: bfloat16 [12288, 768], P(('dp', 'tensor'))
- qkv_weight_grad: float32 [3, 768, 768], P(None, 'dp', 'tensor')
- qv_bias_grad: float32 [2, 768], P(None, 'tensor')
- out_weight_grad: float32 [768, 768], P('tensor', 'dp')
- out_bias_grad: float32 [768], replicated
- norm1_gain_grad: float32 [768], replicated
- norm1_bias_grad: float32 [768], replicated
- up_weight_grad: float32 [768, 3072], P('dp', 'tensor')
- up_bias_grad: float32 [3072], P('tensor')
- down_weight_grad: float32 [3072, 768], P('tensor', 'dp')
- down_bias_grad: float32 [768], replicated
- norm2_gain_grad: float32 [768], replicated
- norm2_bias_grad: float32 [768], replicated
- pool_weight_grad: float32 [768, 768], replicated
- pool_bias_grad: float32 [768], replicated
- class_weight_grad: float32 [768, 3], replicated
- class_bias_grad: float32 [3], replicated
Inputs may be any that keep to these rules, and one draw needn't show every extreme that they name: `segments`: along each packed row of 512 tokens the ids never fall; a document holds at most half of 512 tokens.
All inputs are finite; a program needn't handle non-finite values.
Results may differ from a plain program's by a relative error of at most 0.017.
The roundings to bfloat16 on the way count: a program that leaves them out, or rounds other values in their place, can miss the bound.
Values may be sent and summed in bfloat16 or wider, within the bound.
A program may use at most 128 MiB of HBM per device.

v0:
```python
from functools import partial

import jax
import jax.numpy as jnp
from jax import lax
from jax.sharding import PartitionSpec as P

HEAD = 64


epsilon = 1e-12
masked_value = -1e30


def norm_forward(values, norm_gain, norm_shift):
    centre = values - jnp.mean(values, axis=-1, keepdims=True)
    inverse = lax.rsqrt(jnp.mean(centre * centre, axis=-1, keepdims=True) + epsilon)
    normed = centre * inverse
    return (normed * norm_gain + norm_shift, normed, inverse)


def norm_backward(grad_out, normed, inverse, norm_gain):
    scaled = grad_out * norm_gain
    grad_in = inverse * (
        scaled
        - jnp.mean(scaled, axis=-1, keepdims=True)
        - normed * jnp.mean(scaled * normed, axis=-1, keepdims=True)
    )
    return (grad_in, jnp.sum(grad_out * normed, axis=0), jnp.sum(grad_out, axis=0))


def split_heads(rows):
    return rows.reshape(rows.shape[0], rows.shape[1] // HEAD, HEAD)


def masked_scores(query_heads, key_heads, segment_row):
    raw_scores = jnp.einsum(
        "qhe,khe->hqk", query_heads, key_heads, preferred_element_type=jnp.float32
    ) * HEAD ** (-0.5)
    allowed = segment_row[:, None] == segment_row[None, :]
    return (jnp.where(allowed[None], raw_scores, masked_value), allowed)


def attend_sequence(block_items):
    query_seq, key_seq, value_seq, segment_row = block_items
    scores, allowed = masked_scores(split_heads(query_seq), split_heads(key_seq), segment_row)
    largest = jnp.max(scores, axis=-1, keepdims=True)
    exponent = jnp.exp(scores - largest)
    row_total = jnp.sum(exponent, axis=-1, keepdims=True)
    soft_low = (exponent / row_total).astype(jnp.bfloat16)
    context = jnp.einsum(
        "hqk,khe->qhe", soft_low, split_heads(value_seq), preferred_element_type=jnp.float32
    )
    context = context.reshape(query_seq.shape).astype(jnp.bfloat16)
    return (context, largest[..., 0] + jnp.log(row_total[..., 0]))


def attend_backward(block_items):
    query_seq, key_seq, value_seq, segment_row, log_total, grad_context = block_items
    query_heads = split_heads(query_seq)
    key_heads = split_heads(key_seq)
    value_heads = split_heads(value_seq)
    grad_heads = split_heads(grad_context)
    scores, allowed = masked_scores(query_heads, key_heads, segment_row)
    soft_probs = jnp.exp(scores - log_total[..., None])
    grad_values = jnp.einsum(
        "hqk,qhe->khe",
        soft_probs.astype(jnp.bfloat16),
        grad_heads,
        preferred_element_type=jnp.float32,
    )
    grad_soft = jnp.einsum(
        "qhe,khe->hqk", grad_heads, value_heads, preferred_element_type=jnp.float32
    )
    grad_scores = soft_probs * (grad_soft - jnp.sum(soft_probs * grad_soft, axis=-1, keepdims=True))
    grad_low = jnp.where(allowed[None], grad_scores, 0.0).astype(jnp.bfloat16)
    score_scale = HEAD ** (-0.5)
    grad_queries = (
        jnp.einsum("hqk,khe->qhe", grad_low, key_heads, preferred_element_type=jnp.float32)
        * score_scale
    )
    grad_keys = (
        jnp.einsum("hqk,qhe->khe", grad_low, query_heads, preferred_element_type=jnp.float32)
        * score_scale
    )
    full_shape = query_seq.shape
    return (
        grad_queries.reshape(full_shape).astype(jnp.bfloat16),
        grad_keys.reshape(full_shape).astype(jnp.bfloat16),
        grad_values.reshape(full_shape).astype(jnp.bfloat16),
    )


def body(
    inputs,
    segments,
    labels,
    qkv_weight,
    qv_bias,
    out_weight,
    out_bias,
    norm1_gain,
    norm1_bias,
    up_weight,
    up_bias,
    down_weight,
    down_bias,
    norm2_gain,
    norm2_bias,
    pool_weight,
    pool_bias,
    class_weight,
    class_bias,
    cotangent,
):
    share_rows = inputs.shape[0]
    seq_count, seq_length = segments.shape
    offset = lax.axis_index("tensor") * share_rows

    def take_share(array):
        return lax.dynamic_slice_in_dim(array, offset, share_rows, 0)

    gathered = lax.all_gather(inputs, "tensor", axis=0, tiled=True)
    group_rows = gathered.shape[0]
    projected = jnp.einsum("td,kde->kte", gathered, qkv_weight, preferred_element_type=jnp.float32)
    queries = (projected[0] + qv_bias[0]).astype(jnp.bfloat16)
    key_rows = projected[1].astype(jnp.bfloat16)
    value_rows = (projected[2] + qv_bias[1]).astype(jnp.bfloat16)
    local_width = queries.shape[1]

    def by_sequence(rows):
        return rows.reshape(seq_count, seq_length, rows.shape[-1])

    context, log_totals = lax.map(
        attend_sequence,
        (by_sequence(queries), by_sequence(key_rows), by_sequence(value_rows), segments),
    )
    context = context.reshape(group_rows, local_width)
    attended_all = (
        lax.psum(jnp.dot(context, out_weight, preferred_element_type=jnp.float32), "tensor")
        + out_bias
    )
    first_whole, normed_whole, inverse_whole = norm_forward(
        gathered.astype(jnp.float32) + attended_all, norm1_gain, norm1_bias
    )
    first_all = first_whole.astype(jnp.bfloat16)
    normed_one = take_share(normed_whole)
    inverse_one = take_share(inverse_whole)
    up_pre = jnp.dot(first_all, up_weight, preferred_element_type=jnp.float32) + up_bias
    gelu_exact = partial(jax.nn.gelu, approximate=False)
    active = gelu_exact(up_pre).astype(jnp.bfloat16)
    ffn_all = (
        lax.psum(jnp.dot(active, down_weight, preferred_element_type=jnp.float32), "tensor")
        + down_bias
    )
    final_whole, normed_all, inverse_all = norm_forward(
        first_whole + ffn_all, norm2_gain, norm2_bias
    )
    final_norm = take_share(final_whole)
    normed_two = take_share(normed_all)
    inverse_two = take_share(inverse_all)
    positions = offset + jnp.arange(share_rows, dtype=jnp.int32)
    row_starts = jnp.arange(seq_count, dtype=jnp.int32) * seq_length
    selector = (row_starts[:, None] == positions[None, :]).astype(jnp.float32)
    leading_part = jnp.dot(selector, final_norm, precision=lax.Precision.HIGHEST)
    leading = lax.psum(leading_part, "tensor").astype(jnp.bfloat16)
    pooled = jnp.tanh(jnp.dot(leading, pool_weight, preferred_element_type=jnp.float32) + pool_bias)
    pooled_low = pooled.astype(jnp.bfloat16)
    logits = jnp.dot(pooled_low, class_weight, preferred_element_type=jnp.float32) + class_bias
    chosen = (
        labels[:, None] == jnp.arange(class_weight.shape[1], dtype=jnp.int32)[None, :]
    ).astype(jnp.float32)
    grad_logits = (jax.nn.softmax(logits, axis=-1) - chosen).astype(jnp.bfloat16)
    class_weight_grad = jnp.einsum(
        "rd,rc->dc", pooled_low, grad_logits, preferred_element_type=jnp.float32
    )
    class_bias_grad = jnp.sum(grad_logits.astype(jnp.float32), axis=0)
    grad_pre = (
        jnp.einsum("rc,dc->rd", grad_logits, class_weight, preferred_element_type=jnp.float32)
        * (1.0 - pooled * pooled)
    ).astype(jnp.bfloat16)
    pool_weight_grad = jnp.einsum(
        "rd,re->de", leading, grad_pre, preferred_element_type=jnp.float32
    )
    pool_bias_grad = jnp.sum(grad_pre.astype(jnp.float32), axis=0)
    grad_leading = jnp.einsum(
        "re,de->rd", grad_pre, pool_weight, preferred_element_type=jnp.float32
    )
    grad_final = cotangent.astype(jnp.float32) + jnp.einsum(
        "rt,rd->td", selector, grad_leading, precision=lax.Precision.HIGHEST
    )
    grad_second, norm2_gain_grad, norm2_bias_grad = norm_backward(
        grad_final, normed_two, inverse_two, norm2_gain
    )
    grad_fed = grad_second.astype(jnp.bfloat16)
    down_bias_grad = jnp.sum(grad_fed.astype(jnp.float32), axis=0)
    grad_fed_all = lax.all_gather(grad_fed, "tensor", axis=0, tiled=True)
    down_weight_grad = jnp.einsum(
        "tf,td->fd", active, grad_fed_all, preferred_element_type=jnp.float32
    )
    grad_active = jnp.einsum(
        "td,fd->tf", grad_fed_all, down_weight, preferred_element_type=jnp.float32
    )
    grad_up = jax.vjp(gelu_exact, up_pre)[1](grad_active)[0].astype(jnp.bfloat16)
    up_bias_grad = jnp.sum(grad_up.astype(jnp.float32), axis=0)
    up_weight_grad = jnp.einsum("td,tf->df", first_all, grad_up, preferred_element_type=jnp.float32)
    grad_first = (
        lax.psum_scatter(
            jnp.einsum("tf,df->td", grad_up, up_weight, preferred_element_type=jnp.float32),
            "tensor",
            scatter_dimension=0,
            tiled=True,
        )
        + grad_second
    )
    grad_res, norm1_gain_grad, norm1_bias_grad = norm_backward(
        grad_first, normed_one, inverse_one, norm1_gain
    )
    grad_att = grad_res.astype(jnp.bfloat16)
    out_bias_grad = jnp.sum(grad_att.astype(jnp.float32), axis=0)
    grad_att_all = lax.all_gather(grad_att, "tensor", axis=0, tiled=True)
    out_weight_grad = jnp.einsum(
        "te,td->ed", context, grad_att_all, preferred_element_type=jnp.float32
    )
    grad_context = jnp.einsum(
        "td,ed->te", grad_att_all, out_weight, preferred_element_type=jnp.float32
    ).astype(jnp.bfloat16)
    grad_queries, grad_keys, grad_values = lax.map(
        attend_backward,
        (
            by_sequence(queries),
            by_sequence(key_rows),
            by_sequence(value_rows),
            segments,
            log_totals,
            by_sequence(grad_context),
        ),
    )
    stacked = jnp.stack(
        [
            grad_queries.reshape(group_rows, local_width),
            grad_keys.reshape(group_rows, local_width),
            grad_values.reshape(group_rows, local_width),
        ]
    )
    qkv_weight_grad = jnp.einsum(
        "td,kte->kde", gathered, stacked, preferred_element_type=jnp.float32
    )
    qv_bias_grad = jnp.stack(
        [
            jnp.sum(stacked[0].astype(jnp.float32), axis=0),
            jnp.sum(stacked[2].astype(jnp.float32), axis=0),
        ]
    )
    input_grad = (
        lax.psum_scatter(
            jnp.einsum(
                "kte,kde->td", stacked, qkv_weight, preferred_element_type=jnp.float32
            ).astype(jnp.bfloat16),
            "tensor",
            scatter_dimension=0,
            tiled=True,
        ).astype(jnp.float32)
        + grad_res
    ).astype(jnp.bfloat16)
    qkv_sum, out_sum, up_sum, down_sum = (
        lax.psum_scatter(qkv_weight_grad, "dp", scatter_dimension=1, tiled=True),
        lax.psum_scatter(out_weight_grad, "dp", scatter_dimension=1, tiled=True),
        lax.psum_scatter(up_weight_grad, "dp", scatter_dimension=0, tiled=True),
        lax.psum_scatter(down_weight_grad, "dp", scatter_dimension=1, tiled=True),
    )
    token_grads = lax.psum(
        (
            out_bias_grad,
            norm1_gain_grad,
            norm1_bias_grad,
            down_bias_grad,
            norm2_gain_grad,
            norm2_bias_grad,
        ),
        ("dp", "tensor"),
    )
    group_grads = lax.psum(
        (
            qv_bias_grad,
            up_bias_grad,
            pool_weight_grad,
            pool_bias_grad,
            class_weight_grad,
            class_bias_grad,
        ),
        "dp",
    )
    return (
        final_norm.astype(jnp.bfloat16),
        input_grad,
        qkv_sum,
        group_grads[0],
        out_sum,
        token_grads[0],
        token_grads[1],
        token_grads[2],
        up_sum,
        group_grads[1],
        down_sum,
        token_grads[3],
        token_grads[4],
        token_grads[5],
        group_grads[2],
        group_grads[3],
        group_grads[4],
        group_grads[5],
    )


def solution(mesh):
    placed = (
        P(("dp", "tensor"), None),
        P("dp", None),
        P("dp"),
        P(None, None, "tensor"),
        P(None, "tensor"),
        P("tensor", None),
        P(),
        P(),
        P(),
        P(None, "tensor"),
        P("tensor"),
        P("tensor", None),
        P(),
        P(),
        P(),
        P(),
        P(),
        P(),
        P(),
        P(("dp", "tensor"), None),
    )
    return jax.shard_map(
        body,
        mesh=mesh,
        in_specs=placed,
        out_specs=(
            P(("dp", "tensor"), None),
            P(("dp", "tensor"), None),
            P(None, "dp", "tensor"),
            P(None, "tensor"),
            P("tensor", "dp"),
            P(),
            P(),
            P(),
            P("dp", "tensor"),
            P("tensor"),
            P("tensor", "dp"),
            P(),
            P(),
            P(),
            P(),
            P(),
            P(),
            P(),
        ),
        check_vma=False,
    )
```

profile of v0, /device:TPU:0, one launch (start us, length us, event | category | flops | bytes accessed | tf_op | source)
XLA Modules:
  0.0 1093.6 jit_solution(14431650405853245202)
XLA Ops:
  8.8 53.6 %all-gather.4.cloned.1.call-done = bf16[1536,768]{1,0:T(8,128)(2,1)} async-done(((bf16[384,768]{1,0:T(8,128)(2,1)}), bf16[1536,768]{1,0:T(8,128)(2,1)}) %all-gather.4.cloned.1.call-update) | async-done | bytes 2359312 | tf_op jit(solution)/shard_map/all_gather | solution.py:123
  76.6 12.6 %while.26 = (s32[]{:T(128)}, bf16[3,512,192]{1,2,0:T(8,128)(2,1)S(1)}, f32[3,3,512]{2,1,0:T(4,128)}, bf16[3,512,192]{1,2,0:T(8,128)(2,1)S(1)}, s32[3,512]{1,0:T(...) while((s32[]{:T(128)}, bf16[3,512,192]{1,2,0:T(8,128)(2,1)S(1)}, ...), condition=%wide.region_3.4_spmd, body=%wide.region_0.3_spmd.sunk | while | flops 211122688 | bytes 12902513 | solution.py:134
  94.7 170.7 %all-reduce.6.cloned.1.call-done = f32[1536,768]{1,0:T(8,128)} async-done(((f32[1536,768]{1,0:T(8,128)}), f32[1536,768]{1,0:T(8,128)}) %all-reduce.6.cloned.1.call-update) | async-done | bytes 4718608 | tf_op jit(solution)/shard_map/psum | solution.py:140
  272.2 13.3 %multiply_convert_fusion = (bf16[1536,768]{1,0:T(8,128)(2,1)S(1)}, f32[1536,768]{1,0:T(8,128)}, f32[1536,768]{1,0:T(8,128)}) fusion(f32[768]{0:T(1024)S(1)} %copy-done.40, bf16[768,768]{1,0:T(8,128)(2,1)S(1)} %copy-done, f32[1536,768]{1,0:T(8,128)S(1)} %subtract_multiply_fusion.1, f32[768]{0:T(1024)S(1)} %copy-done.35, f32[768]{0:T(1024)S(1)} %copy-done.22), kind=kOutput, calls=%fused_computation.53 | convolution fusion | flops 1893335040 | bytes 17703936 | tf_op jit(solution)/shard_map/dot_general | solution.py:149
  291.2 171.0 %all-reduce.8.cloned.1.call-done = f32[1536,768]{1,0:T(8,128)} async-done(((f32[1536,768]{1,0:T(8,128)}), f32[1536,768]{1,0:T(8,128)}) %all-reduce.8.cloned.1.call-update) | async-done | bytes 4718608 | tf_op jit(solution)/shard_map/psum | solution.py:153
  470.8 16.4 %psum.107 = bf16[3,768]{1,0:T(4,128)(2,1)S(1)} all-reduce(f32[3,768]{1,0:T(4,128)S(1)} %fusion.56), channel_id=1, replica_groups=mesh['dp'=8,'tensor'=4] {'tensor'}, use_global_device_ids=true, to_apply=%region_10.11 | all-reduce | flops 2304 | bytes 13824 | tf_op jit(solution)/shard_map/psum | solution.py:166
  495.9 48.2 %all-gather.6.cloned.1.call-done = bf16[1536,768]{1,0:T(8,128)(2,1)} async-done(((bf16[384,768]{1,0:T(8,128)(2,1)}), bf16[1536,768]{1,0:T(8,128)(2,1)}) %all-gather.6.cloned.1.call-update) | async-done | bytes 2359312 | tf_op jit(solution)/shard_map/all_gather | solution.py:197
  544.1 8.8 convert_reduce_fusion
  559.5 83.4 %reduce-scatter.11.cloned.1.call-done = f32[384,768]{1,0:T(8,128)} async-done(((f32[1536,768]{1,0:T(8,128)}), f32[384,768]{1,0:T(8,128)}) %reduce-scatter.11.cloned.1.call-update) | async-done | bytes 1179664 | tf_op jit(solution)/shard_map/reduce_scatter | solution.py:208
  651.4 50.2 %all-gather.8.cloned.1.call-done = bf16[1536,768]{1,0:T(8,128)(2,1)} async-done(((bf16[384,768]{1,0:T(8,128)(2,1)}), bf16[1536,768]{1,0:T(8,128)(2,1)}) %all-gather.8.cloned.1.call-update) | async-done | bytes 2359312 | tf_op jit(solution)/shard_map/all_gather | solution.py:221
  706.1 75.7 %while.27 = (s32[]{:T(128)}, bf16[3,512,192]{1,2,0:T(8,128)(2,1)S(1)}, bf16[3,512,192]{1,2,0:T(8,128)(2,1)}, bf16[3,512,192]{1,2,0:T(8,128)(2,1)S(1)}, bf16[3,51...) while((s32[]{:T(128)}, ...), condition=%wide.region_20.21_spmd, body=%wide.region_18.20_spmd.sunk | while | flops 515084288 | bytes 27811988 | solution.py:228
  724.8 5.8 fusion.178
  741.7 5.8 fusion.176
  750.0 5.8 fusion.178
  767.0 5.8 fusion.176
  775.3 5.8 fusion.178
  821.7 6.6 fusion.58
  828.4 5.9 fusion.96
  835.9 40.0 %all-reduce = (f32[768]{0:T(1024)}, f32[768]{0:T(1024)}, f32[768]{0:T(1024)}, f32[768]{0:T(1024)}, f32[768]{0:T(1024)}, /*index=5*/f32[768]{0:T(1024)}) all-reduce(f32[768]{0:T(1024)} %get-tuple-element.275, f32[768]{0:T(1024)} %get-tuple-element.222, ...), channel_id=1, replica_groups=mesh['dp'=8,'tensor'=4] {'dp','tensor'}, use_global_device_ids=true, to_apply=%region_28.29 | all-reduce | flops 4608 | bytes 36864 | tf_op jit(solution)/shard_map/psum | solution.py:272
  876.3 25.2 %all-reduce.1 = (f32[2,192]{1,0:T(2,128)}, f32[768]{0:T(1024)}, f32[768]{0:T(1024)}, f32[768,3]{0,1:T(4,128)}, f32[3]{0:T(128)}) all-reduce(f32[2,192]{1,0:T(2,128)S(1)} %pad_maximum_fusion, f32[768]{0:T(1024)} %get-tuple-element.279, f32[768]{0:T(1024)} %get-tuple-element.301, ...), channel_id=1, replica_groups=mesh['dp'=8,'tensor'=4] {'dp'}, use_global_device_ids=true, to_apply=%region_25.26 | all-reduce | flops 4227 | bytes 33816 | tf_op jit(solution)/shard_map/psum | solution.py:283
  905.0 21.0 %reduce-scatter.13.cloned.1.call-done = bf16[384,768]{1,0:T(8,128)(2,1)} async-done(((bf16[1536,768]{1,0:T(8,128)(2,1)}), bf16[384,768]{1,0:T(8,128)(2,1)}) %reduce-scatter.13.cloned.1.call-update) | async-done | bytes 589840 | tf_op jit(solution)/shard_map/reduce_scatter | solution.py:256
  928.7 62.9 %all-reduce.10.cloned.1.call-done = f32[768,768]{1,0:T(8,128)} async-done(((f32[768,768]{1,0:T(8,128)}), f32[768,768]{1,0:T(8,128)}) %all-reduce.10.cloned.1.call-update) | async-done | bytes 2359312 | tf_op jit(solution)/shard_map/psum | solution.py:283
  991.6 45.7 %reduce-scatter.15.cloned.1.call-done = f32[96,768]{1,0:T(8,128)} async-done(((f32[768,768]{1,0:T(8,128)}), f32[96,768]{1,0:T(8,128)}) %reduce-scatter.15.cloned.1.call-update) | async-done | bytes 294928 | tf_op jit(solution)/shard_map/reduce_scatter | solution.py:269
  1037.2 46.2 %reduce-scatter.17.cloned.1.call-done = f32[768,96]{0,1:T(8,128)} async-done(((f32[768,768]{0,1:T(8,128)}), f32[768,96]{0,1:T(8,128)}) %reduce-scatter.17.cloned.1.call-update) | async-done | bytes 294928 | tf_op jit(solution)/shard_map/reduce_scatter | solution.py:270
  (255 shorter events, 180.4 us)
Async XLA Ops:
  7.2 264.9 %copy-start = (bf16[768,768]{1,0:T(8,128)(2,1)S(1)}, bf16[768,768]{1,0:T(8,128)(2,1)}, u32[]{:S(2)}) copy-start(bf16[768,768]{1,0:T(8,128)(2,1)} %param.33) | copy-start | bytes 3538948
  7.2 55.1 %all-gather.4.cloned.1.call-start = ((), (), s32[]{:S(2)}) async-start(), calls=%async_computation.6 | async-start | bytes 2949120 | tf_op jit(solution)/shard_map/all_gather | solution.py:123
  7.9 257.5 %all-reduce.6.cloned.1.call-start = ((), (), s32[]{:S(2)}) async-start(), calls=%async_computation.7 | async-start | bytes 9437184 | tf_op jit(solution)/shard_map/psum | solution.py:140
  94.5 170.9 %copy-start.3 = (bf16[1536,768]{1,0:T(8,128)(2,1)S(1)}, bf16[1536,768]{1,0:T(8,128)(2,1)}, u32[]{:S(2)}) copy-start(bf16[1536,768]{1,0:T(8,128)(2,1)} %all-gather.4.cloned.1.call-done) | copy-start | bytes 7077892
  94.5 170.9 %copy-start.26 = (f32[768]{0:T(1024)S(1)}, f32[768]{0:T(1024)}, u32[]{:S(2)}) copy-start(f32[768]{0:T(1024)} %param.30) | copy-start | bytes 9220
  94.5 367.7 %all-reduce.8.cloned.1.call-start = ((), (), s32[]{:S(2)}) async-start(), calls=%async_computation.8 | async-start | bytes 9437184 | tf_op jit(solution)/shard_map/psum | solution.py:153
  291.1 171.1 %copy-start.33 = (f32[768]{0:T(1024)S(1)}, f32[768]{0:T(1024)}, u32[]{:S(2)}) copy-start(f32[768]{0:T(1024)} %param.36) | copy-start | bytes 9220
  291.1 253.0 %all-gather.6.cloned.1.call-start = ((), (), s32[]{:S(2)}) async-start(), calls=%async_computation.9 | async-start | bytes 2949120 | tf_op jit(solution)/shard_map/all_gather | solution.py:197
  489.6 54.5 %copy-start.41 = (f32[768]{0:T(1024)S(1)}, f32[768]{0:T(1024)}, u32[]{:S(2)}) copy-start(f32[768]{0:T(1024)} %param.34) | copy-start | bytes 9220
  495.6 147.2 %reduce-scatter.11.cloned.1.call-start = ((), (), s32[]{:S(2)}) async-start(), calls=%async_computation.10 | async-start | bytes 5898240 | tf_op jit(solution)/shard_map/reduce_scatter | solution.py:208
  558.6 143.0 %all-gather.8.cloned.1.call-start = ((), (), s32[]{:S(2)}) async-start(), calls=%async_computation.11 | async-start | bytes 2949120 | tf_op jit(solution)/shard_map/all_gather | solution.py:221
  559.5 87.5 %copy-start.29 = (f32[384]{0:T(512)}, f32[384]{0:T(512)S(1)}, u32[]{:S(2)}) copy-start(f32[384]{0:T(512)S(1)} %dynamic-slice.6) | copy-start | bytes 4612
  647.0 54.7 %copy-start.19 = (bf16[192,768]{1,0:T(8,128)(2,1)S(1)}, bf16[192,768]{1,0:T(8,128)(2,1)}, u32[]{:S(2)}) copy-start(bf16[192,768]{1,0:T(8,128)(2,1)} %param.29) | copy-start | bytes 884740
  647.0 57.3 %copy-start.30 = (f32[384]{0:T(512)}, f32[384]{0:T(512)S(1)}, u32[]{:S(2)}) copy-start(f32[384]{0:T(512)S(1)} %broadcast_multiply_fusion.2) | copy-start | bytes 4612
  647.0 57.3 %copy-start.31 = (f32[384]{0:T(512)}, f32[384]{0:T(512)S(1)}, u32[]{:S(2)}) copy-start(f32[384]{0:T(512)S(1)} %broadcast_multiply_fusion.3) | copy-start | bytes 4612
  651.0 250.5 %reduce-scatter.21.cloned.1.call-start = ((), (), s32[]{:S(2)}) async-start(), calls=%async_computation.17 | async-start | bytes 884736
  797.5 105.6 %reduce-scatter.19.cloned.1.call-start = ((), (), s32[]{:S(2)}) async-start(), calls=%async_computation.16 | async-start | bytes 2211840
  814.7 111.3 %reduce-scatter.13.cloned.1.call-start = ((), (), s32[]{:S(2)}) async-start(), calls=%async_computation.12 | async-start | bytes 2949120 | tf_op jit(solution)/shard_map/reduce_scatter | solution.py:256
  819.6 172.0 %all-reduce.10.cloned.1.call-start = ((), (), s32[]{:S(2)}) async-start(), calls=%async_computation.15 | async-start | bytes 4718592 | tf_op jit(solution)/shard_map/psum | solution.py:283
  821.7 215.6 %reduce-scatter.15.cloned.1.call-start = ((), (), s32[]{:S(2)}) async-start(), calls=%async_computation.13 | async-start | bytes 2654208 | tf_op jit(solution)/shard_map/reduce_scatter | solution.py:269
  828.4 47.6 %copy-start.14 = (bf16[3,512,192]{1,2,0:T(8,128)(2,1)S(1)}, bf16[3,512,192]{1,2,0:T(8,128)(2,1)}, u32[]{:S(2)}) copy-start(bf16[3,512,192]{1,2,0:T(8,128)(2,1)} %copy-done.13) | copy-start | bytes 1769476
  828.4 255.0 %reduce-scatter.17.cloned.1.call-start = ((), (), s32[]{:S(2)}) async-start(), calls=%async_computation.14 | async-start | bytes 2654208 | tf_op jit(solution)/shard_map/reduce_scatter | solution.py:270
  834.4 41.8 %copy-start.12 = (bf16[3,512,192]{1,2,0:T(8,128)(2,1)S(1)}, bf16[3,512,192]{1,2,0:T(8,128)(2,1)}, u32[]{:S(2)}) copy-start(bf16[3,512,192]{1,2,0:T(8,128)(2,1)} %copy-done.11) | copy-start | bytes 1769476
  834.4 91.7 %copy-start.10 = (f32[384,768]{1,0:T(8,128)S(1)}, f32[384,768]{1,0:T(8,128)}, u32[]{:S(2)}) copy-start(f32[384,768]{1,0:T(8,128)} %copy-done.9) | copy-start | bytes 3538948
  (33 other events, 230.5 us)
Sparse Core Ops, SparseCore 0:
  9.6 52.6 all-gather.3
  94.6 170.7 all-reduce.5
  291.2 170.9 all-reduce.7
  495.7 48.3 all-gather.5
  558.7 84.0 reduce-scatter.10
  651.1 50.4 all-gather.7
  797.7 33.6 reduce-scatter.20
  834.8 40.5 reduce-scatter.18
  878.3 47.6 reduce-scatter.12
  929.2 62.3 all-reduce.9
  995.5 41.6 reduce-scatter.14
  1041.0 42.3 reduce-scatter.16
where the time goes:
time: 1100 us; the launch traced here: 1090 us
  waiting for transfers between devices  754 us (69%)
  matrix products  137 us (12%)
  blocking collectives  81.6 us (7%)
  local copies, waits for them, and re-layouts  73.4 us (7%)
  other arithmetic  31 us (3%)
  between operations  15 us (1%)
    psum x1, waiting for transfers between devices, body(): lax.psum(jnp.dot(active, down_weight, preferred_element_type=jnp.float32)...  171 us
    psum x1, waiting for transfers between devices, body(): lax.psum(jnp.dot(context, out_weight, preferred_element_type=jnp.float32)...  171 us
    reduce_scatter x1, waiting for transfers between devices, body(): lax.psum_scatter(jnp.einsum('tf,df->td', grad_up, up_weight, preferred_el...  83.4 us
    psum x1, waiting for transfers between devices, body(): lax.psum((qv_bias_grad, up_bias_grad, pool_weight_grad, pool_bias_grad, c...  62.9 us
    all_gather x1, waiting for transfers between devices, body(): gathered = lax.all_gather(inputs, 'tensor', axis=0, tiled=True)  53.6 us
    all_gather x1, waiting for transfers between devices, body(): grad_att_all = lax.all_gather(grad_att, 'tensor', axis=0, tiled=True)  50.2 us
    all_gather x1, waiting for transfers between devices, body(): grad_fed_all = lax.all_gather(grad_fed, 'tensor', axis=0, tiled=True)  48.2 us
    reduce_scatter x1, waiting for transfers between devices, body(): lax.psum_scatter(down_weight_grad, 'dp', scatter_dimension=1, tiled=True)  46.2 us
  transfers between devices with their start and end apart: 12, of which 10 were waited for; matrix products, arithmetic and copies ran while one was open for 4% of the time, Pallas kernels for 0%

commit v1 on v0

v1 whole, which is shorter than its diff:
```python
from functools import partial

import jax
import jax.numpy as jnp
from jax import lax
from jax.sharding import PartitionSpec as P

HEAD = 64


epsilon = 1e-12
masked_value = -1e30


def norm_forward(values, norm_gain, norm_shift):
    centre = values - jnp.mean(values, axis=-1, keepdims=True)
    inverse = lax.rsqrt(jnp.mean(centre * centre, axis=-1, keepdims=True) + epsilon)
    normed = centre * inverse
    return (normed * norm_gain + norm_shift, normed, inverse)


def norm_backward(grad_out, normed, inverse, norm_gain):
    scaled = grad_out * norm_gain
    grad_in = inverse * (
        scaled
        - jnp.mean(scaled, axis=-1, keepdims=True)
        - normed * jnp.mean(scaled * normed, axis=-1, keepdims=True)
    )
    return (grad_in, jnp.sum(grad_out * normed, axis=0), jnp.sum(grad_out, axis=0))


def split_heads(rows, seq_count):
    return rows.reshape(seq_count, rows.shape[0] // seq_count, rows.shape[1] // HEAD, HEAD)


def masked_scores(query_heads, key_heads, segments):
    raw_scores = jnp.einsum(
        "rqhe,rkhe->rhqk", query_heads, key_heads, preferred_element_type=jnp.float32
    ) * HEAD ** (-0.5)
    allowed = segments[:, None, :, None] == segments[:, None, None, :]
    return (jnp.where(allowed, raw_scores, masked_value), allowed)


def attend_forward(queries, key_rows, value_rows, segments):
    seq_count = segments.shape[0]
    scores, allowed = masked_scores(
        split_heads(queries, seq_count), split_heads(key_rows, seq_count), segments
    )
    largest = jnp.max(scores, axis=-1, keepdims=True)
    exponent = jnp.exp(scores - largest)
    row_total = jnp.sum(exponent, axis=-1, keepdims=True)
    soft_low = (exponent / row_total).astype(jnp.bfloat16)
    context = jnp.einsum(
        "rhqk,rkhe->rqhe",
        soft_low,
        split_heads(value_rows, seq_count),
        preferred_element_type=jnp.float32,
    )
    context = context.reshape(queries.shape).astype(jnp.bfloat16)
    return (context, largest + jnp.log(row_total))


def attend_backward(queries, key_rows, value_rows, segments, log_total, grad_context):
    seq_count = segments.shape[0]
    query_heads = split_heads(queries, seq_count)
    key_heads = split_heads(key_rows, seq_count)
    value_heads = split_heads(value_rows, seq_count)
    grad_heads = split_heads(grad_context, seq_count)
    scores, allowed = masked_scores(query_heads, key_heads, segments)
    soft_probs = jnp.exp(scores - log_total)
    grad_values = jnp.einsum(
        "rhqk,rqhe->rkhe",
        soft_probs.astype(jnp.bfloat16),
        grad_heads,
        preferred_element_type=jnp.float32,
    )
    grad_soft = jnp.einsum(
        "rqhe,rkhe->rhqk", grad_heads, value_heads, preferred_element_type=jnp.float32
    )
    grad_scores = soft_probs * (grad_soft - jnp.sum(soft_probs * grad_soft, axis=-1, keepdims=True))
    grad_low = jnp.where(allowed, grad_scores, 0.0).astype(jnp.bfloat16)
    score_scale = HEAD ** (-0.5)
    grad_queries = (
        jnp.einsum("rhqk,rkhe->rqhe", grad_low, key_heads, preferred_element_type=jnp.float32)
        * score_scale
    )
    grad_keys = (
        jnp.einsum("rhqk,rqhe->rkhe", grad_low, query_heads, preferred_element_type=jnp.float32)
        * score_scale
    )
    full_shape = queries.shape
    return (
        grad_queries.reshape(full_shape).astype(jnp.bfloat16),
        grad_keys.reshape(full_shape).astype(jnp.bfloat16),
        grad_values.reshape(full_shape).astype(jnp.bfloat16),
    )


def to_blocks(array, axis, count):
    shape = array.shape
    split = shape[:axis] + (count, shape[axis] // count) + shape[axis + 1 :]
    return jnp.moveaxis(array.reshape(split), axis, 0).reshape(count, -1)


def from_block(flat, shape, axis, count):
    local = shape[:axis] + (shape[axis] // count,) + shape[axis + 1 :]
    return flat.reshape(local)


def body(
    inputs,
    segments,
    labels,
    qkv_weight,
    qv_bias,
    out_weight,
    out_bias,
    norm1_gain,
    norm1_bias,
    up_weight,
    up_bias,
    down_weight,
    down_bias,
    norm2_gain,
    norm2_bias,
    pool_weight,
    pool_bias,
    class_weight,
    class_bias,
    cotangent,
):
    share_rows = inputs.shape[0]
    seq_count, seq_length = segments.shape
    tensor_index = lax.axis_index("tensor")
    dp_index = lax.axis_index("dp")
    tensor_count = lax.axis_size("tensor")
    dp_count = lax.axis_size("dp")
    offset = tensor_index * share_rows

    gathered = lax.all_gather(inputs, "tensor", axis=0, tiled=True)
    group_rows = gathered.shape[0]
    projected = jnp.einsum("td,kde->kte", gathered, qkv_weight, preferred_element_type=jnp.float32)
    queries = (projected[0] + qv_bias[0]).astype(jnp.bfloat16)
    key_rows = projected[1].astype(jnp.bfloat16)
    value_rows = (projected[2] + qv_bias[1]).astype(jnp.bfloat16)
    local_width = queries.shape[1]

    context, log_totals = attend_forward(queries, key_rows, value_rows, segments)
    attended = (
        lax.psum_scatter(
            jnp.dot(context, out_weight, preferred_element_type=jnp.float32),
            "tensor",
            scatter_dimension=0,
            tiled=True,
        )
        + out_bias
    )
    first_norm, normed_one, inverse_one = norm_forward(
        inputs.astype(jnp.float32) + attended, norm1_gain, norm1_bias
    )
    first_low = first_norm.astype(jnp.bfloat16)
    first_all = lax.all_gather(first_low, "tensor", axis=0, tiled=True)
    up_pre = jnp.dot(first_all, up_weight, preferred_element_type=jnp.float32) + up_bias
    gelu_exact = partial(jax.nn.gelu, approximate=False)
    active = gelu_exact(up_pre).astype(jnp.bfloat16)
    ffn_out = (
        lax.psum_scatter(
            jnp.dot(active, down_weight, preferred_element_type=jnp.float32),
            "tensor",
            scatter_dimension=0,
            tiled=True,
        )
        + down_bias
    )
    final_norm, normed_two, inverse_two = norm_forward(
        first_norm + ffn_out, norm2_gain, norm2_bias
    )

    positions = offset + jnp.arange(share_rows, dtype=jnp.int32)
    row_starts = jnp.arange(seq_count, dtype=jnp.int32) * seq_length
    selector = (row_starts[:, None] == positions[None, :]).astype(jnp.float32)
    owned = jnp.sum(selector, axis=1, keepdims=True)
    leading = jnp.dot(selector, final_norm, precision=lax.Precision.HIGHEST).astype(jnp.bfloat16)
    pooled = jnp.tanh(jnp.dot(leading, pool_weight, preferred_element_type=jnp.float32) + pool_bias)
    pooled_low = pooled.astype(jnp.bfloat16)
    logits = jnp.dot(pooled_low, class_weight, preferred_element_type=jnp.float32) + class_bias
    chosen = (
        labels[:, None] == jnp.arange(class_weight.shape[1], dtype=jnp.int32)[None, :]
    ).astype(jnp.float32)
    grad_logits = jnp.where(
        owned > 0, jax.nn.softmax(logits, axis=-1) - chosen, 0.0
    ).astype(jnp.bfloat16)
    grad_pre = (
        jnp.einsum("rc,dc->rd", grad_logits, class_weight, preferred_element_type=jnp.float32)
        * (1.0 - pooled * pooled)
    ).astype(jnp.bfloat16)
    grad_leading = jnp.einsum(
        "re,de->rd", grad_pre, pool_weight, preferred_element_type=jnp.float32
    )
    grad_final = cotangent.astype(jnp.float32) + jnp.einsum(
        "rt,rd->td", selector, grad_leading, precision=lax.Precision.HIGHEST
    )
    grad_second, norm2_gain_grad, norm2_bias_grad = norm_backward(
        grad_final, normed_two, inverse_two, norm2_gain
    )
    grad_fed = grad_second.astype(jnp.bfloat16)
    down_bias_grad = jnp.sum(grad_fed.astype(jnp.float32), axis=0)
    grad_fed_all = lax.all_gather(grad_fed, "tensor", axis=0, tiled=True)
    down_weight_grad = jnp.einsum(
        "tf,td->fd", active, grad_fed_all, preferred_element_type=jnp.float32
    )
    grad_active = jnp.einsum(
        "td,fd->tf", grad_fed_all, down_weight, preferred_element_type=jnp.float32
    )
    grad_up = jax.vjp(gelu_exact, up_pre)[1](grad_active)[0].astype(jnp.bfloat16)
    up_bias_grad = jnp.sum(grad_up.astype(jnp.float32), axis=0)
    up_weight_grad = jnp.einsum("td,tf->df", first_all, grad_up, preferred_element_type=jnp.float32)
    grad_first = (
        lax.psum_scatter(
            jnp.einsum("tf,df->td", grad_up, up_weight, preferred_element_type=jnp.float32),
            "tensor",
            scatter_dimension=0,
            tiled=True,
        )
        + grad_second
    )
    grad_res, norm1_gain_grad, norm1_bias_grad = norm_backward(
        grad_first, normed_one, inverse_one, norm1_gain
    )
    grad_att = grad_res.astype(jnp.bfloat16)
    out_bias_grad = jnp.sum(grad_att.astype(jnp.float32), axis=0)
    grad_att_all = lax.all_gather(grad_att, "tensor", axis=0, tiled=True)
    out_weight_grad = jnp.einsum(
        "te,td->ed", context, grad_att_all, preferred_element_type=jnp.float32
    )
    grad_context = jnp.einsum(
        "td,ed->te", grad_att_all, out_weight, preferred_element_type=jnp.float32
    ).astype(jnp.bfloat16)
    grad_queries, grad_keys, grad_values = attend_backward(
        queries, key_rows, value_rows, segments, log_totals, grad_context
    )
    stacked = jnp.stack([grad_queries, grad_keys, grad_values])
    qkv_weight_grad = jnp.einsum(
        "td,kte->kde", gathered, stacked, preferred_element_type=jnp.float32
    )
    qv_bias_grad = jnp.stack(
        [
            jnp.sum(grad_queries.astype(jnp.float32), axis=0),
            jnp.sum(grad_values.astype(jnp.float32), axis=0),
        ]
    )
    input_grad = (
        lax.psum_scatter(
            jnp.einsum(
                "kte,kde->td", stacked, qkv_weight, preferred_element_type=jnp.float32
            ).astype(jnp.bfloat16),
            "tensor",
            scatter_dimension=0,
            tiled=True,
        ).astype(jnp.float32)
        + grad_res
    ).astype(jnp.bfloat16)

    weight_parts = (
        (qkv_weight_grad, 1),
        (out_weight_grad, 1),
        (up_weight_grad, 0),
        (down_weight_grad, 1),
    )
    weight_flat = jnp.concatenate(
        [to_blocks(grad, axis, dp_count) for grad, axis in weight_parts], axis=1
    )
    lanes = 1024 if weight_flat.shape[1] % 1024 == 0 else 128
    weight_sum = lax.psum_scatter(
        weight_flat.reshape(-1, lanes), "dp", scatter_dimension=0, tiled=True
    ).reshape(-1)
    weight_out = []
    start = 0
    for grad, axis in weight_parts:
        size = grad.size // dp_count
        weight_out.append(from_block(weight_sum[start : start + size], grad.shape, axis, dp_count))
        start += size

    def slot(values, index, count):
        holder = jnp.zeros((count,) + values.shape, values.dtype)
        return lax.dynamic_update_slice(holder, values[None], (index,) + (0,) * values.ndim)

    row_block = jnp.concatenate(
        [
            leading.astype(jnp.float32) * owned,
            grad_pre.astype(jnp.float32),
            pooled_low.astype(jnp.float32) * owned,
            grad_logits.astype(jnp.float32),
        ],
        axis=1,
    )
    small_parts = [
        jnp.stack(
            [
                out_bias_grad,
                norm1_gain_grad,
                norm1_bias_grad,
                down_bias_grad,
                norm2_gain_grad,
                norm2_bias_grad,
            ]
        ),
        slot(qv_bias_grad, tensor_index, tensor_count),
        slot(up_bias_grad, tensor_index, tensor_count),
        slot(row_block, dp_index, dp_count),
    ]
    small_flat = jnp.concatenate([part.reshape(-1) for part in small_parts])
    small_sum = lax.psum(small_flat, ("dp", "tensor"))
    small_out = []
    start = 0
    for part in small_parts:
        small_out.append(small_sum[start : start + part.size].reshape(part.shape))
        start += part.size
    token_grads = small_out[0]
    qv_bias_total = small_out[1][tensor_index]
    up_bias_total = small_out[2][tensor_index]
    rows_all = small_out[3].reshape(dp_count * seq_count, row_block.shape[1])
    width = leading.shape[1]
    classes = class_weight.shape[1]
    leading_all = rows_all[:, :width].astype(jnp.bfloat16)
    grad_pre_all = rows_all[:, width : 2 * width].astype(jnp.bfloat16)
    pooled_all = rows_all[:, 2 * width : 3 * width].astype(jnp.bfloat16)
    grad_logits_all = rows_all[:, 3 * width : 3 * width + classes].astype(jnp.bfloat16)
    pool_weight_grad = jnp.einsum(
        "rd,re->de", leading_all, grad_pre_all, preferred_element_type=jnp.float32
    )
    pool_bias_grad = jnp.sum(grad_pre_all.astype(jnp.float32), axis=0)
    class_weight_grad = jnp.einsum(
        "rd,rc->dc", pooled_all, grad_logits_all, preferred_element_type=jnp.float32
    )
    class_bias_grad = jnp.sum(grad_logits_all.astype(jnp.float32), axis=0)

    return (
        final_norm.astype(jnp.bfloat16),
        input_grad,
        weight_out[0],
        qv_bias_total,
        weight_out[1],
        token_grads[0],
        token_grads[1],
        token_grads[2],
        weight_out[2],
        up_bias_total,
        weight_out[3],
        token_grads[3],
        token_grads[4],
        token_grads[5],
        pool_weight_grad,
        pool_bias_grad,
        class_weight_grad,
        class_bias_grad,
    )


def solution(mesh):
    placed = (
        P(("dp", "tensor"), None),
        P("dp", None),
        P("dp"),
        P(None, None, "tensor"),
        P(None, "tensor"),
        P("tensor", None),
        P(),
        P(),
        P(),
        P(None, "tensor"),
        P("tensor"),
        P("tensor", None),
        P(),
        P(),
        P(),
        P(),
        P(),
        P(),
        P(),
        P(("dp", "tensor"), None),
    )
    return jax.shard_map(
        body,
        mesh=mesh,
        in_specs=placed,
        out_specs=(
            P(("dp", "tensor"), None),
            P(("dp", "tensor"), None),
            P(None, "dp", "tensor"),
            P(None, "tensor"),
            P("tensor", "dp"),
            P(),
            P(),
            P(),
            P("dp", "tensor"),
            P("tensor"),
            P("tensor", "dp"),
            P(),
            P(),
            P(),
            P(),
            P(),
            P(),
            P(),
        ),
        check_vma=False,
    )
```

time: 1100 us -> 867 us (0.79)
  waiting for transfers between devices: 754 us -> 614 us
  blocking collectives: 81.6 us -> 0 us
  matrix products: 137 us -> 120 us
    psum x3 -> x1, waiting for transfers between devices: 405 us -> 76.3 us  [body(): small_sum = lax.psum(small_flat, ('dp', 'tensor'))]
    reduce_scatter x2 -> x3, waiting for transfers between devices: 91.8 us -> 234 us  [the longest x1 84.1 us: body(): lax.psum_scatter(jnp.dot(context, out_weight, preferred_element_type=jnp....]
    psum x3 -> x0, blocking collectives: 81.6 us -> none  [the longest x1 40 us: body(): lax.psum((out_bias_grad, norm1_gain_grad, norm1_bias_grad, down_bias_grad...]
    all_gather x0 -> x1, waiting for transfers between devices: none -> 50.4 us  [body(): first_all = lax.all_gather(first_low, 'tensor', axis=0, tiled=True)]
    reshape x2 -> x18, local copies, waits for them, and re-layouts: 0.91 us -> 32.1 us  [the longest x6 20.7 us: to_blocks(): return jnp.moveaxis(array.reshape(split), axis, 0).reshape(count, -1)]
    all_gather x1, waiting for transfers between devices: 50.2 us -> 26 us  [body(): grad_att_all = lax.all_gather(grad_att, 'tensor', axis=0, tiled=True)]
    reduce_scatter x1, waiting for transfers between devices: 21 us -> 39.8 us  [body(): lax.psum_scatter(jnp.einsum('kte,kde->td', stacked, qkv_weight, preferred...]
    unnamed x98 -> x82, local copies, waits for them, and re-layouts: 28.1 us -> 11.1 us
  transfers between devices with their start and end apart: 12 -> 10, of which waited for: 10 -> 10; matrix products, arithmetic and copies ran while one was open for 4% -> 10% of each run, Pallas kernels for 0% -> 0%
where the time goes in v1:
time: 867 us; the launch traced here: 857 us
  waiting for transfers between devices  614 us (71%)
  matrix products  120 us (14%)
  local copies, waits for them, and re-layouts  78.1 us (9%)
  other arithmetic  28.5 us (3%)
  between operations  15.3 us (2%)
    reduce_scatter x1, waiting for transfers between devices, body(): lax.psum_scatter(jnp.einsum('tf,df->td', grad_up, up_weight, preferred_el...  84.2 us
    reduce_scatter x1, waiting for transfers between devices, body(): lax.psum_scatter(jnp.dot(context, out_weight, preferred_element_type=jnp....  84.1 us
    reduce_scatter x1, waiting for transfers between devices, body(): lax.psum_scatter(jnp.dot(active, down_weight, preferred_element_type=jnp....  83.9 us
    psum x1, waiting for transfers between devices, body(): small_sum = lax.psum(small_flat, ('dp', 'tensor'))  76.3 us
    reduce_scatter x1, waiting for transfers between devices, body(): lax.psum_scatter(weight_flat.reshape(-1, lanes), 'dp', scatter_dimension=...  66.2 us
    all_gather x1, waiting for transfers between devices, body(): gathered = lax.all_gather(inputs, 'tensor', axis=0, tiled=True)  52.1 us
    all_gather x1, waiting for transfers between devices, body(): first_all = lax.all_gather(first_low, 'tensor', axis=0, tiled=True)  50.4 us
    all_gather x1, waiting for transfers between devices, body(): grad_fed_all = lax.all_gather(grad_fed, 'tensor', axis=0, tiled=True)  50.2 us
  transfers between devices with their start and end apart: 10, of which 10 were waited for; matrix products, arithmetic and copies ran while one was open for 10% of the time, Pallas kernels for 0%

profile of v1, /device:TPU:0, one launch (start us, length us, event | category | flops | bytes accessed | tf_op | source)
XLA Modules:
  0.0 856.9 jit_solution(17596073723384709013)
XLA Ops:
  10.2 52.1 %all-gather.5.cloned.1.call-done = bf16[1536,768]{1,0:T(8,128)(2,1)} async-done(((bf16[384,768]{1,0:T(8,128)(2,1)}), bf16[1536,768]{1,0:T(8,128)(2,1)}) %all-gather.5.cloned.1.call-update) | async-done | bytes 2359312 | tf_op jit(solution)/shard_map/all_gather | solution.py:140
  88.9 84.1 %reduce-scatter.6.cloned.1.call-done = f32[384,768]{1,0:T(8,128)} async-done(((f32[1536,768]{1,0:T(8,128)}), f32[384,768]{1,0:T(8,128)}) %reduce-scatter.6.cloned.1.call-update) | async-done | bytes 1179664 | tf_op jit(solution)/shard_map/reduce_scatter | solution.py:150
  176.3 50.4 %all-gather.7.cloned.1.call-done = bf16[1536,768]{1,0:T(8,128)(2,1)} async-done(((bf16[384,768]{1,0:T(8,128)(2,1)}), bf16[1536,768]{1,0:T(8,128)(2,1)}) %all-gather.7.cloned.1.call-update) | async-done | bytes 2359312 | tf_op jit(solution)/shard_map/all_gather | solution.py:162
  226.7 14.6 %multiply_convert_fusion = (bf16[1536,768]{1,0:T(8,128)(2,1)S(1)}, f32[1536,768]{1,0:T(8,128)}, f32[1536,768]{1,0:T(8,128)}) fusion(f32[768]{0:T(1024)S(1)} %copy-done.35, bf16[1536,768]{1,0:T(8,128)(2,1)} %all-gather.7.cloned.1.call-done, bf16[768,768]{1,0:T(8,128)(2,1)S(1)} %copy-done), kind=kOutput, calls=%fused_computation.23 | convolution fusion | flops 1889796096 | bytes 15338496 | tf_op jit(solution)/shard_map/dot_general | solution.py:163
  247.3 83.9 %reduce-scatter.8.cloned.1.call-done = f32[384,768]{1,0:T(8,128)} async-done(((f32[1536,768]{1,0:T(8,128)}), f32[384,768]{1,0:T(8,128)}) %reduce-scatter.8.cloned.1.call-update) | async-done | bytes 1179664 | tf_op jit(solution)/shard_map/reduce_scatter | solution.py:167
  339.2 50.2 %all-gather.9.cloned.1.call-done = bf16[1536,768]{1,0:T(8,128)(2,1)} async-done(((bf16[384,768]{1,0:T(8,128)(2,1)}), bf16[1536,768]{1,0:T(8,128)(2,1)}) %all-gather.9.cloned.1.call-update) | async-done | bytes 2359312 | tf_op jit(solution)/shard_map/all_gather | solution.py:208
  389.4 8.2 convert_reduce_fusion
  399.0 4.4 fusion.130
  403.4 84.2 %reduce-scatter.10.cloned.1.call-done = f32[384,768]{1,0:T(8,128)} async-done(((f32[1536,768]{1,0:T(8,128)}), f32[384,768]{1,0:T(8,128)}) %reduce-scatter.10.cloned.1.call-update) | async-done | bytes 1179664 | tf_op jit(solution)/shard_map/reduce_scatter | solution.py:219
  493.3 5.9 fusion.131
  501.3 5.9 fusion.132
  510.7 5.1 reshape.263
  515.8 26.0 %all-gather.11.cloned.1.call-done = bf16[1536,768]{1,0:T(8,128)(2,1)} async-done(((bf16[384,768]{1,0:T(8,128)(2,1)}), bf16[1536,768]{1,0:T(8,128)(2,1)}) %all-gather.11.cloned.1.call-update) | async-done | bytes 2359312 | tf_op jit(solution)/shard_map/all_gather | solution.py:232
  545.7 6.6 fusion.76
  552.2 7.2 convert_reduce_fusion.1
  559.4 16.2 %fusion.63 = bf16[3,512,3,64]{1,3,2,0:T(8,128)(2,1)} fusion(f32[3,3,512,512]{2,3,1,0:T(8,128)} %fusion.76, f32[3,3,512,512]{2,3,1,0:T(8,128)} %copy-done.2, f32[3,3,512]{2,1,0:T(4,128)S(1)} %log_add_fusion, pred[3,512,512]{1,2,0:T(8,128)(4,1)S(1)} %copy-done.8, bf16[3,512,3,64]{1,0,3,2:T(4,128)(2,1)} %copy-done.15), kind=kOutput, calls=%fused_computation.63 | convolution fusion | flops 328537088 | bytes 20858880 | tf_op jit(solution)/shard_map/rhqk,rqhe->rkhe/dot_general | solution.py:88
  575.6 16.3 %convert_reduce_fusion.2 = (f32[3,64]{1,0:T(4,128)S(1)}, bf16[3,3,64,512]{3,2,1,0:T(8,128)(2,1)}) fusion(f32[3,3,512,512]{2,3,1,0:T(8,128)} %fusion.76, f32[3,3,512,512]{2,3,1,0:T(8,128)} %copy-done.2, f32[3,3,512]{2,1,0:T(4,128)S(1)} %log_add_fusion, pred[3,512,512]{1,2,0:T(8,128)(4,1)S(1)} %copy-done.8, bf16[3,512,3,64]{1,0,3,2:T(4,128)(2,1)} %convert_element_type.183), kind=kOutput, calls=%fused_computation.67 | convolution fusion | flops 329126720 | bytes 20859648 | tf_op jit(solution)/shard_map/rhqk,rkhe->rqhe/dot_general | solution.py:84
  595.1 4.3 copy.129
  613.7 5.1 fusion.44
  632.9 9.3 %pad_maximum_fusion = f32[8,221184]{1,0:T(8,128)} fusion(f32[8,73728]{1,0:T(8,128)} %reshape.263, f32[8,73728]{1,0:T(8,128)S(1)} %reshape_reshape.6, f32[8,18432]{1,0:T(8,128)S(1)} %reshape.261, f32[8,55296]{1,0:T(8,128)} %reshape.260), kind=kLoop, calls=%fused_computation.9 | loop fusion | flops 5308416 | bytes 14155776 | tf_op jit(solution)/shard_map/concatenate | solution.py:270
  642.3 7.2 reshape.264
  649.5 76.3 %all-reduce.2.cloned.1.call-done = f32[64584]{0:T(1024)} async-done(((f32[64584]{0:T(1024)}), f32[64584]{0:T(1024)}) %all-reduce.2.cloned.1.call-update) | async-done | bytes 258352 | tf_op jit(solution)/shard_map/psum | solution.py:313
  735.2 39.8 %reduce-scatter.12.cloned.1.call-done = bf16[384,768]{1,0:T(8,128)(2,1)} async-done(((bf16[1536,768]{1,0:T(8,128)(2,1)}), bf16[384,768]{1,0:T(8,128)(2,1)}) %reduce-scatter.12.cloned.1.call-update) | async-done | bytes 589840 | tf_op jit(solution)/shard_map/reduce_scatter | solution.py:253
  777.0 66.2 %reduce-scatter.14.cloned.1.call-done = f32[216,1024]{1,0:T(8,128)} async-done(((f32[1728,1024]{1,0:T(8,128)}), f32[216,1024]{1,0:T(8,128)}) %reduce-scatter.14.cloned.1.call-update) | async-done | bytes 884752 | tf_op jit(solution)/shard_map/reduce_scatter | solution.py:274
  (208 shorter events, 112.2 us)
Async XLA Ops:
  7.2 219.5 %copy-start = (bf16[768,768]{1,0:T(8,128)(2,1)S(1)}, bf16[768,768]{1,0:T(8,128)(2,1)}, u32[]{:S(2)}) copy-start(bf16[768,768]{1,0:T(8,128)(2,1)} %param.29) | copy-start | bytes 3538948
  7.2 55.1 %all-gather.5.cloned.1.call-start = ((), (), s32[]{:S(2)}) async-start(), calls=%async_computation.5 | async-start | bytes 2949120 | tf_op jit(solution)/shard_map/all_gather | solution.py:140
  7.9 165.1 %reduce-scatter.6.cloned.1.call-start = ((), (), s32[]{:S(2)}) async-start(), calls=%async_computation.6 | async-start | bytes 5898240 | tf_op jit(solution)/shard_map/reduce_scatter | solution.py:150
  10.2 69.3 %copy-start.7 = (pred[3,512,512]{1,2,0:T(8,128)(4,1)}, pred[3,512,512]{1,2,0:T(8,128)(4,1)S(1)}, u32[]{:S(2)}) copy-start(pred[3,512,512]{1,2,0:T(8,128)(4,1)S(1)} %broadcast_compare_fusion) | copy-start | bytes 2359300
  88.8 84.2 %copy-start.28 = (f32[768]{0:T(1024)S(1)}, f32[768]{0:T(1024)}, u32[]{:S(2)}) copy-start(f32[768]{0:T(1024)} %param.26) | copy-start | bytes 9220
  88.8 86.1 %copy-start.23 = (f32[768]{0:T(1024)S(1)}, f32[768]{0:T(1024)}, u32[]{:S(2)}) copy-start(f32[768]{0:T(1024)} %param.27) | copy-start | bytes 9220
  88.8 86.1 %copy-start.24 = (f32[768]{0:T(1024)S(1)}, f32[768]{0:T(1024)}, u32[]{:S(2)}) copy-start(f32[768]{0:T(1024)} %param.28) | copy-start | bytes 9220
  88.8 137.9 %all-gather.7.cloned.1.call-start = ((), (), s32[]{:S(2)}) async-start(), calls=%async_computation.7 | async-start | bytes 2949120 | tf_op jit(solution)/shard_map/all_gather | solution.py:162
  174.7 52.1 %copy-start.35 = (f32[768]{0:T(1024)S(1)}, f32[768]{0:T(1024)}, u32[]{:S(2)}) copy-start(f32[768]{0:T(1024)} %param.30) | copy-start | bytes 9220
  176.1 155.2 %reduce-scatter.8.cloned.1.call-start = ((), (), s32[]{:S(2)}) async-start(), calls=%async_computation.8 | async-start | bytes 5898240 | tf_op jit(solution)/shard_map/reduce_scatter | solution.py:167
  226.7 16.0 %copy-start.32 = (bf16[768,768]{1,0:T(8,128)(2,1)S(1)}, bf16[768,768]{1,0:T(8,128)(2,1)}, u32[]{:S(2)}) copy-start(bf16[768,768]{1,0:T(8,128)(2,1)} %param.31) | copy-start | bytes 3538948
  247.0 84.2 %copy-start.29 = (f32[768]{0:T(1024)S(1)}, f32[768]{0:T(1024)}, u32[]{:S(2)}) copy-start(f32[768]{0:T(1024)} %param.32) | copy-start | bytes 9220
  247.0 142.4 %all-gather.9.cloned.1.call-start = ((), (), s32[]{:S(2)}) async-start(), calls=%async_computation.9 | async-start | bytes 2949120 | tf_op jit(solution)/shard_map/all_gather | solution.py:208
  247.3 86.1 %copy-start.25 = (f32[768]{0:T(1024)S(1)}, f32[768]{0:T(1024)}, u32[]{:S(2)}) copy-start(f32[768]{0:T(1024)} %param.33) | copy-start | bytes 9220
  247.3 86.1 %copy-start.26 = (f32[768]{0:T(1024)S(1)}, f32[768]{0:T(1024)}, u32[]{:S(2)}) copy-start(f32[768]{0:T(1024)} %param.34) | copy-start | bytes 9220
  247.3 86.8 %copy-start.30 = (f32[768]{0:T(1024)S(1)}, f32[768]{0:T(1024)}, u32[]{:S(2)}) copy-start(f32[768]{0:T(1024)} %param.36) | copy-start | bytes 9220
  338.8 148.8 %reduce-scatter.10.cloned.1.call-start = ((), (), s32[]{:S(2)}) async-start(), calls=%async_computation.10 | async-start | bytes 5898240 | tf_op jit(solution)/shard_map/reduce_scatter | solution.py:219
  403.3 84.2 %copy-start.6 = (f32[384,768]{1,0:T(8,128)S(1)}, f32[384,768]{1,0:T(8,128)}, u32[]{:S(2)}) copy-start(f32[384,768]{1,0:T(8,128)} %get-tuple-element.102) | copy-start | bytes 3538948
  403.4 138.5 %all-gather.11.cloned.1.call-start = ((), (), s32[]{:S(2)}) async-start(), calls=%async_computation.11 | async-start | bytes 2949120 | tf_op jit(solution)/shard_map/all_gather | solution.py:232
  491.2 234.7 %all-reduce.2.cloned.1.call-start = ((), (), s32[]{:S(2)}) async-start(), calls=%async_computation.14 | async-start | bytes 524288 | tf_op jit(solution)/shard_map/psum | solution.py:313
  600.4 174.6 %reduce-scatter.12.cloned.1.call-start = ((), (), s32[]{:S(2)}) async-start(), calls=%async_computation.12 | async-start | bytes 2949120 | tf_op jit(solution)/shard_map/reduce_scatter | solution.py:253
  632.9 210.3 %reduce-scatter.14.cloned.1.call-start = ((), (), s32[]{:S(2)}) async-start(), calls=%async_computation.13 | async-start | bytes 7962624 | tf_op jit(solution)/shard_map/reduce_scatter | solution.py:274
  649.5 125.5 %copy-start.5 = (f32[384,768]{1,0:T(8,128)S(1)}, f32[384,768]{1,0:T(8,128)}, u32[]{:S(2)}) copy-start(f32[384,768]{1,0:T(8,128)} %get-tuple-element.105) | copy-start | bytes 3538948
  775.0 74.6 %copy-start.1 = (bf16[768,768]{1,0:T(8,128)(2,1)S(1)}, bf16[768,768]{1,0:T(8,128)(2,1)}, u32[]{:S(2)}) copy-start(bf16[768,768]{1,0:T(8,128)(2,1)} %param.29) | copy-start | bytes 3538948
  (24 other events, 68.8 us)
Sparse Core Ops, SparseCore 0:
  9.6 52.6 all-gather.4
  88.9 84.0 reduce-scatter.5
  176.2 50.4 all-gather.6
  247.1 84.0 reduce-scatter.7
  338.9 50.4 all-gather.8
  403.5 84.0 reduce-scatter.9
  491.3 50.4 all-gather.10
  600.5 125.3 all-reduce.1
  728.2 46.7 reduce-scatter.11
  778.3 64.8 reduce-scatter.13

commit v2 on v1

--- a/solution.py
+++ b/solution.py
@@ -148,11 +148,12 @@
     context, log_totals = attend_forward(queries, key_rows, value_rows, segments)
     attended = (
         lax.psum_scatter(
-            jnp.dot(context, out_weight, preferred_element_type=jnp.float32),
+            jnp.dot(context, out_weight, preferred_element_type=jnp.float32).astype(jnp.bfloat16),
             "tensor",
             scatter_dimension=0,
             tiled=True,
         )
+        .astype(jnp.float32)
         + out_bias
     )
     first_norm, normed_one, inverse_one = norm_forward(
@@ -165,11 +166,12 @@
     active = gelu_exact(up_pre).astype(jnp.bfloat16)
     ffn_out = (
         lax.psum_scatter(
-            jnp.dot(active, down_weight, preferred_element_type=jnp.float32),
+            jnp.dot(active, down_weight, preferred_element_type=jnp.float32).astype(jnp.bfloat16),
             "tensor",
             scatter_dimension=0,
             tiled=True,
         )
+        .astype(jnp.float32)
         + down_bias
     )
     final_norm, normed_two, inverse_two = norm_forward(
@@ -217,11 +219,12 @@
     up_weight_grad = jnp.einsum("td,tf->df", first_all, grad_up, preferred_element_type=jnp.float32)
     grad_first = (
         lax.psum_scatter(
-            jnp.einsum("tf,df->td", grad_up, up_weight, preferred_element_type=jnp.float32),
+            jnp.einsum("tf,df->td", grad_up, up_weight, preferred_element_type=jnp.float32).astype(jnp.bfloat16),
             "tensor",
             scatter_dimension=0,
             tiled=True,
         )
+        .astype(jnp.float32)
         + grad_second
     )
     grad_res, norm1_gain_grad, norm1_bias_grad = norm_backward(
@@ -261,29 +264,33 @@
         + grad_res
     ).astype(jnp.bfloat16)
 
-    weight_parts = (
-        (qkv_weight_grad, 1),
-        (out_weight_grad, 1),
-        (up_weight_grad, 0),
-        (down_weight_grad, 1),
-    )
-    weight_flat = jnp.concatenate(
-        [to_blocks(grad, axis, dp_count) for grad, axis in weight_parts], axis=1
-    )
-    lanes = 1024 if weight_flat.shape[1] % 1024 == 0 else 128
-    weight_sum = lax.psum_scatter(
-        weight_flat.reshape(-1, lanes), "dp", scatter_dimension=0, tiled=True
-    ).reshape(-1)
-    weight_out = []
-    start = 0
-    for grad, axis in weight_parts:
-        size = grad.size // dp_count
-        weight_out.append(from_block(weight_sum[start : start + size], grad.shape, axis, dp_count))
-        start += size
-
-    def slot(values, index, count):
-        holder = jnp.zeros((count,) + values.shape, values.dtype)
-        return lax.dynamic_update_slice(holder, values[None], (index,) + (0,) * values.ndim)
+    def reduce_over_dp(parts):
+        flat = jnp.concatenate([to_blocks(grad, axis, dp_count) for grad, axis in parts], axis=1)
+        lanes = 1024 if flat.shape[1] % 1024 == 0 else 128
+        summed = lax.psum_scatter(
+            flat.reshape(-1, lanes), "dp", scatter_dimension=0, tiled=True
+        ).reshape(-1)
+        pieces = []
+        begin = 0
+        for grad, axis in parts:
+            size = grad.size // dp_count
+            pieces.append(from_block(summed[begin : begin + size], grad.shape, axis, dp_count))
+            begin += size
+        return pieces
+
+    up_sum, down_sum = reduce_over_dp(((up_weight_grad, 0), (down_weight_grad, 1)))
+    qkv_sum, out_sum = reduce_over_dp(((qkv_weight_grad, 1), (out_weight_grad, 1)))
+
+    def joined(parts):
+        return jnp.concatenate([part.reshape(-1) for part in parts])
+
+    def parted(flat, parts):
+        pieces = []
+        begin = 0
+        for part in parts:
+            pieces.append(flat[..., begin : begin + part.size].reshape(flat.shape[:-1] + part.shape))
+            begin += part.size
+        return pieces
 
     row_block = jnp.concatenate(
         [
@@ -294,7 +301,7 @@
         ],
         axis=1,
     )
-    small_parts = [
+    token_parts = [
         jnp.stack(
             [
                 out_bias_grad,
@@ -305,21 +312,16 @@
                 norm2_bias_grad,
             ]
         ),
-        slot(qv_bias_grad, tensor_index, tensor_count),
-        slot(up_bias_grad, tensor_index, tensor_count),
-        slot(row_block, dp_index, dp_count),
+        row_block,
     ]
-    small_flat = jnp.concatenate([part.reshape(-1) for part in small_parts])
-    small_sum = lax.psum(small_flat, ("dp", "tensor"))
-    small_out = []
-    start = 0
-    for part in small_parts:
-        small_out.append(small_sum[start : start + part.size].reshape(part.shape))
-        start += part.size
-    token_grads = small_out[0]
-    qv_bias_total = small_out[1][tensor_index]
-    up_bias_total = small_out[2][tensor_index]
-    rows_all = small_out[3].reshape(dp_count * seq_count, row_block.shape[1])
+    token_sum, rows_group = parted(lax.psum(joined(token_parts), "tensor"), token_parts)
+    group_parts = [token_sum, rows_group, qv_bias_grad, up_bias_grad]
+    gathered_small = lax.all_gather(joined(group_parts), "dp", axis=0, tiled=False)
+    token_each, rows_each, qv_each, up_each = parted(gathered_small, group_parts)
+    token_grads = jnp.sum(token_each, axis=0)
+    qv_bias_total = jnp.sum(qv_each, axis=0)
+    up_bias_total = jnp.sum(up_each, axis=0)
+    rows_all = rows_each.reshape(dp_count * seq_count, row_block.shape[1])
     width = leading.shape[1]
     classes = class_weight.shape[1]
     leading_all = rows_all[:, :width].astype(jnp.bfloat16)
@@ -338,15 +340,15 @@
     return (
         final_norm.astype(jnp.bfloat16),
         input_grad,
-        weight_out[0],
+        qkv_sum,
         qv_bias_total,
-        weight_out[1],
+        out_sum,
         token_grads[0],
         token_grads[1],
         token_grads[2],
-        weight_out[2],
+        up_sum,
         up_bias_total,
-        weight_out[3],
+        down_sum,
         token_grads[3],
         token_grads[4],
         token_grads[5],

time: 867 us -> 674 us (0.78)
  waiting for transfers between devices: 614 us -> 398 us
  blocking collectives: 0 us -> 20.2 us
  starting transfers between devices: 1.03 us -> 12 us
    psum x1 -> x0, waiting for transfers between devices: 76.3 us -> none  [body(): small_sum = lax.psum(small_flat, ('dp', 'tensor'))]
    reduce_scatter x1, waiting for transfers between devices: 84.2 us -> 22.8 us  [body(): lax.psum_scatter(jnp.einsum('tf,df->td', grad_up, up_weight, preferred_el...]
    unnamed x10 -> x12, waiting for transfers between devices: 0.83 us -> 42.4 us
    reduce_scatter x1, waiting for transfers between devices: 83.9 us -> 44.9 us  [body(): lax.psum_scatter(jnp.dot(active, down_weight, preferred_element_type=jnp....]
    reduce_scatter x1, waiting for transfers between devices: 84.1 us -> 46.2 us  [body(): lax.psum_scatter(jnp.dot(context, out_weight, preferred_element_type=jnp....]
    reduce_scatter x1 -> x2, waiting for transfers between devices: 66.2 us -> 38.2 us  [reduce_over_dp(): lax.psum_scatter(flat.reshape(-1, lanes), 'dp', scatter_dimension=0, tile...]
    psum x0 -> x1, blocking collectives: none -> 20.2 us  [body(): lax.psum(joined(token_parts), 'tensor')]
    all_gather x1, waiting for transfers between devices: 50.2 us -> 38.4 us  [body(): grad_fed_all = lax.all_gather(grad_fed, 'tensor', axis=0, tiled=True)]
  transfers between devices with their start and end apart: 10 -> 11, of which waited for: 10 -> 10; matrix products, arithmetic and copies ran while one was open for 10% -> 20% of each run, Pallas kernels for 0% -> 0%
where the time goes in v2:
time: 674 us; the launch traced here: 665 us
  waiting for transfers between devices  398 us (59%)
  matrix products  117 us (17%)
  local copies, waits for them, and re-layouts  73.4 us (11%)
  other arithmetic  28.1 us (4%)
  blocking collectives  20.2 us (3%)
  between operations  15.6 us (2%)
  starting transfers between devices  12 us (2%)
    all_gather x1, waiting for transfers between devices, body(): gathered = lax.all_gather(inputs, 'tensor', axis=0, tiled=True)  52.1 us
    all_gather x1, waiting for transfers between devices, body(): first_all = lax.all_gather(first_low, 'tensor', axis=0, tiled=True)  49.5 us
    reduce_scatter x1, waiting for transfers between devices, body(): lax.psum_scatter(jnp.einsum('kte,kde->td', stacked, qkv_weight, preferred...  46.6 us
    reduce_scatter x1, waiting for transfers between devices, body(): lax.psum_scatter(jnp.dot(context, out_weight, preferred_element_type=jnp....  46.2 us
    reduce_scatter x1, waiting for transfers between devices, body(): lax.psum_scatter(jnp.dot(active, down_weight, preferred_element_type=jnp....  44.9 us
    unnamed x12, waiting for transfers between devices  42.4 us
    all_gather x1, waiting for transfers between devices, body(): grad_fed_all = lax.all_gather(grad_fed, 'tensor', axis=0, tiled=True)  38.4 us
    reduce_scatter x2, waiting for transfers between devices, reduce_over_dp(): lax.psum_scatter(flat.reshape(-1, lanes), 'dp', scatter_dimension=0, tile...  38.2 us
  transfers between devices with their start and end apart: 11, of which 10 were waited for; matrix products, arithmetic and copies ran while one was open for 20% of the time, Pallas kernels for 0%

profile of v2, /device:TPU:0, one launch (start us, length us, event | category | flops | bytes accessed | tf_op | source)
XLA Modules:
  0.0 664.9 jit_solution(2203228888798162206)
XLA Ops:
  10.2 52.1 %all-gather.6.cloned.1.call-done = bf16[1536,768]{1,0:T(8,128)(2,1)} async-done(((bf16[384,768]{1,0:T(8,128)(2,1)}), bf16[1536,768]{1,0:T(8,128)(2,1)}) %all-gather.6.cloned.1.call-update) | async-done | bytes 2359312 | tf_op jit(solution)/shard_map/all_gather | solution.py:140
  88.8 46.2 %reduce-scatter.7.cloned.1.call-done = bf16[384,768]{1,0:T(8,128)(2,1)} async-done(((bf16[1536,768]{1,0:T(8,128)(2,1)}), bf16[384,768]{1,0:T(8,128)(2,1)}) %reduce-scatter.7.cloned.1.call-update) | async-done | bytes 589840 | tf_op jit(solution)/shard_map/reduce_scatter | solution.py:150
  139.1 49.5 %all-gather.8.cloned.1.call-done = bf16[1536,768]{1,0:T(8,128)(2,1)} async-done(((bf16[384,768]{1,0:T(8,128)(2,1)}), bf16[1536,768]{1,0:T(8,128)(2,1)}) %all-gather.8.cloned.1.call-update) | async-done | bytes 2359312 | tf_op jit(solution)/shard_map/all_gather | solution.py:163
  188.6 14.5 %multiply_convert_fusion = (bf16[1536,768]{1,0:T(8,128)(2,1)S(1)}, f32[1536,768]{1,0:T(8,128)}, f32[1536,768]{1,0:T(8,128)}) fusion(f32[768]{0:T(1024)} %param.30, bf16[1536,768]{1,0:T(8,128)(2,1)} %all-gather.8.cloned.1.call-done, bf16[768,768]{1,0:T(8,128)(2,1)S(1)} %copy-done), kind=kOutput, calls=%fused_computation.23 | convolution fusion | flops 1889796096 | bytes 15338496 | tf_op jit(solution)/shard_map/dot_general | solution.py:164
  209.7 44.9 %reduce-scatter.9.cloned.1.call-done = bf16[384,768]{1,0:T(8,128)(2,1)} async-done(((bf16[1536,768]{1,0:T(8,128)(2,1)}), bf16[384,768]{1,0:T(8,128)(2,1)}) %reduce-scatter.9.cloned.1.call-update) | async-done | bytes 589840 | tf_op jit(solution)/shard_map/reduce_scatter | solution.py:168
  265.2 11.1 %reduce-scatter.11.cloned.1.call-start = ((), (), s32[]{:S(2)}) async-start(), calls=%async_computation.11 | async-start | bytes 2949120 | tf_op jit(solution)/shard_map/reduce_scatter | solution.py:221
  276.3 38.4 %all-gather.10.cloned.1.call-done = bf16[1536,768]{1,0:T(8,128)(2,1)} async-done(((bf16[384,768]{1,0:T(8,128)(2,1)}), bf16[1536,768]{1,0:T(8,128)(2,1)}) %all-gather.10.cloned.1.call-update) | async-done | bytes 2359312 | tf_op jit(solution)/shard_map/all_gather | solution.py:210
  314.7 8.7 %convert_reduce_fusion = (f32[768]{0:T(1024)}, bf16[1536,768]{1,0:T(8,128)(2,1)S(1)}) fusion(f32[1536,768]{1,0:T(8,128)} %get-tuple-element.113, f32[1536,768]{1,0:T(8,128)} %get-tuple-element.129, f32[768]{0:T(1024)} %param.30, bf16[1536,768]{1,0:T(8,128)(2,1)} %all-gather.10.cloned.1.call-done, bf16[768,768]{1,0:T(8,128)(2,1)} %param.31), kind=kOutput, calls=%fused_computation.17 | convolution fusion | flops 1831992576 | bytes 15341568 | tf_op jit(solution)/shard_map/td,fd->tf/dot_general | solution.py:214
  328.4 5.9 fusion.127
  337.9 5.9 fusion.128
  347.1 5.1 reshape.267
  352.2 22.8 %reduce-scatter.11.cloned.1.call-done = bf16[384,768]{1,0:T(8,128)(2,1)} async-done(((bf16[1536,768]{1,0:T(8,128)(2,1)}), bf16[384,768]{1,0:T(8,128)(2,1)}) %reduce-scatter.11.cloned.1.call-update) | async-done | bytes 589840 | tf_op jit(solution)/shard_map/reduce_scatter | solution.py:221
  379.3 4.5 pad_maximum_fusion
  383.8 5.5 reshape.268
  393.1 20.2 %psum.7 = f32[11529]{0:T(1024)S(1)} all-reduce(f32[11529]{0:T(1024)S(1)} %pad_maximum_fusion.2), channel_id=1, replica_groups=mesh['dp'=8,'tensor'=4] {'tensor'}, use_global_device_ids=true, to_apply=%region_25.26 | all-reduce | flops 11529 | bytes 92232 | tf_op jit(solution)/shard_map/psum | solution.py:317
  413.3 17.1 %all-gather.12.cloned.1.call-done = bf16[1536,768]{1,0:T(8,128)(2,1)} async-done(((bf16[384,768]{1,0:T(8,128)(2,1)}), bf16[1536,768]{1,0:T(8,128)(2,1)}) %all-gather.12.cloned.1.call-update) | async-done | bytes 2359312 | tf_op jit(solution)/shard_map/all_gather | solution.py:235
  433.4 6.4 convert_reduce_fusion.1
  441.3 4.4 copy.129
  452.0 5.3 fusion.77
  457.4 15.6 %convert_reduce_fusion.2 = (f32[3,64]{1,0:T(4,128)S(1)}, bf16[3,3,64,512]{3,2,1,0:T(8,128)(2,1)S(1)}) fusion(f32[3,3,512,512]{2,3,1,0:T(8,128)} %fusion.77, f32[3,3,512,512]{2,3,1,0:T(8,128)} %copy-done.4, f32[3,3,512]{2,1,0:T(4,128)S(1)} %log_add_fusion, pred[3,512,512]{1,2,0:T(8,128)(4,1)S(1)} %copy-done.11, bf16[3,512,3,64]{1,0,3,2:T(4,128)(2,1)} %convert_element_type.201), kind=kOutput, calls=%fused_computation.71 | convolution fusion | flops 329126720 | bytes 20859648 | tf_op jit(solution)/shard_map/rhqk,rkhe->rqhe/dot_general | solution.py:84
  474.5 16.3 %fusion.63 = bf16[3,512,3,64]{1,3,2,0:T(8,128)(2,1)S(1)} fusion(f32[3,3,512,512]{2,3,1,0:T(8,128)} %fusion.77, f32[3,3,512,512]{2,3,1,0:T(8,128)} %copy-done.4, f32[3,3,512]{2,1,0:T(4,128)S(1)} %log_add_fusion, pred[3,512,512]{1,2,0:T(8,128)(4,1)S(1)} %copy-done.11, bf16[3,512,3,64]{1,0,3,2:T(4,128)(2,1)} %copy-done.18), kind=kOutput, calls=%fused_computation.67 | convolution fusion | flops 328537088 | bytes 20858880 | tf_op jit(solution)/shard_map/rhqk,rqhe->rkhe/dot_general | solution.py:88
  518.8 41.5 %all-reduce.3.cloned.1.call-done = f32[101448]{0:T(1024)} async-done(((f32[101448]{0:T(1024)}), f32[101448]{0:T(1024)}) %all-reduce.3.cloned.1.call-update) | async-done | bytes 405808
  568.0 38.2 %reduce-scatter.15.cloned.1.call-done = f32[72,1024]{1,0:T(8,128)} async-done(((f32[576,1024]{1,0:T(8,128)}), f32[72,1024]{1,0:T(8,128)}) %reduce-scatter.15.cloned.1.call-update) | async-done | bytes 294928 | tf_op jit(solution)/shard_map/reduce_scatter | solution.py:270
  609.6 46.6 %reduce-scatter.13.cloned.1.call-done = bf16[384,768]{1,0:T(8,128)(2,1)} async-done(((bf16[1536,768]{1,0:T(8,128)(2,1)}), bf16[384,768]{1,0:T(8,128)(2,1)}) %reduce-scatter.13.cloned.1.call-update) | async-done | bytes 589840 | tf_op jit(solution)/shard_map/reduce_scatter | solution.py:256
  (253 shorter events, 122.5 us)
Async XLA Ops:
  7.2 181.4 %copy-start = (bf16[768,768]{1,0:T(8,128)(2,1)S(1)}, bf16[768,768]{1,0:T(8,128)(2,1)}, u32[]{:S(2)}) copy-start(bf16[768,768]{1,0:T(8,128)(2,1)} %param.29) | copy-start | bytes 3538948
  7.2 55.1 %all-gather.6.cloned.1.call-start = ((), (), s32[]{:S(2)}) async-start(), calls=%async_computation.6 | async-start | bytes 2949120 | tf_op jit(solution)/shard_map/all_gather | solution.py:140
  7.9 127.1 %reduce-scatter.7.cloned.1.call-start = ((), (), s32[]{:S(2)}) async-start(), calls=%async_computation.7 | async-start | bytes 2949120 | tf_op jit(solution)/shard_map/reduce_scatter | solution.py:150
  10.2 69.3 %copy-start.10 = (pred[3,512,512]{1,2,0:T(8,128)(4,1)}, pred[3,512,512]{1,2,0:T(8,128)(4,1)S(1)}, u32[]{:S(2)}) copy-start(pred[3,512,512]{1,2,0:T(8,128)(4,1)S(1)} %broadcast_compare_fusion) | copy-start | bytes 2359300
  86.1 48.9 %copy-start.2 = (bf16[384,768]{1,0:T(8,128)(2,1)S(1)}, bf16[384,768]{1,0:T(8,128)(2,1)}, u32[]{:S(2)}) copy-start(bf16[384,768]{1,0:T(8,128)(2,1)} %param.20) | copy-start | bytes 1769476
  86.1 48.9 %copy-start.24 = (f32[768]{0:T(1024)S(1)}, f32[768]{0:T(1024)}, u32[]{:S(2)}) copy-start(f32[768]{0:T(1024)} %param.26) | copy-start | bytes 9220
  88.4 49.5 %copy-start.29 = (f32[768]{0:T(1024)S(1)}, f32[768]{0:T(1024)}, u32[]{:S(2)}) copy-start(f32[768]{0:T(1024)} %param.27) | copy-start | bytes 9220
  88.4 49.5 %copy-start.35 = (f32[768]{0:T(1024)S(1)}, f32[768]{0:T(1024)}, u32[]{:S(2)}) copy-start(f32[768]{0:T(1024)} %param.28) | copy-start | bytes 9220
  88.4 100.2 %all-gather.8.cloned.1.call-start = ((), (), s32[]{:S(2)}) async-start(), calls=%async_computation.8 | async-start | bytes 2949120 | tf_op jit(solution)/shard_map/all_gather | solution.py:163
  139.1 65.4 %copy-start.53 = (bf16[768,768]{1,0:T(8,128)(2,1)S(1)}, bf16[768,768]{1,0:T(8,128)(2,1)}, u32[]{:S(2)}) copy-start(bf16[768,768]{1,0:T(8,128)(2,1)} %param.31) | copy-start | bytes 3538948
  139.1 115.5 %reduce-scatter.9.cloned.1.call-start = ((), (), s32[]{:S(2)}) async-start(), calls=%async_computation.9 | async-start | bytes 2949120 | tf_op jit(solution)/shard_map/reduce_scatter | solution.py:168
  208.0 106.8 %all-gather.10.cloned.1.call-start = ((), (), s32[]{:S(2)}) async-start(), calls=%async_computation.10 | async-start | bytes 2949120 | tf_op jit(solution)/shard_map/all_gather | solution.py:210
  209.7 48.4 %copy-start.8 = (bf16[768,768]{1,0:T(8,128)(2,1)S(1)}, bf16[768,768]{1,0:T(8,128)(2,1)}, u32[]{:S(2)}) copy-start(bf16[768,768]{1,0:T(8,128)(2,1)} %param.35) | copy-start | bytes 3538948
  265.2 109.8 %reduce-scatter.11.cloned.1.call-start = ((), (), s32[]{:S(2)}) async-start(), calls=%async_computation.11 | async-start | bytes 2949120 | tf_op jit(solution)/shard_map/reduce_scatter | solution.py:221
  328.4 102.0 %all-gather.12.cloned.1.call-start = ((), (), s32[]{:S(2)}) async-start(), calls=%async_computation.12 | async-start | bytes 2949120 | tf_op jit(solution)/shard_map/all_gather | solution.py:235
  379.3 136.6 %reduce-scatter.17.cloned.1.call-start = ((), (), s32[]{:S(2)}) async-start(), calls=%async_computation.15 | async-start | bytes 5308416 | tf_op jit(solution)/shard_map/reduce_scatter | solution.py:270
  389.4 41.0 %copy-start.21 = (bf16[192,768]{1,0:T(8,128)(2,1)S(1)}, bf16[192,768]{1,0:T(8,128)(2,1)}, u32[]{:S(2)}) copy-start(bf16[192,768]{1,0:T(8,128)(2,1)} %param.25) | copy-start | bytes 884740
  389.5 170.9 %all-reduce.3.cloned.1.call-start = ((), (), s32[]{:S(2)}) async-start(), calls=%async_computation.16 | async-start | bytes 819200
  413.3 20.1 %copy-start.11 = (pred[3,512,512]{1,2,0:T(8,128)(4,1)S(1)}, pred[3,512,512]{1,2,0:T(8,128)(4,1)}, u32[]{:S(2)}) copy-start(pred[3,512,512]{1,2,0:T(8,128)(4,1)} %copy-done.10) | copy-start | bytes 2359300
  445.8 6.3 copy-start.13
  507.4 98.8 %reduce-scatter.15.cloned.1.call-start = ((), (), s32[]{:S(2)}) async-start(), calls=%async_computation.14 | async-start | bytes 2654208 | tf_op jit(solution)/shard_map/reduce_scatter | solution.py:270
  510.9 145.3 %reduce-scatter.13.cloned.1.call-start = ((), (), s32[]{:S(2)}) async-start(), calls=%async_computation.13 | async-start | bytes 2949120 | tf_op jit(solution)/shard_map/reduce_scatter | solution.py:256
  561.6 94.6 %copy-start.9 = (f32[384,768]{1,0:T(8,128)S(1)}, f32[384,768]{1,0:T(8,128)}, u32[]{:S(2)}) copy-start(f32[384,768]{1,0:T(8,128)} %get-tuple-element.107) | copy-start | bytes 3538948
  566.1 92.1 %copy-start.1 = (bf16[768,768]{1,0:T(8,128)(2,1)S(1)}, bf16[768,768]{1,0:T(8,128)(2,1)}, u32[]{:S(2)}) copy-start(bf16[768,768]{1,0:T(8,128)(2,1)} %param.29) | copy-start | bytes 3538948
  (46 other events, 121.0 us)
Sparse Core Ops, SparseCore 0:
  9.6 52.6 all-gather.5
  88.5 46.4 reduce-scatter.6
  139.2 49.3 all-gather.7
  208.1 46.4 reduce-scatter.8
  265.3 49.3 all-gather.9
  328.5 46.4 reduce-scatter.10
  379.4 50.9 all-gather.11
  433.8 52.6 reduce-scatter.16
  507.5 52.8 all-reduce.2
  563.6 42.5 reduce-scatter.14
  608.5 47.6 reduce-scatter.12

commit v3 on v2

--- a/solution.py
+++ b/solution.py
@@ -4,6 +4,7 @@
 import jax.numpy as jnp
 from jax import lax
 from jax.sharding import PartitionSpec as P
+
 
 HEAD = 64
 
@@ -43,7 +44,7 @@
 
 def attend_forward(queries, key_rows, value_rows, segments):
     seq_count = segments.shape[0]
-    scores, allowed = masked_scores(
+    scores, _ = masked_scores(
         split_heads(queries, seq_count), split_heads(key_rows, seq_count), segments
     )
     largest = jnp.max(scores, axis=-1, keepdims=True)
@@ -143,7 +144,6 @@
     queries = (projected[0] + qv_bias[0]).astype(jnp.bfloat16)
     key_rows = projected[1].astype(jnp.bfloat16)
     value_rows = (projected[2] + qv_bias[1]).astype(jnp.bfloat16)
-    local_width = queries.shape[1]
 
     context, log_totals = attend_forward(queries, key_rows, value_rows, segments)
     attended = (
@@ -232,54 +232,6 @@
     )
     grad_att = grad_res.astype(jnp.bfloat16)
     out_bias_grad = jnp.sum(grad_att.astype(jnp.float32), axis=0)
-    grad_att_all = lax.all_gather(grad_att, "tensor", axis=0, tiled=True)
-    out_weight_grad = jnp.einsum(
-        "te,td->ed", context, grad_att_all, preferred_element_type=jnp.float32
-    )
-    grad_context = jnp.einsum(
-        "td,ed->te", grad_att_all, out_weight, preferred_element_type=jnp.float32
-    ).astype(jnp.bfloat16)
-    grad_queries, grad_keys, grad_values = attend_backward(
-        queries, key_rows, value_rows, segments, log_totals, grad_context
-    )
-    stacked = jnp.stack([grad_queries, grad_keys, grad_values])
-    qkv_weight_grad = jnp.einsum(
-        "td,kte->kde", gathered, stacked, preferred_element_type=jnp.float32
-    )
-    qv_bias_grad = jnp.stack(
-        [
-            jnp.sum(grad_queries.astype(jnp.float32), axis=0),
-            jnp.sum(grad_values.astype(jnp.float32), axis=0),
-        ]
-    )
-    input_grad = (
-        lax.psum_scatter(
-            jnp.einsum(
-                "kte,kde->td", stacked, qkv_weight, preferred_element_type=jnp.float32
-            ).astype(jnp.bfloat16),
-            "tensor",
-            scatter_dimension=0,
-            tiled=True,
-        ).astype(jnp.float32)
-        + grad_res
-    ).astype(jnp.bfloat16)
-
-    def reduce_over_dp(parts):
-        flat = jnp.concatenate([to_blocks(grad, axis, dp_count) for grad, axis in parts], axis=1)
-        lanes = 1024 if flat.shape[1] % 1024 == 0 else 128
-        summed = lax.psum_scatter(
-            flat.reshape(-1, lanes), "dp", scatter_dimension=0, tiled=True
-        ).reshape(-1)
-        pieces = []
-        begin = 0
-        for grad, axis in parts:
-            size = grad.size // dp_count
-            pieces.append(from_block(summed[begin : begin + size], grad.shape, axis, dp_count))
-            begin += size
-        return pieces
-
-    up_sum, down_sum = reduce_over_dp(((up_weight_grad, 0), (down_weight_grad, 1)))
-    qkv_sum, out_sum = reduce_over_dp(((qkv_weight_grad, 1), (out_weight_grad, 1)))
 
     def joined(parts):
         return jnp.concatenate([part.reshape(-1) for part in parts])
@@ -288,7 +240,7 @@
         pieces = []
         begin = 0
         for part in parts:
-            pieces.append(flat[..., begin : begin + part.size].reshape(flat.shape[:-1] + part.shape))
+            pieces.append(flat[begin : begin + part.size].reshape(part.shape))
             begin += part.size
         return pieces
 
@@ -314,13 +266,97 @@
         ),
         row_block,
     ]
-    token_sum, rows_group = parted(lax.psum(joined(token_parts), "tensor"), token_parts)
-    group_parts = [token_sum, rows_group, qv_bias_grad, up_bias_grad]
-    gathered_small = lax.all_gather(joined(group_parts), "dp", axis=0, tiled=False)
-    token_each, rows_each, qv_each, up_each = parted(gathered_small, group_parts)
-    token_grads = jnp.sum(token_each, axis=0)
-    qv_bias_total = jnp.sum(qv_each, axis=0)
-    up_bias_total = jnp.sum(up_each, axis=0)
+    small_flat = joined(token_parts)
+    small_round = lax.reduce_precision(small_flat, exponent_bits=8, mantissa_bits=7)
+    small_high = small_round.astype(jnp.bfloat16)
+    small_low = (small_flat - small_round).astype(jnp.bfloat16)
+    model_width = grad_att.shape[1]
+    small_rows = -(-2 * small_flat.size // model_width)
+    small_rows += (-(share_rows + small_rows)) % 16
+    small_pad = small_rows * model_width - 2 * small_flat.size
+    riding = jnp.concatenate(
+        [small_high, small_low, jnp.zeros((small_pad,), jnp.bfloat16)]
+    ).reshape(small_rows, model_width)
+    att_gathered = lax.all_gather(
+        jnp.concatenate([grad_att, riding], axis=0), "tensor", axis=0, tiled=False
+    )
+    grad_att_all = att_gathered[:, :share_rows].reshape(group_rows, model_width)
+    small_back = att_gathered[:, share_rows:].reshape(tensor_count, -1)
+    small_total = jnp.sum(
+        small_back[:, : small_flat.size].astype(jnp.float32)
+        + small_back[:, small_flat.size : 2 * small_flat.size].astype(jnp.float32),
+        axis=0,
+    )
+    token_sum, rows_group = parted(small_total, token_parts)
+    out_weight_grad = jnp.einsum(
+        "te,td->ed", context, grad_att_all, preferred_element_type=jnp.float32
+    )
+    grad_context = jnp.einsum(
+        "td,ed->te", grad_att_all, out_weight, preferred_element_type=jnp.float32
+    ).astype(jnp.bfloat16)
+    grad_queries, grad_keys, grad_values = attend_backward(
+        queries, key_rows, value_rows, segments, log_totals, grad_context
+    )
+    stacked = jnp.stack([grad_queries, grad_keys, grad_values])
+    qkv_weight_grad = jnp.einsum(
+        "td,kte->kde", gathered, stacked, preferred_element_type=jnp.float32
+    )
+    qv_bias_grad = jnp.stack(
+        [
+            jnp.sum(grad_queries.astype(jnp.float32), axis=0),
+            jnp.sum(grad_values.astype(jnp.float32), axis=0),
+        ]
+    )
+    input_grad = (
+        lax.psum_scatter(
+            jnp.einsum(
+                "kte,kde->td", stacked, qkv_weight, preferred_element_type=jnp.float32
+            ).astype(jnp.bfloat16),
+            "tensor",
+            scatter_dimension=0,
+            tiled=True,
+        ).astype(jnp.float32)
+        + grad_res
+    ).astype(jnp.bfloat16)
+
+    def reduce_over_dp(parts, shared):
+        blocks = [to_blocks(grad, axis, dp_count) for grad, axis in parts]
+        shared_flat = joined(shared)
+        blocks.append(jnp.broadcast_to(shared_flat[None], (dp_count, shared_flat.size)))
+        flat = jnp.concatenate(blocks, axis=1)
+        pad = (-flat.shape[1]) % 8192
+        flat = jnp.pad(flat, ((0, 0), (0, pad)))
+        summed = lax.psum_scatter(
+            flat.reshape(-1, 1024), "dp", scatter_dimension=0, tiled=True
+        ).reshape(-1)
+        pieces = []
+        begin = 0
+        for grad, axis in parts:
+            size = grad.size // dp_count
+            pieces.append(from_block(summed[begin : begin + size], grad.shape, axis, dp_count))
+            begin += size
+        return pieces, parted(summed[begin : begin + shared_flat.size], shared)
+
+    copied_rows = dp_count * dp_count * rows_group.size <= (1 << 20)
+    if copied_rows:
+        rows_shared = [
+            lax.dynamic_update_slice(
+                jnp.zeros((dp_count,) + rows_group.shape, rows_group.dtype),
+                rows_group[None],
+                (dp_index, 0, 0),
+            )
+        ]
+    else:
+        rows_shared = []
+        rows_each = lax.all_gather(rows_group.astype(jnp.bfloat16), "dp", axis=0, tiled=False)
+    (up_sum, down_sum, out_sum), shared_sums = reduce_over_dp(
+        ((up_weight_grad, 0), (down_weight_grad, 1), (out_weight_grad, 1)),
+        [token_sum, up_bias_grad] + rows_shared,
+    )
+    token_grads, up_bias_total = shared_sums[:2]
+    if copied_rows:
+        rows_each = shared_sums[2]
+    (qkv_sum,), (qv_bias_total,) = reduce_over_dp(((qkv_weight_grad, 1),), [qv_bias_grad])
     rows_all = rows_each.reshape(dp_count * seq_count, row_block.shape[1])
     width = leading.shape[1]
     classes = class_weight.shape[1]

time: 674 us -> 688 us (1.021)
  waiting for transfers between devices: 398 us -> 437 us
  blocking collectives: 20.2 us -> 0 us
  starting transfers between devices: 12 us -> 1.05 us
    unnamed x12 -> x10, waiting for transfers between devices: 42.4 us -> 0.83 us
    all_gather x1, waiting for transfers between devices: 17.1 us -> 53.1 us  [body(): lax.all_gather(jnp.concatenate([grad_att, riding], axis=0), 'tensor', axi...]
    reduce_scatter x2, waiting for transfers between devices: 38.2 us -> 67.6 us  [reduce_over_dp(): lax.psum_scatter(flat.reshape(-1, 1024), 'dp', scatter_dimension=0, tiled...]
    reduce_scatter x1, waiting for transfers between devices: 22.8 us -> 43.5 us  [body(): lax.psum_scatter(jnp.einsum('tf,df->td', grad_up, up_weight, preferred_el...]
    psum x1 -> x0, blocking collectives: 20.2 us -> none  [body(): lax.psum(joined(token_parts), 'tensor')]
    reduce_scatter x1, waiting for transfers between devices: 46.6 us -> 30.3 us  [body(): lax.psum_scatter(jnp.einsum('kte,kde->td', stacked, qkv_weight, preferred...]
    reduce_scatter x1, starting transfers between devices: 11.1 us -> 0.21 us  [body(): lax.psum_scatter(jnp.einsum('tf,df->td', grad_up, up_weight, preferred_el...]
    all_gather x1, waiting for transfers between devices: 38.4 us -> 49.3 us  [body(): grad_fed_all = lax.all_gather(grad_fed, 'tensor', axis=0, tiled=True)]
  transfers between devices with their start and end apart: 11 -> 10, of which waited for: 10 -> 9; matrix products, arithmetic and copies ran while one was open for 20% -> 9% of each run, Pallas kernels for 0% -> 0%
where the time goes in v3:
time: 688 us; the launch traced here: 679 us
  waiting for transfers between devices  437 us (64%)
  matrix products  112 us (16%)
  local copies, waits for them, and re-layouts  79.7 us (12%)
  other arithmetic  33.5 us (5%)
  between operations  15.3 us (2%)
    reduce_scatter x2, waiting for transfers between devices, reduce_over_dp(): lax.psum_scatter(flat.reshape(-1, 1024), 'dp', scatter_dimension=0, tiled...  67.6 us
    all_gather x1, waiting for transfers between devices, body(): lax.all_gather(jnp.concatenate([grad_att, riding], axis=0), 'tensor', axi...  53.1 us
    all_gather x1, waiting for transfers between devices, body(): gathered = lax.all_gather(inputs, 'tensor', axis=0, tiled=True)  52.1 us
    all_gather x1, waiting for transfers between devices, body(): first_all = lax.all_gather(first_low, 'tensor', axis=0, tiled=True)  49.5 us
    all_gather x1, waiting for transfers between devices, body(): grad_fed_all = lax.all_gather(grad_fed, 'tensor', axis=0, tiled=True)  49.3 us
    reduce_scatter x1, waiting for transfers between devices, body(): lax.psum_scatter(jnp.dot(context, out_weight, preferred_element_type=jnp....  46.1 us
    reduce_scatter x1, waiting for transfers between devices, body(): lax.psum_scatter(jnp.dot(active, down_weight, preferred_element_type=jnp....  44.9 us
    reduce_scatter x1, waiting for transfers between devices, body(): lax.psum_scatter(jnp.einsum('tf,df->td', grad_up, up_weight, preferred_el...  43.5 us
  transfers between devices with their start and end apart: 10, of which 9 were waited for; matrix products, arithmetic and copies ran while one was open for 9% of the time, Pallas kernels for 0%

profile of v3, /device:TPU:0, one launch (start us, length us, event | category | flops | bytes accessed | tf_op | source)
XLA Modules:
  0.0 679.0 jit_solution(6284683927545751960)
XLA Ops:
  10.2 52.1 %all-gather.6.cloned.1.call-done = bf16[1536,768]{1,0:T(8,128)(2,1)} async-done(((bf16[384,768]{1,0:T(8,128)(2,1)}), bf16[1536,768]{1,0:T(8,128)(2,1)}) %all-gather.6.cloned.1.call-update) | async-done | bytes 2359312 | tf_op jit(solution)/shard_map/all_gather | solution.py:141
  62.3 3.5 convolution_bitcast_fusion
  88.8 46.1 %reduce-scatter.7.cloned.1.call-done = bf16[384,768]{1,0:T(8,128)(2,1)} async-done(((bf16[1536,768]{1,0:T(8,128)(2,1)}), bf16[384,768]{1,0:T(8,128)(2,1)}) %reduce-scatter.7.cloned.1.call-update) | async-done | bytes 589840 | tf_op jit(solution)/shard_map/reduce_scatter | solution.py:150
  139.0 49.5 %all-gather.8.cloned.1.call-done = bf16[1536,768]{1,0:T(8,128)(2,1)} async-done(((bf16[384,768]{1,0:T(8,128)(2,1)}), bf16[1536,768]{1,0:T(8,128)(2,1)}) %all-gather.8.cloned.1.call-update) | async-done | bytes 2359312 | tf_op jit(solution)/shard_map/all_gather | solution.py:163
  188.4 14.5 %multiply_convert_fusion = (bf16[1536,768]{1,0:T(8,128)(2,1)S(1)}, f32[1536,768]{1,0:T(8,128)}, f32[1536,768]{1,0:T(8,128)}) fusion(f32[768]{0:T(1024)} %param.30, bf16[1536,768]{1,0:T(8,128)(2,1)} %all-gather.8.cloned.1.call-done, bf16[768,768]{1,0:T(8,128)(2,1)S(1)} %copy-done), kind=kOutput, calls=%fused_computation.23 | convolution fusion | flops 1889796096 | bytes 15338496 | tf_op jit(solution)/shard_map/dot_general | solution.py:164
  209.5 44.9 %reduce-scatter.9.cloned.1.call-done = bf16[384,768]{1,0:T(8,128)(2,1)} async-done(((bf16[1536,768]{1,0:T(8,128)(2,1)}), bf16[384,768]{1,0:T(8,128)(2,1)}) %reduce-scatter.9.cloned.1.call-update) | async-done | bytes 589840 | tf_op jit(solution)/shard_map/reduce_scatter | solution.py:168
  265.2 49.3 %all-gather.10.cloned.1.call-done = bf16[1536,768]{1,0:T(8,128)(2,1)} async-done(((bf16[384,768]{1,0:T(8,128)(2,1)}), bf16[1536,768]{1,0:T(8,128)(2,1)}) %all-gather.10.cloned.1.call-update) | async-done | bytes 2359312 | tf_op jit(solution)/shard_map/all_gather | solution.py:210
  314.5 8.8 %convert_reduce_fusion = (f32[768]{0:T(1024)}, bf16[1536,768]{1,0:T(8,128)(2,1)S(1)}) fusion(f32[1536,768]{1,0:T(8,128)} %get-tuple-element.113, f32[1536,768]{1,0:T(8,128)} %get-tuple-element.132, f32[768]{0:T(1024)} %param.30, bf16[1536,768]{1,0:T(8,128)(2,1)} %all-gather.10.cloned.1.call-done, bf16[768,768]{1,0:T(8,128)(2,1)} %param.31), kind=kOutput, calls=%fused_computation.17 | convolution fusion | flops 1831992576 | bytes 15341568 | tf_op jit(solution)/shard_map/td,fd->tf/dot_general | solution.py:214
  324.7 3.5 convolution_convert_fusion
  331.4 43.5 %reduce-scatter.11.cloned.1.call-done = bf16[384,768]{1,0:T(8,128)(2,1)} async-done(((bf16[1536,768]{1,0:T(8,128)(2,1)}), bf16[384,768]{1,0:T(8,128)(2,1)}) %reduce-scatter.11.cloned.1.call-update) | async-done | bytes 589840 | tf_op jit(solution)/shard_map/reduce_scatter | solution.py:221
  383.9 53.1 %all-gather.12.cloned.1.call-done = bf16[1664,768]{1,0:T(8,128)(2,1)} async-done(((bf16[416,768]{1,0:T(8,128)(2,1)}), bf16[1664,768]{1,0:T(8,128)(2,1)}) %all-gather.12.cloned.1.call-update) | async-done | bytes 2555920 | tf_op jit(solution)/shard_map/all_gather | solution.py:280
  442.0 5.0 fusion.77
  447.0 7.2 %convert_reduce_fusion.1 = (f32[3,64]{1,0:T(4,128)S(1)}, bf16[3,3,64,512]{3,2,1,0:T(8,128)(2,1)}) fusion(f32[3,3,512,512]{2,3,1,0:T(8,128)} %copy-done.4, f32[3,3,512]{2,1,0:T(4,128)S(1)} %log_add_fusion, pred[3,512,512]{1,2,0:T(8,128)(4,1)S(1)} %copy-done.12, bf16[3,512,3,64]{1,0,3,2:T(4,128)(2,1)S(1)} %reshape.275), kind=kOutput, calls=%fused_computation.70 | convolution fusion | flops 312311616 | bytes 11422464 | tf_op jit(solution)/shard_map/rhqk,rqhe->rkhe/dot_general | solution.py:72
  454.3 15.1 %convert_reduce_fusion.2 = (f32[3,64]{1,0:T(4,128)S(1)}, bf16[3,3,64,512]{3,2,1,0:T(8,128)(2,1)S(1)}) fusion(f32[3,3,512,512]{2,3,1,0:T(8,128)} %fusion.77, f32[3,3,512,512]{2,3,1,0:T(8,128)} %copy-done.4, f32[3,3,512]{2,1,0:T(4,128)S(1)} %log_add_fusion, pred[3,512,512]{1,2,0:T(8,128)(4,1)S(1)} %copy-done.12, bf16[3,512,3,64]{1,0,3,2:T(4,128)(2,1)S(1)} %copy-done.19), kind=kOutput, calls=%fused_computation.71 | convolution fusion | flops 329126720 | bytes 20859648 | tf_op jit(solution)/shard_map/rhqk,rkhe->rqhe/dot_general | solution.py:85
  469.4 15.9 %fusion.63 = bf16[3,512,3,64]{1,3,2,0:T(8,128)(2,1)} fusion(f32[3,3,512,512]{2,3,1,0:T(8,128)} %fusion.77, f32[3,3,512,512]{2,3,1,0:T(8,128)} %copy-done.4, f32[3,3,512]{2,1,0:T(4,128)S(1)} %log_add_fusion, pred[3,512,512]{1,2,0:T(8,128)(4,1)S(1)} %copy-done.12, bf16[3,512,3,64]{1,0,3,2:T(4,128)(2,1)S(1)} %copy-done.21), kind=kOutput, calls=%fused_computation.67 | convolution fusion | flops 328537088 | bytes 20858880 | tf_op jit(solution)/shard_map/rhqk,rqhe->rkhe/dot_general | solution.py:89
  506.0 4.4 fusion.129
  512.8 5.3 reshape.283
  518.1 4.4 fusion.128
  532.2 5.2 bitcast_convert_fusion
  539.1 9.5 %maximum_maximum_fusion = f32[8,226632]{1,0:T(8,128)S(1)} fusion(f32[8,18432]{1,0:T(8,128)} %reshape.284, f32[8,73728]{1,0:T(8,128)} %reshape.283, f32[8,73728]{1,0:T(8,128)S(1)} %copy-done.6, f32[226632]{0:T(1024)S(1)} %pad_maximum_fusion.1), kind=kLoop, calls=%fused_computation.9 | loop fusion | flops 5439168 | bytes 13467168 | tf_op jit(solution)/shard_map/concatenate | solution.py:326
  548.5 3.5 pad.9
  552.1 7.4 %reshape.287 = f32[1792,1024]{1,0:T(8,128)} reshape(f32[8,229376]{1,0:T(8,128)} %pad.9) | data formatting | bytes 14680064 | tf_op jit(solution)/shard_map/reshape | solution.py:330
  563.1 30.3 %reduce-scatter.13.cloned.1.call-done = bf16[384,768]{1,0:T(8,128)(2,1)} async-done(((bf16[1536,768]{1,0:T(8,128)(2,1)}), bf16[384,768]{1,0:T(8,128)(2,1)}) %reduce-scatter.13.cloned.1.call-update) | async-done | bytes 589840 | tf_op jit(solution)/shard_map/reduce_scatter | solution.py:311
  595.3 67.6 %reduce-scatter.17.cloned.1.call-done = f32[224,1024]{1,0:T(8,128)} async-done(((f32[1792,1024]{1,0:T(8,128)}), f32[224,1024]{1,0:T(8,128)}) %reduce-scatter.17.cloned.1.call-update) | async-done | bytes 917520 | tf_op jit(solution)/shard_map/reduce_scatter | solution.py:329
  (267 shorter events, 114.2 us)
Async XLA Ops:
  7.2 181.2 %copy-start = (bf16[768,768]{1,0:T(8,128)(2,1)S(1)}, bf16[768,768]{1,0:T(8,128)(2,1)}, u32[]{:S(2)}) copy-start(bf16[768,768]{1,0:T(8,128)(2,1)} %param.29) | copy-start | bytes 3538948
  7.2 55.1 %all-gather.6.cloned.1.call-start = ((), (), s32[]{:S(2)}) async-start(), calls=%async_computation.6 | async-start | bytes 2949120 | tf_op jit(solution)/shard_map/all_gather | solution.py:141
  7.9 126.9 %reduce-scatter.7.cloned.1.call-start = ((), (), s32[]{:S(2)}) async-start(), calls=%async_computation.7 | async-start | bytes 2949120 | tf_op jit(solution)/shard_map/reduce_scatter | solution.py:150
  10.2 70.0 %copy-start.11 = (pred[3,512,512]{1,2,0:T(8,128)(4,1)}, pred[3,512,512]{1,2,0:T(8,128)(4,1)S(1)}, u32[]{:S(2)}) copy-start(pred[3,512,512]{1,2,0:T(8,128)(4,1)S(1)} %broadcast_compare_fusion) | copy-start | bytes 2359300
  86.0 48.9 %copy-start.2 = (bf16[384,768]{1,0:T(8,128)(2,1)S(1)}, bf16[384,768]{1,0:T(8,128)(2,1)}, u32[]{:S(2)}) copy-start(bf16[384,768]{1,0:T(8,128)(2,1)} %param.20) | copy-start | bytes 1769476
  86.0 48.9 %copy-start.28 = (f32[768]{0:T(1024)S(1)}, f32[768]{0:T(1024)}, u32[]{:S(2)}) copy-start(f32[768]{0:T(1024)} %param.26) | copy-start | bytes 9220
  88.2 49.5 %copy-start.33 = (f32[768]{0:T(1024)S(1)}, f32[768]{0:T(1024)}, u32[]{:S(2)}) copy-start(f32[768]{0:T(1024)} %param.27) | copy-start | bytes 9220
  88.2 49.5 %copy-start.39 = (f32[768]{0:T(1024)S(1)}, f32[768]{0:T(1024)}, u32[]{:S(2)}) copy-start(f32[768]{0:T(1024)} %param.28) | copy-start | bytes 9220
  88.2 100.2 %all-gather.8.cloned.1.call-start = ((), (), s32[]{:S(2)}) async-start(), calls=%async_computation.8 | async-start | bytes 2949120 | tf_op jit(solution)/shard_map/all_gather | solution.py:163
  138.9 65.4 %copy-start.56 = (bf16[768,768]{1,0:T(8,128)(2,1)S(1)}, bf16[768,768]{1,0:T(8,128)(2,1)}, u32[]{:S(2)}) copy-start(bf16[768,768]{1,0:T(8,128)(2,1)} %param.31) | copy-start | bytes 3538948
  138.9 115.5 %reduce-scatter.9.cloned.1.call-start = ((), (), s32[]{:S(2)}) async-start(), calls=%async_computation.9 | async-start | bytes 2949120 | tf_op jit(solution)/shard_map/reduce_scatter | solution.py:168
  207.8 106.8 %all-gather.10.cloned.1.call-start = ((), (), s32[]{:S(2)}) async-start(), calls=%async_computation.10 | async-start | bytes 2949120 | tf_op jit(solution)/shard_map/all_gather | solution.py:210
  209.5 48.4 %copy-start.9 = (bf16[768,768]{1,0:T(8,128)(2,1)S(1)}, bf16[768,768]{1,0:T(8,128)(2,1)}, u32[]{:S(2)}) copy-start(bf16[768,768]{1,0:T(8,128)(2,1)} %param.35) | copy-start | bytes 3538948
  265.0 109.9 %reduce-scatter.11.cloned.1.call-start = ((), (), s32[]{:S(2)}) async-start(), calls=%async_computation.11 | async-start | bytes 2949120 | tf_op jit(solution)/shard_map/reduce_scatter | solution.py:221
  328.2 108.8 %all-gather.12.cloned.1.call-start = ((), (), s32[]{:S(2)}) async-start(), calls=%async_computation.15 | async-start | bytes 3194880 | tf_op jit(solution)/shard_map/all_gather | solution.py:280
  383.8 175.7 %reduce-scatter.15.cloned.1.call-start = ((), (), s32[]{:S(2)}) async-start(), calls=%async_computation.13 | async-start | bytes 2064384 | tf_op jit(solution)/shard_map/reduce_scatter | solution.py:329
  447.0 7.2 %copy-start.19 = (bf16[3,512,3,64]{1,0,3,2:T(4,128)(2,1)S(1)}, bf16[3,512,3,64]{1,0,3,2:T(4,128)(2,1)}, u32[]{:S(2)}) copy-start(bf16[3,512,3,64]{1,0,3,2:T(4,128)(2,1)} %convert_element_type.217) | copy-start | bytes 1769476
  454.3 15.1 %copy-start.21 = (bf16[3,512,3,64]{1,0,3,2:T(4,128)(2,1)S(1)}, bf16[3,512,3,64]{1,0,3,2:T(4,128)(2,1)}, u32[]{:S(2)}) copy-start(bf16[3,512,3,64]{1,0,3,2:T(4,128)(2,1)} %copy-done.20) | copy-start | bytes 1769476
  469.3 16.2 %copy-start.22 = (bf16[3,3,64,512]{3,2,1,0:T(8,128)(2,1)S(1)}, bf16[3,3,64,512]{3,2,1,0:T(8,128)(2,1)}, u32[]{:S(2)}) copy-start(bf16[3,3,64,512]{3,2,1,0:T(8,128)(2,1)} %get-tuple-element.140) | copy-start | bytes 1769476
  504.3 89.1 %reduce-scatter.13.cloned.1.call-start = ((), (), s32[]{:S(2)}) async-start(), calls=%async_computation.12 | async-start | bytes 2949120 | tf_op jit(solution)/shard_map/reduce_scatter | solution.py:311
  537.4 125.5 %reduce-scatter.17.cloned.1.call-start = ((), (), s32[]{:S(2)}) async-start(), calls=%async_computation.14 | async-start | bytes 8257536 | tf_op jit(solution)/shard_map/reduce_scatter | solution.py:329
  559.5 33.9 %copy-start.10 = (f32[384,768]{1,0:T(8,128)S(1)}, f32[384,768]{1,0:T(8,128)}, u32[]{:S(2)}) copy-start(f32[384,768]{1,0:T(8,128)} %get-tuple-element.109) | copy-start | bytes 3538948
  662.9 5.6 copy-start.13
  664.6 7.3 %copy-start.1 = (bf16[768,768]{1,0:T(8,128)(2,1)S(1)}, bf16[768,768]{1,0:T(8,128)(2,1)}, u32[]{:S(2)}) copy-start(bf16[768,768]{1,0:T(8,128)(2,1)} %param.29) | copy-start | bytes 3538948
  (47 other events, 113.3 us)
Sparse Core Ops, SparseCore 0:
  9.6 52.6 all-gather.5
  88.4 46.4 reduce-scatter.6
  139.0 49.3 all-gather.7
  207.9 46.4 reduce-scatter.8
  265.1 49.3 all-gather.9
  328.4 46.4 reduce-scatter.10
  383.9 53.0 all-gather.11
  504.4 38.2 reduce-scatter.14
  545.6 47.6 reduce-scatter.12
  596.6 66.3 reduce-scatter.16

commit v4 on v3

--- a/solution.py
+++ b/solution.py
@@ -95,17 +95,6 @@
         grad_keys.reshape(full_shape).astype(jnp.bfloat16),
         grad_values.reshape(full_shape).astype(jnp.bfloat16),
     )
-
-
-def to_blocks(array, axis, count):
-    shape = array.shape
-    split = shape[:axis] + (count, shape[axis] // count) + shape[axis + 1 :]
-    return jnp.moveaxis(array.reshape(split), axis, 0).reshape(count, -1)
-
-
-def from_block(flat, shape, axis, count):
-    local = shape[:axis] + (shape[axis] // count,) + shape[axis + 1 :]
-    return flat.reshape(local)
 
 
 def body(
@@ -208,8 +197,8 @@
     grad_fed = grad_second.astype(jnp.bfloat16)
     down_bias_grad = jnp.sum(grad_fed.astype(jnp.float32), axis=0)
     grad_fed_all = lax.all_gather(grad_fed, "tensor", axis=0, tiled=True)
-    down_weight_grad = jnp.einsum(
-        "tf,td->fd", active, grad_fed_all, preferred_element_type=jnp.float32
+    down_weight_grad_t = jnp.einsum(
+        "td,tf->df", grad_fed_all, active, preferred_element_type=jnp.float32
     )
     grad_active = jnp.einsum(
         "td,fd->tf", grad_fed_all, down_weight, preferred_element_type=jnp.float32
@@ -244,12 +233,14 @@
             begin += part.size
         return pieces
 
-    row_block = jnp.concatenate(
+    model_width = grad_att.shape[1]
+    classes = class_weight.shape[1]
+    row_block = jnp.stack(
         [
             leading.astype(jnp.float32) * owned,
             grad_pre.astype(jnp.float32),
             pooled_low.astype(jnp.float32) * owned,
-            grad_logits.astype(jnp.float32),
+            jnp.pad(grad_logits.astype(jnp.float32), ((0, 0), (0, model_width - classes))),
         ],
         axis=1,
     )
@@ -270,7 +261,6 @@
     small_round = lax.reduce_precision(small_flat, exponent_bits=8, mantissa_bits=7)
     small_high = small_round.astype(jnp.bfloat16)
     small_low = (small_flat - small_round).astype(jnp.bfloat16)
-    model_width = grad_att.shape[1]
     small_rows = -(-2 * small_flat.size // model_width)
     small_rows += (-(share_rows + small_rows)) % 16
     small_pad = small_rows * model_width - 2 * small_flat.size
@@ -288,8 +278,8 @@
         axis=0,
     )
     token_sum, rows_group = parted(small_total, token_parts)
-    out_weight_grad = jnp.einsum(
-        "te,td->ed", context, grad_att_all, preferred_element_type=jnp.float32
+    out_weight_grad_t = jnp.einsum(
+        "td,te->de", grad_att_all, context, preferred_element_type=jnp.float32
     )
     grad_context = jnp.einsum(
         "td,ed->te", grad_att_all, out_weight, preferred_element_type=jnp.float32
@@ -299,7 +289,10 @@
     )
     stacked = jnp.stack([grad_queries, grad_keys, grad_values])
     qkv_weight_grad = jnp.einsum(
-        "td,kte->kde", gathered, stacked, preferred_element_type=jnp.float32
+        "td,tq->dq",
+        gathered,
+        jnp.concatenate([grad_queries, grad_keys, grad_values], axis=1),
+        preferred_element_type=jnp.float32,
     )
     qv_bias_grad = jnp.stack(
         [
@@ -319,51 +312,63 @@
         + grad_res
     ).astype(jnp.bfloat16)
 
-    def reduce_over_dp(parts, shared):
-        blocks = [to_blocks(grad, axis, dp_count) for grad, axis in parts]
-        shared_flat = joined(shared)
-        blocks.append(jnp.broadcast_to(shared_flat[None], (dp_count, shared_flat.size)))
-        flat = jnp.concatenate(blocks, axis=1)
-        pad = (-flat.shape[1]) % 8192
-        flat = jnp.pad(flat, ((0, 0), (0, pad)))
+    def stacked_sum(parts, dtype):
+        flat = jnp.concatenate([part.astype(dtype) for part in parts], axis=1)
+        lanes = flat.shape[2]
+        pad = (-flat.shape[1]) % 16
+        flat = jnp.pad(flat, ((0, 0), (0, pad), (0, 0)))
         summed = lax.psum_scatter(
-            flat.reshape(-1, 1024), "dp", scatter_dimension=0, tiled=True
-        ).reshape(-1)
+            flat.reshape(-1, lanes), "dp", scatter_dimension=0, tiled=True
+        )
         pieces = []
         begin = 0
-        for grad, axis in parts:
-            size = grad.size // dp_count
-            pieces.append(from_block(summed[begin : begin + size], grad.shape, axis, dp_count))
-            begin += size
-        return pieces, parted(summed[begin : begin + shared_flat.size], shared)
+        for part in parts:
+            pieces.append(summed[begin : begin + part.shape[1]])
+            begin += part.shape[1]
+        return pieces
+
+    def in_blocks(grad):
+        return grad.reshape(dp_count, grad.shape[0] // dp_count, grad.shape[1])
+
+    def copied(flat, lanes):
+        rows = -(-flat.size // lanes)
+        flat = jnp.pad(flat, (0, rows * lanes - flat.size)).reshape(1, rows, lanes)
+        return jnp.broadcast_to(flat, (dp_count, rows, lanes))
 
     copied_rows = dp_count * dp_count * rows_group.size <= (1 << 20)
+    out_blocks = in_blocks(out_weight_grad_t).reshape(dp_count, -1, model_width)
+    early_parts = [in_blocks(up_weight_grad), in_blocks(down_weight_grad_t), out_blocks]
     if copied_rows:
-        rows_shared = [
-            lax.dynamic_update_slice(
-                jnp.zeros((dp_count,) + rows_group.shape, rows_group.dtype),
-                rows_group[None],
-                (dp_index, 0, 0),
-            )
-        ]
+        rows_slotted = lax.dynamic_update_slice(
+            jnp.zeros((dp_count,) + rows_group.shape, rows_group.dtype),
+            rows_group[None],
+            (dp_index, 0, 0, 0),
+        )
+        early_parts.append(copied(rows_slotted.reshape(-1), model_width))
     else:
-        rows_shared = []
         rows_each = lax.all_gather(rows_group.astype(jnp.bfloat16), "dp", axis=0, tiled=False)
-    (up_sum, down_sum, out_sum), shared_sums = reduce_over_dp(
-        ((up_weight_grad, 0), (down_weight_grad, 1), (out_weight_grad, 1)),
-        [token_sum, up_bias_grad] + rows_shared,
-    )
-    token_grads, up_bias_total = shared_sums[:2]
+    early_sums = stacked_sum(early_parts, jnp.bfloat16)
+    up_sum = early_sums[0].astype(jnp.float32)
+    down_sum = early_sums[1].astype(jnp.float32).T
+    out_sum = early_sums[2].reshape(-1, out_weight_grad_t.shape[1]).astype(jnp.float32).T
     if copied_rows:
-        rows_each = shared_sums[2]
-    (qkv_sum,), (qv_bias_total,) = reduce_over_dp(((qkv_weight_grad, 1),), [qv_bias_grad])
-    rows_all = rows_each.reshape(dp_count * seq_count, row_block.shape[1])
-    width = leading.shape[1]
-    classes = class_weight.shape[1]
-    leading_all = rows_all[:, :width].astype(jnp.bfloat16)
-    grad_pre_all = rows_all[:, width : 2 * width].astype(jnp.bfloat16)
-    pooled_all = rows_all[:, 2 * width : 3 * width].astype(jnp.bfloat16)
-    grad_logits_all = rows_all[:, 3 * width : 3 * width + classes].astype(jnp.bfloat16)
+        rows_each = early_sums[3].reshape(-1)[: rows_slotted.size]
+    late_shared = [token_sum, up_bias_grad, qv_bias_grad]
+    qkv_lanes = qkv_weight_grad.shape[1]
+    late_sums = stacked_sum(
+        [in_blocks(qkv_weight_grad), copied(joined(late_shared), qkv_lanes)], jnp.float32
+    )
+    qkv_sum = jnp.transpose(
+        late_sums[0].reshape(late_sums[0].shape[0], 3, qkv_lanes // 3), (1, 0, 2)
+    )
+    token_grads, up_bias_total, qv_bias_total = parted(
+        late_sums[1].reshape(-1), late_shared
+    )
+    rows_all = rows_each.reshape(dp_count * seq_count, 4, model_width).astype(jnp.bfloat16)
+    leading_all = rows_all[:, 0]
+    grad_pre_all = rows_all[:, 1]
+    pooled_all = rows_all[:, 2]
+    grad_logits_all = rows_all[:, 3, :classes]
     pool_weight_grad = jnp.einsum(
         "rd,re->de", leading_all, grad_pre_all, preferred_element_type=jnp.float32
     )

time: 688 us -> 668 us (0.971)
  local copies, waits for them, and re-layouts: 79.7 us -> 48.8 us
  waiting for transfers between devices: 437 us -> 448 us
    reshape x13 -> x1, local copies, waits for them, and re-layouts: 31.5 us -> 0.08 us  [body(): late_sums[1].reshape(-1)]
    unnamed x10 -> x11, waiting for transfers between devices: 0.83 us -> 18.4 us
    reduce_scatter x2 -> x1, waiting for transfers between devices: 67.6 us -> 50.6 us  [stacked_sum(): lax.psum_scatter(flat.reshape(-1, lanes), 'dp', scatter_dimension=0, tile...]
    reduce_scatter x1, waiting for transfers between devices: 30.3 us -> 45.1 us  [body(): lax.psum_scatter(jnp.einsum('kte,kde->td', stacked, qkv_weight, preferred...]
    unnamed x131 -> x139, local copies, waits for them, and re-layouts: 17.7 us -> 14.3 us
  transfers between devices with their start and end apart: 10 -> 10, of which waited for: 9 -> 10; matrix products, arithmetic and copies ran while one was open for 9% -> 6% of each run, Pallas kernels for 0% -> 0%
where the time goes in v4:
time: 668 us; the launch traced here: 658 us
  waiting for transfers between devices  448 us (67%)
  matrix products  109 us (16%)
  local copies, waits for them, and re-layouts  48.8 us (7%)
  other arithmetic  34.6 us (5%)
  between operations  15.6 us (2%)
    all_gather x1, waiting for transfers between devices, body(): lax.all_gather(jnp.concatenate([grad_att, riding], axis=0), 'tensor', axi...  54 us
    all_gather x1, waiting for transfers between devices, body(): gathered = lax.all_gather(inputs, 'tensor', axis=0, tiled=True)  52.1 us
    reduce_scatter x1, waiting for transfers between devices, stacked_sum(): lax.psum_scatter(flat.reshape(-1, lanes), 'dp', scatter_dimension=0, tile...  50.6 us
    all_gather x1, waiting for transfers between devices, body(): first_all = lax.all_gather(first_low, 'tensor', axis=0, tiled=True)  49.5 us
    all_gather x1, waiting for transfers between devices, body(): grad_fed_all = lax.all_gather(grad_fed, 'tensor', axis=0, tiled=True)  49.1 us
    reduce_scatter x1, waiting for transfers between devices, body(): lax.psum_scatter(jnp.dot(context, out_weight, preferred_element_type=jnp....  46.4 us
    reduce_scatter x1, waiting for transfers between devices, body(): lax.psum_scatter(jnp.einsum('kte,kde->td', stacked, qkv_weight, preferred...  45.1 us
    reduce_scatter x1, waiting for transfers between devices, body(): lax.psum_scatter(jnp.dot(active, down_weight, preferred_element_type=jnp....  44.9 us
  transfers between devices with their start and end apart: 10, of which 10 were waited for; matrix products, arithmetic and copies ran while one was open for 6% of the time, Pallas kernels for 0%

profile of v4, /device:TPU:0, one launch (start us, length us, event | category | flops | bytes accessed | tf_op | source)
XLA Modules:
  0.0 658.3 jit_solution(13067224307184980820)
XLA Ops:
  10.2 52.1 %all-gather.6.cloned.1.call-done = bf16[1536,768]{1,0:T(8,128)(2,1)} async-done(((bf16[384,768]{1,0:T(8,128)(2,1)}), bf16[1536,768]{1,0:T(8,128)(2,1)}) %all-gather.6.cloned.1.call-update) | async-done | bytes 2359312 | tf_op jit(solution)/shard_map/all_gather | solution.py:130
  62.3 3.5 convolution_bitcast_fusion
  81.4 3.0 fusion.82
  88.6 46.4 %reduce-scatter.9.cloned.1.call-done = bf16[384,768]{1,0:T(8,128)(2,1)} async-done(((bf16[1536,768]{1,0:T(8,128)(2,1)}), bf16[384,768]{1,0:T(8,128)(2,1)}) %reduce-scatter.9.cloned.1.call-update) | async-done | bytes 589840 | tf_op jit(solution)/shard_map/reduce_scatter | solution.py:139
  139.1 49.5 %all-gather.8.cloned.1.call-done = bf16[1536,768]{1,0:T(8,128)(2,1)} async-done(((bf16[384,768]{1,0:T(8,128)(2,1)}), bf16[1536,768]{1,0:T(8,128)(2,1)}) %all-gather.8.cloned.1.call-update) | async-done | bytes 2359312 | tf_op jit(solution)/shard_map/all_gather | solution.py:152
  188.5 14.5 %multiply_convert_fusion = (bf16[1536,768]{1,0:T(8,128)(2,1)S(1)}, f32[1536,768]{1,0:T(8,128)}, f32[1536,768]{1,0:T(8,128)}) fusion(f32[768]{0:T(1024)} %param.30, bf16[1536,768]{1,0:T(8,128)(2,1)} %all-gather.8.cloned.1.call-done, bf16[768,768]{1,0:T(8,128)(2,1)S(1)} %copy-done), kind=kOutput, calls=%fused_computation.27 | convolution fusion | flops 1889796096 | bytes 15338496 | tf_op jit(solution)/shard_map/dot_general | solution.py:153
  204.5 3.4 convolution_convert_fusion.1
  209.7 44.9 %reduce-scatter.11.cloned.1.call-done = bf16[384,768]{1,0:T(8,128)(2,1)} async-done(((bf16[1536,768]{1,0:T(8,128)(2,1)}), bf16[384,768]{1,0:T(8,128)(2,1)}) %reduce-scatter.11.cloned.1.call-update) | async-done | bytes 589840 | tf_op jit(solution)/shard_map/reduce_scatter | solution.py:157
  265.1 49.1 %all-gather.10.cloned.1.call-done = bf16[1536,768]{1,0:T(8,128)(2,1)} async-done(((bf16[384,768]{1,0:T(8,128)(2,1)}), bf16[1536,768]{1,0:T(8,128)(2,1)}) %all-gather.10.cloned.1.call-update) | async-done | bytes 2359312 | tf_op jit(solution)/shard_map/all_gather | solution.py:199
  314.1 8.7 %convert_reduce_fusion = (f32[768]{0:T(1024)}, bf16[1536,768]{1,0:T(8,128)(2,1)S(1)}) fusion(f32[1536,768]{1,0:T(8,128)} %get-tuple-element.117, f32[1536,768]{1,0:T(8,128)} %get-tuple-element.133, f32[768]{0:T(1024)} %param.30, bf16[1536,768]{1,0:T(8,128)(2,1)} %all-gather.10.cloned.1.call-done, bf16[768,768]{1,0:T(8,128)(2,1)} %param.31), kind=kOutput, calls=%fused_computation.21 | convolution fusion | flops 1831992576 | bytes 15341568 | tf_op jit(solution)/shard_map/td,fd->tf/dot_general | solution.py:203
  324.4 3.5 convolution_convert_fusion
  336.0 38.5 %reduce-scatter.13.cloned.1.call-done = bf16[384,768]{1,0:T(8,128)(2,1)} async-done(((bf16[1536,768]{1,0:T(8,128)(2,1)}), bf16[384,768]{1,0:T(8,128)(2,1)}) %reduce-scatter.13.cloned.1.call-update) | async-done | bytes 589840 | tf_op jit(solution)/shard_map/reduce_scatter | solution.py:210
  385.6 54.0 %all-gather.12.cloned.1.call-done = bf16[1728,768]{1,0:T(8,128)(2,1)} async-done(((bf16[432,768]{1,0:T(8,128)(2,1)}), bf16[1728,768]{1,0:T(8,128)(2,1)}) %all-gather.12.cloned.1.call-update) | async-done | bytes 2654224 | tf_op jit(solution)/shard_map/all_gather | solution.py:270
  444.7 5.1 fusion.93
  449.8 16.1 %convert_reduce_fusion.2 = (f32[3,64]{1,0:T(4,128)S(1)}, bf16[3,3,64,512]{3,2,1,0:T(8,128)(2,1)}) fusion(f32[3,3,512,512]{2,3,1,0:T(8,128)} %fusion.93, f32[3,3,512,512]{2,3,1,0:T(8,128)} %copy-done.3, f32[3,3,512]{2,1,0:T(4,128)} %log_add_fusion, pred[3,512,512]{1,2,0:T(8,128)(4,1)S(1)} %copy-done.13, bf16[3,512,3,64]{1,0,3,2:T(4,128)(2,1)} %convert_element_type.256), kind=kOutput, calls=%fused_computation.90 | convolution fusion | flops 329126720 | bytes 20859648 | tf_op jit(solution)/shard_map/rhqk,rkhe->rqhe/dot_general | solution.py:85
  465.9 16.1 %fusion.79 = bf16[3,512,3,64]{1,3,2,0:T(8,128)(2,1)} fusion(f32[3,3,512,512]{2,3,1,0:T(8,128)} %fusion.93, f32[3,3,512,512]{2,3,1,0:T(8,128)} %copy-done.3, f32[3,3,512]{2,1,0:T(4,128)} %log_add_fusion, pred[3,512,512]{1,2,0:T(8,128)(4,1)S(1)} %copy-done.13, bf16[3,512,3,64]{1,0,3,2:T(4,128)(2,1)S(1)} %copy-done.24), kind=kOutput, calls=%fused_computation.85 | convolution fusion | flops 328537088 | bytes 20858880 | tf_op jit(solution)/shard_map/rhqk,rqhe->rkhe/dot_general | solution.py:89
  482.1 6.5 convert_reduce_fusion.1
  504.0 4.9 bitcast_convert_fusion
  509.3 4.7 convolution_convert_fusion.4
  514.0 3.1 convolution_convert_fusion.5
  519.4 3.1 fusion.47
  522.5 17.6 %reduce-scatter.19.cloned.1.call-done = f32[112,576]{1,0:T(8,128)} async-done(((f32[896,576]{1,0:T(8,128)}), f32[112,576]{1,0:T(8,128)}) %reduce-scatter.19.cloned.1.call-update) | async-done | bytes 258064
  545.6 45.1 %reduce-scatter.15.cloned.1.call-done = bf16[384,768]{1,0:T(8,128)(2,1)} async-done(((bf16[1536,768]{1,0:T(8,128)(2,1)}), bf16[384,768]{1,0:T(8,128)(2,1)}) %reduce-scatter.15.cloned.1.call-update) | async-done | bytes 589840 | tf_op jit(solution)/shard_map/reduce_scatter | solution.py:304
  592.6 50.6 %reduce-scatter.17.cloned.1.call-done = bf16[320,768]{1,0:T(8,128)(2,1)} async-done(((bf16[2560,768]{1,0:T(8,128)(2,1)}), bf16[320,768]{1,0:T(8,128)(2,1)}) %reduce-scatter.17.cloned.1.call-update) | async-done | bytes 491536 | tf_op jit(solution)/shard_map/reduce_scatter | solution.py:320
  (274 shorter events, 98.7 us)
Async XLA Ops:
  7.2 181.3 %copy-start = (bf16[768,768]{1,0:T(8,128)(2,1)S(1)}, bf16[768,768]{1,0:T(8,128)(2,1)}, u32[]{:S(2)}) copy-start(bf16[768,768]{1,0:T(8,128)(2,1)} %param.29) | copy-start | bytes 3538948
  7.2 55.1 %all-gather.6.cloned.1.call-start = ((), (), s32[]{:S(2)}) async-start(), calls=%async_computation.6 | async-start | bytes 2949120 | tf_op jit(solution)/shard_map/all_gather | solution.py:130
  7.9 127.0 %reduce-scatter.9.cloned.1.call-start = ((), (), s32[]{:S(2)}) async-start(), calls=%async_computation.7 | async-start | bytes 2949120 | tf_op jit(solution)/shard_map/reduce_scatter | solution.py:139
  10.2 70.0 %copy-start.12 = (pred[3,512,512]{1,2,0:T(8,128)(4,1)}, pred[3,512,512]{1,2,0:T(8,128)(4,1)S(1)}, u32[]{:S(2)}) copy-start(pred[3,512,512]{1,2,0:T(8,128)(4,1)S(1)} %broadcast_compare_fusion) | copy-start | bytes 2359300
  86.0 48.9 %copy-start.1 = (bf16[384,768]{1,0:T(8,128)(2,1)S(1)}, bf16[384,768]{1,0:T(8,128)(2,1)}, u32[]{:S(2)}) copy-start(bf16[384,768]{1,0:T(8,128)(2,1)} %param.20) | copy-start | bytes 1769476
  86.0 48.9 %copy-start.31 = (f32[768]{0:T(1024)S(1)}, f32[768]{0:T(1024)}, u32[]{:S(2)}) copy-start(f32[768]{0:T(1024)} %param.26) | copy-start | bytes 9220
  88.3 49.5 %copy-start.38 = (f32[768]{0:T(1024)S(1)}, f32[768]{0:T(1024)}, u32[]{:S(2)}) copy-start(f32[768]{0:T(1024)} %param.27) | copy-start | bytes 9220
  88.3 49.5 %copy-start.45 = (f32[768]{0:T(1024)S(1)}, f32[768]{0:T(1024)}, u32[]{:S(2)}) copy-start(f32[768]{0:T(1024)} %param.28) | copy-start | bytes 9220
  88.3 100.2 %all-gather.8.cloned.1.call-start = ((), (), s32[]{:S(2)}) async-start(), calls=%async_computation.8 | async-start | bytes 2949120 | tf_op jit(solution)/shard_map/all_gather | solution.py:152
  136.3 118.3 %copy-start.36 = (f32[384]{0:T(512)}, f32[384]{0:T(512)S(1)}, u32[]{:S(2)}) copy-start(f32[384]{0:T(512)S(1)} %broadcast_multiply_fusion.5) | copy-start | bytes 4612
  137.8 116.8 %copy-start.41 = (f32[384]{0:T(512)}, f32[384]{0:T(512)S(1)}, u32[]{:S(2)}) copy-start(f32[384]{0:T(512)S(1)} %add_rsqrt_fusion.1) | copy-start | bytes 4612
  139.0 65.5 %copy-start.59 = (bf16[768,768]{1,0:T(8,128)(2,1)S(1)}, bf16[768,768]{1,0:T(8,128)(2,1)}, u32[]{:S(2)}) copy-start(bf16[768,768]{1,0:T(8,128)(2,1)} %param.31) | copy-start | bytes 3538948
  139.0 115.6 %reduce-scatter.11.cloned.1.call-start = ((), (), s32[]{:S(2)}) async-start(), calls=%async_computation.9 | async-start | bytes 2949120 | tf_op jit(solution)/shard_map/reduce_scatter | solution.py:157
  208.0 106.1 %all-gather.10.cloned.1.call-start = ((), (), s32[]{:S(2)}) async-start(), calls=%async_computation.10 | async-start | bytes 2949120 | tf_op jit(solution)/shard_map/all_gather | solution.py:199
  209.7 49.0 %copy-start.10 = (bf16[768,768]{1,0:T(8,128)(2,1)S(1)}, bf16[768,768]{1,0:T(8,128)(2,1)}, u32[]{:S(2)}) copy-start(bf16[768,768]{1,0:T(8,128)(2,1)} %param.35) | copy-start | bytes 3538948
  264.6 109.9 %reduce-scatter.13.cloned.1.call-start = ((), (), s32[]{:S(2)}) async-start(), calls=%async_computation.11 | async-start | bytes 2949120 | tf_op jit(solution)/shard_map/reduce_scatter | solution.py:210
  327.9 111.7 %all-gather.12.cloned.1.call-start = ((), (), s32[]{:S(2)}) async-start(), calls=%async_computation.14 | async-start | bytes 3317760 | tf_op jit(solution)/shard_map/all_gather | solution.py:270
  329.4 47.0 %copy-start.37 = (f32[384]{0:T(512)S(1)}, f32[384]{0:T(512)}, u32[]{:S(2)}) copy-start(f32[384]{0:T(512)} %copy-done.36) | copy-start | bytes 4612
  329.4 47.0 %copy-start.39 = (f32[768]{0:T(1024)S(1)}, f32[768]{0:T(1024)}, u32[]{:S(2)}) copy-start(f32[768]{0:T(1024)} %param.27) | copy-start | bytes 9220
  329.4 47.0 %copy-start.42 = (f32[384]{0:T(512)S(1)}, f32[384]{0:T(512)}, u32[]{:S(2)}) copy-start(f32[384]{0:T(512)} %copy-done.41) | copy-start | bytes 4612
  384.7 155.3 %reduce-scatter.19.cloned.1.call-start = ((), (), s32[]{:S(2)}) async-start(), calls=%async_computation.15 | async-start | bytes 2580480
  499.0 91.6 %reduce-scatter.15.cloned.1.call-start = ((), (), s32[]{:S(2)}) async-start(), calls=%async_computation.12 | async-start | bytes 2949120 | tf_op jit(solution)/shard_map/reduce_scatter | solution.py:304
  509.0 134.3 %reduce-scatter.17.cloned.1.call-start = ((), (), s32[]{:S(2)}) async-start(), calls=%async_computation.13 | async-start | bytes 4423680 | tf_op jit(solution)/shard_map/reduce_scatter | solution.py:320
  522.4 68.2 %copy-start.11 = (f32[384,768]{1,0:T(8,128)S(1)}, f32[384,768]{1,0:T(8,128)}, u32[]{:S(2)}) copy-start(f32[384,768]{1,0:T(8,128)} %get-tuple-element.113) | copy-start | bytes 3538948
  (51 other events, 160.6 us)
Sparse Core Ops, SparseCore 0:
  9.6 52.6 all-gather.5
  88.4 46.4 reduce-scatter.8
  139.1 49.3 all-gather.7
  208.1 46.4 reduce-scatter.10
  264.7 49.3 all-gather.9
  328.0 46.4 reduce-scatter.12
  384.9 54.6 all-gather.11
  499.2 40.8 reduce-scatter.18
  542.9 47.6 reduce-scatter.14
  594.0 49.1 reduce-scatter.16

commit v5 on v4

--- a/solution.py
+++ b/solution.py
@@ -95,6 +95,18 @@
         grad_keys.reshape(full_shape).astype(jnp.bfloat16),
         grad_values.reshape(full_shape).astype(jnp.bfloat16),
     )
+
+
+def ring_order(count):
+    chips = []
+    for row in range(count // 4):
+        chips += [2 * row, 2 * row + 1] if row % 2 == 0 else [2 * row + 1, 2 * row]
+    if count % 4:
+        chips += list(range(len(chips), count // 2))
+    members = []
+    for step, chip in enumerate(chips):
+        members += [2 * chip, 2 * chip + 1] if step % 2 == 0 else [2 * chip + 1, 2 * chip]
+    return members if count % 2 == 0 else list(range(count))
 
 
 def body(
@@ -300,70 +312,94 @@
             jnp.sum(grad_values.astype(jnp.float32), axis=0),
         ]
     )
-    input_grad = (
-        lax.psum_scatter(
-            jnp.einsum(
-                "kte,kde->td", stacked, qkv_weight, preferred_element_type=jnp.float32
-            ).astype(jnp.bfloat16),
-            "tensor",
-            scatter_dimension=0,
-            tiled=True,
-        ).astype(jnp.float32)
-        + grad_res
-    ).astype(jnp.bfloat16)
-
-    def stacked_sum(parts, dtype):
-        flat = jnp.concatenate([part.astype(dtype) for part in parts], axis=1)
-        lanes = flat.shape[2]
-        pad = (-flat.shape[1]) % 16
-        flat = jnp.pad(flat, ((0, 0), (0, pad), (0, 0)))
-        summed = lax.psum_scatter(
-            flat.reshape(-1, lanes), "dp", scatter_dimension=0, tiled=True
-        )
-        pieces = []
-        begin = 0
-        for part in parts:
-            pieces.append(summed[begin : begin + part.shape[1]])
-            begin += part.shape[1]
-        return pieces
+    input_part = lax.psum_scatter(
+        jnp.einsum(
+            "kte,kde->td", stacked, qkv_weight, preferred_element_type=jnp.float32
+        ).astype(jnp.bfloat16),
+        "tensor",
+        scatter_dimension=0,
+        tiled=True,
+    )
+    input_grad = (input_part.astype(jnp.float32) + grad_res).astype(jnp.bfloat16)
 
     def in_blocks(grad):
         return grad.reshape(dp_count, grad.shape[0] // dp_count, grad.shape[1])
 
     def copied(flat, lanes):
         rows = -(-flat.size // lanes)
+        rows += rows % 2
         flat = jnp.pad(flat, (0, rows * lanes - flat.size)).reshape(1, rows, lanes)
         return jnp.broadcast_to(flat, (dp_count, rows, lanes))
 
+    ring = ring_order(dp_count)
+    ring_place = [0] * dp_count
+    for place, member in enumerate(ring):
+        ring_place[member] = place
+    place = jnp.asarray(ring_place, jnp.int32)[dp_index]
+    ring_members = jnp.asarray(ring, jnp.int32)
+    ahead = [(ring[i], ring[(i + 1) % dp_count]) for i in range(dp_count)]
+    behind = [(ring[i], ring[(i - 1) % dp_count]) for i in range(dp_count)]
+
+    def ring_sum(parts):
+        if dp_count > 8:
+            return [
+                lax.psum_scatter(
+                    part.reshape(-1, part.shape[2]), "dp", scatter_dimension=0, tiled=True
+                )
+                for part in parts
+            ]
+        halves = [part.shape[1] // 2 for part in parts]
+        first = [part[:, :half] for part, half in zip(parts, halves)]
+        second = [part[:, half:] for part, half in zip(parts, halves)]
+
+        def pick(blocks, shift):
+            member = ring_members[(place + shift) % dp_count]
+            return [lax.dynamic_index_in_dim(block, member, 0, keepdims=False) for block in blocks]
+
+        going = pick(first, -1)
+        coming = pick(second, 1)
+        for step in range(dp_count - 1):
+            going = [
+                got + own
+                for got, own in zip(lax.ppermute(going, "dp", ahead), pick(first, -step - 2))
+            ]
+            coming = [
+                got + own
+                for got, own in zip(lax.ppermute(coming, "dp", behind), pick(second, step + 2))
+            ]
+        return [jnp.concatenate([one, two], axis=0) for one, two in zip(going, coming)]
+
     copied_rows = dp_count * dp_count * rows_group.size <= (1 << 20)
-    out_blocks = in_blocks(out_weight_grad_t).reshape(dp_count, -1, model_width)
-    early_parts = [in_blocks(up_weight_grad), in_blocks(down_weight_grad_t), out_blocks]
+    up_sum, down_sum_t, up_bias_rows = ring_sum(
+        [in_blocks(up_weight_grad), in_blocks(down_weight_grad_t), copied(up_bias_grad, model_width)]
+    )
+    down_sum = down_sum_t.T
+    up_bias_total = up_bias_rows.reshape(-1)[: up_bias_grad.size]
+    late_shared = [token_sum, qv_bias_grad]
     if copied_rows:
         rows_slotted = lax.dynamic_update_slice(
             jnp.zeros((dp_count,) + rows_group.shape, rows_group.dtype),
             rows_group[None],
             (dp_index, 0, 0, 0),
         )
-        early_parts.append(copied(rows_slotted.reshape(-1), model_width))
+        late_shared.append(rows_slotted)
     else:
         rows_each = lax.all_gather(rows_group.astype(jnp.bfloat16), "dp", axis=0, tiled=False)
-    early_sums = stacked_sum(early_parts, jnp.bfloat16)
-    up_sum = early_sums[0].astype(jnp.float32)
-    down_sum = early_sums[1].astype(jnp.float32).T
-    out_sum = early_sums[2].reshape(-1, out_weight_grad_t.shape[1]).astype(jnp.float32).T
+    qkv_lanes = qkv_weight_grad.shape[1]
+    qkv_flat, out_sum_t, late_rows = ring_sum(
+        [
+            in_blocks(qkv_weight_grad),
+            in_blocks(out_weight_grad_t),
+            copied(joined(late_shared), model_width),
+        ]
+    )
+    out_sum = out_sum_t.T
+    late_back = parted(late_rows.reshape(-1), late_shared)
+    token_grads = late_back[0]
+    qv_bias_total = late_back[1]
     if copied_rows:
-        rows_each = early_sums[3].reshape(-1)[: rows_slotted.size]
-    late_shared = [token_sum, up_bias_grad, qv_bias_grad]
-    qkv_lanes = qkv_weight_grad.shape[1]
-    late_sums = stacked_sum(
-        [in_blocks(qkv_weight_grad), copied(joined(late_shared), qkv_lanes)], jnp.float32
-    )
-    qkv_sum = jnp.transpose(
-        late_sums[0].reshape(late_sums[0].shape[0], 3, qkv_lanes // 3), (1, 0, 2)
-    )
-    token_grads, up_bias_total, qv_bias_total = parted(
-        late_sums[1].reshape(-1), late_shared
-    )
+        rows_each = late_back[2]
+    qkv_sum = jnp.transpose(qkv_flat.reshape(qkv_flat.shape[0], 3, qkv_lanes // 3), (1, 0, 2))
     rows_all = rows_each.reshape(dp_count * seq_count, 4, model_width).astype(jnp.bfloat16)
     leading_all = rows_all[:, 0]
     grad_pre_all = rows_all[:, 1]

time: 668 us -> 648 us (0.970)
  waiting for transfers between devices: 448 us -> 301 us
  starting transfers between devices: 1.45 us -> 63.9 us
  between operations: 15.6 us -> 56.7 us
  local copies, waits for them, and re-layouts: 48.8 us -> 60.7 us
  other arithmetic: 34.6 us -> 45.7 us
    ppermute x0 -> x77, waiting for transfers between devices: none -> 76.1 us  [the longest x42 52.6 us: ring_sum(): lax.ppermute(going, 'dp', ahead)]
    ppermute x0 -> x77, starting transfers between devices: none -> 62.9 us  [the longest x35 57.4 us: ring_sum(): lax.ppermute(coming, 'dp', behind)]
    reduce_scatter x1 -> x0, waiting for transfers between devices: 50.6 us -> none  [stacked_sum(): lax.psum_scatter(flat.reshape(-1, lanes), 'dp', scatter_dimension=0, tile...]
    all_gather x1, waiting for transfers between devices: 49.1 us -> 0.01 us  [body(): grad_fed_all = lax.all_gather(grad_fed, 'tensor', axis=0, tiled=True)]
    reduce_scatter x1, waiting for transfers between devices: 45.1 us -> 0.01 us  [body(): lax.psum_scatter(jnp.einsum('kte,kde->td', stacked, qkv_weight, preferred...]
    reduce_scatter x1, waiting for transfers between devices: 38.5 us -> 2.48 us  [body(): lax.psum_scatter(jnp.einsum('tf,df->td', grad_up, up_weight, preferred_el...]
    all_gather x1, waiting for transfers between devices: 54 us -> 28.3 us  [body(): lax.all_gather(jnp.concatenate([grad_att, riding], axis=0), 'tensor', axi...]
    unnamed x11 -> x8, waiting for transfers between devices: 18.4 us -> 0.8 us
  transfers between devices with their start and end apart: 10 -> 85, of which waited for: 10 -> 41; matrix products, arithmetic and copies ran while one was open for 6% -> 13% of each run, Pallas kernels for 0% -> 0%
where the time goes in v5:
time: 648 us; the launch traced here: 638 us
  waiting for transfers between devices  301 us (46%)
  matrix products  111 us (17%)
  starting transfers between devices  63.9 us (10%)
  local copies, waits for them, and re-layouts  60.7 us (9%)
  between operations  56.7 us (9%)
  other arithmetic  45.7 us (7%)
    ppermute x35, starting transfers between devices, ring_sum(): lax.ppermute(coming, 'dp', behind)  57.4 us
    ppermute x42, waiting for transfers between devices, ring_sum(): lax.ppermute(going, 'dp', ahead)  52.6 us
    all_gather x1, waiting for transfers between devices, body(): gathered = lax.all_gather(inputs, 'tensor', axis=0, tiled=True)  52.1 us
    all_gather x1, waiting for transfers between devices, body(): first_all = lax.all_gather(first_low, 'tensor', axis=0, tiled=True)  49.5 us
    reduce_scatter x1, waiting for transfers between devices, body(): lax.psum_scatter(jnp.dot(context, out_weight, preferred_element_type=jnp....  46.4 us
    reduce_scatter x1, waiting for transfers between devices, body(): lax.psum_scatter(jnp.dot(active, down_weight, preferred_element_type=jnp....  44.9 us
    all_gather x1, waiting for transfers between devices, body(): lax.all_gather(jnp.concatenate([grad_att, riding], axis=0), 'tensor', axi...  28.3 us
    ppermute x35, waiting for transfers between devices, ring_sum(): lax.ppermute(coming, 'dp', behind)  23.5 us
  transfers between devices with their start and end apart: 85, of which 41 were waited for; matrix products, arithmetic and copies ran while one was open for 13% of the time, Pallas kernels for 0%

profile of v5, /device:TPU:0, one launch (start us, length us, event | category | flops | bytes accessed | tf_op | source)
XLA Modules:
  0.0 638.2 jit_solution(2464540902562107905)
XLA Ops:
  10.2 52.1 %all-gather.6.cloned.1.call-done = bf16[1536,768]{1,0:T(8,128)(2,1)} async-done(((bf16[384,768]{1,0:T(8,128)(2,1)}), bf16[1536,768]{1,0:T(8,128)(2,1)}) %all-gather.6.cloned.1.call-update) | async-done | bytes 2359312 | tf_op jit(solution)/shard_map/all_gather | solution.py:142
  62.3 3.5 convolution_bitcast_fusion
  88.7 46.4 %reduce-scatter.5.cloned.1.call-done = bf16[384,768]{1,0:T(8,128)(2,1)} async-done(((bf16[1536,768]{1,0:T(8,128)(2,1)}), bf16[384,768]{1,0:T(8,128)(2,1)}) %reduce-scatter.5.cloned.1.call-update) | async-done | bytes 589840 | tf_op jit(solution)/shard_map/reduce_scatter | solution.py:151
  139.2 49.5 %all-gather.8.cloned.1.call-done = bf16[1536,768]{1,0:T(8,128)(2,1)} async-done(((bf16[384,768]{1,0:T(8,128)(2,1)}), bf16[1536,768]{1,0:T(8,128)(2,1)}) %all-gather.8.cloned.1.call-update) | async-done | bytes 2359312 | tf_op jit(solution)/shard_map/all_gather | solution.py:164
  188.7 14.4 %multiply_convert_fusion = (bf16[1536,768]{1,0:T(8,128)(2,1)S(1)}, f32[1536,768]{1,0:T(8,128)}, f32[1536,768]{1,0:T(8,128)}) fusion(f32[768]{0:T(1024)} %param.32, bf16[1536,768]{1,0:T(8,128)(2,1)} %all-gather.8.cloned.1.call-done, bf16[768,768]{1,0:T(8,128)(2,1)S(1)} %copy-done), kind=kOutput, calls=%fused_computation.22 | convolution fusion | flops 1889796096 | bytes 15338496 | tf_op jit(solution)/shard_map/dot_general | solution.py:165
  204.5 3.4 convolution_convert_fusion.1
  209.7 44.9 %reduce-scatter.7.cloned.1.call-done = bf16[384,768]{1,0:T(8,128)(2,1)} async-done(((bf16[1536,768]{1,0:T(8,128)(2,1)}), bf16[384,768]{1,0:T(8,128)(2,1)}) %reduce-scatter.7.cloned.1.call-update) | async-done | bytes 589840 | tf_op jit(solution)/shard_map/reduce_scatter | solution.py:169
  317.6 8.2 %convert_reduce_fusion = (f32[768]{0:T(1024)S(1)}, bf16[1536,768]{1,0:T(8,128)(2,1)S(1)}) fusion(f32[1536,768]{1,0:T(8,128)} %get-tuple-element.101, f32[1536,768]{1,0:T(8,128)} %get-tuple-element.142, f32[768]{0:T(1024)} %param.32, bf16[1536,768]{1,0:T(8,128)(2,1)} %all-gather.10.cloned.1.call-done, bf16[768,768]{1,0:T(8,128)(2,1)} %param.33), kind=kOutput, calls=%fused_computation.16 | convolution fusion | flops 1831992576 | bytes 15341568 | tf_op jit(solution)/shard_map/td,fd->tf/dot_general | solution.py:215
  327.2 3.5 convolution_convert_fusion
  330.9 4.6 fusion.167
  345.1 3.6 collective-permute-done.59
  352.3 3.6 collective-permute-done.61
  419.4 28.3 %all-gather.12.cloned.1.call-done = bf16[1728,768]{1,0:T(8,128)(2,1)} async-done(((bf16[432,768]{1,0:T(8,128)(2,1)}), bf16[1728,768]{1,0:T(8,128)(2,1)}) %all-gather.12.cloned.1.call-update) | async-done | bytes 2654224 | tf_op jit(solution)/shard_map/all_gather | solution.py:282
  455.0 6.2 fusion.86
  461.3 7.2 %convert_reduce_fusion.1 = (f32[3,64]{1,0:T(4,128)S(1)}, bf16[3,3,64,512]{3,2,1,0:T(8,128)(2,1)}) fusion(f32[3,3,512,512]{2,3,1,0:T(8,128)} %copy-done.4, f32[3,3,512]{2,1,0:T(4,128)S(1)} %copy-done.51, pred[3,512,512]{1,2,0:T(8,128)(4,1)S(1)} %copy-done.19, bf16[3,512,3,64]{1,0,3,2:T(4,128)(2,1)S(1)} %reshape.312), kind=kOutput, calls=%fused_computation.76 | convolution fusion | flops 312311616 | bytes 11422464 | tf_op jit(solution)/shard_map/rhqk,rqhe->rkhe/dot_general | solution.py:72
  468.5 15.9 %fusion.72 = bf16[3,512,3,64]{1,3,2,0:T(8,128)(2,1)} fusion(f32[3,3,512,512]{2,3,1,0:T(8,128)} %fusion.86, f32[3,3,512,512]{2,3,1,0:T(8,128)} %copy-done.4, f32[3,3,512]{2,1,0:T(4,128)S(1)} %copy-done.51, pred[3,512,512]{1,2,0:T(8,128)(4,1)S(1)} %copy-done.19, bf16[3,512,3,64]{1,0,3,2:T(4,128)(2,1)S(1)} %copy-done.31), kind=kOutput, calls=%fused_computation.73 | convolution fusion | flops 328537088 | bytes 20858880 | tf_op jit(solution)/shard_map/rhqk,rqhe->rkhe/dot_general | solution.py:89
  484.4 16.1 %convert_reduce_fusion.2 = (f32[3,64]{1,0:T(4,128)S(1)}, bf16[3,3,64,512]{3,2,1,0:T(8,128)(2,1)}) fusion(f32[3,3,512,512]{2,3,1,0:T(8,128)} %fusion.86, f32[3,3,512,512]{2,3,1,0:T(8,128)} %copy-done.4, f32[3,3,512]{2,1,0:T(4,128)S(1)} %copy-done.51, pred[3,512,512]{1,2,0:T(8,128)(4,1)S(1)} %copy-done.19, bf16[3,512,3,64]{1,0,3,2:T(4,128)(2,1)} %convert_element_type.227), kind=kOutput, calls=%fused_computation.77 | convolution fusion | flops 329126720 | bytes 20859648 | tf_op jit(solution)/shard_map/rhqk,rkhe->rqhe/dot_general | solution.py:85
  517.3 4.4 fusion.53
  526.2 3.5 bitcast_convert_fusion
  534.8 4.1 collective-permute-done.29
  540.6 4.4 collective-permute-done.30
  555.7 4.1 collective-permute-done.33
  571.3 4.4 collective-permute-done.17
  581.4 5.3 collective-permute-done.19
  (519 shorter events, 240.1 us)
Async XLA Ops:
  7.2 55.1 %all-gather.6.cloned.1.call-start = ((), (), s32[]{:S(2)}) async-start(), calls=%async_computation.4 | async-start | bytes 2949120 | tf_op jit(solution)/shard_map/all_gather | solution.py:142
  7.9 127.2 %reduce-scatter.5.cloned.1.call-start = ((), (), s32[]{:S(2)}) async-start(), calls=%async_computation.5 | async-start | bytes 2949120 | tf_op jit(solution)/shard_map/reduce_scatter | solution.py:151
  88.5 100.2 %all-gather.8.cloned.1.call-start = ((), (), s32[]{:S(2)}) async-start(), calls=%async_computation.6 | async-start | bytes 2949120 | tf_op jit(solution)/shard_map/all_gather | solution.py:164
  139.2 115.5 %reduce-scatter.7.cloned.1.call-start = ((), (), s32[]{:S(2)}) async-start(), calls=%async_computation.7 | async-start | bytes 2949120 | tf_op jit(solution)/shard_map/reduce_scatter | solution.py:169
  208.0 109.6 %all-gather.10.cloned.1.call-start = ((), (), s32[]{:S(2)}) async-start(), calls=%async_computation.8 | async-start | bytes 2949120 | tf_op jit(solution)/shard_map/all_gather | solution.py:211
  263.6 114.4 %reduce-scatter.9.cloned.1.call-start = ((), (), s32[]{:S(2)}) async-start(), calls=%async_computation.9 | async-start | bytes 2949120 | tf_op jit(solution)/shard_map/reduce_scatter | solution.py:222
  330.7 117.0 %all-gather.12.cloned.1.call-start = ((), (), s32[]{:S(2)}) async-start(), calls=%async_computation.11 | async-start | bytes 3317760 | tf_op jit(solution)/shard_map/all_gather | solution.py:282
  348.7 11.4 %collective-permute-start.70 = (f32[48,768]{1,0:T(8,128)S(1)}, f32[48,768]{1,0:T(8,128)S(1)}, u32[]{:S(2)}, u32[]{:S(2)}) collective-permute-start(f32[48,768]{1,0:T(8,128)S(1)} %dynamic-slice_bitcast_fusion), channel_id=1, source_target_pairs={{0,16},{4,0},{12,4},{8,12},{24,8},{28,24},{20,28},{16,20},{1,17},{... | collective-permute-start | bytes 442376 | tf_op jit(solution)/shard_map/ppermute | solution.py:368
  369.4 23.6 %collective-permute-start.44 = (f32[48,768]{1,0:T(8,128)}, f32[48,768]{1,0:T(8,128)}, u32[]{:S(2)}, u32[]{:S(2)}) collective-permute-start(f32[48,768]{1,0:T(8,128)} %bitcast_add_fusion.26), channel_id=1, source_target_pairs={{0,4},{4,12},{12,8},{8,24},{24,28},{28,20},{20,16},{16,0},{1,5},{5... | collective-permute-start | bytes 442376 | tf_op jit(solution)/shard_map/ppermute | solution.py:364
  370.1 24.0 %collective-permute-start.73 = (f32[48,768]{1,0:T(8,128)}, f32[48,768]{1,0:T(8,128)}, u32[]{:S(2)}, u32[]{:S(2)}) collective-permute-start(f32[48,768]{1,0:T(8,128)} %bitcast_add_fusion.4), channel_id=1, source_target_pairs={{0,16},{4,0},{12,4},{8,12},{24,8},{28,24},{20,28},{16,20},{1,17},{... | collective-permute-start | bytes 442376 | tf_op jit(solution)/shard_map/ppermute | solution.py:368
  372.8 24.3 %collective-permute-start.66 = (f32[48,768]{1,0:T(8,128)}, f32[48,768]{1,0:T(8,128)}, u32[]{:S(2)}, u32[]{:S(2)}) collective-permute-start(f32[48,768]{1,0:T(8,128)} %bitcast_add_fusion.11), channel_id=1, source_target_pairs={{0,4},{4,12},{12,8},{8,24},{24,28},{28,20},{20,16},{16,0},{1,5},{5... | collective-permute-start | bytes 442376 | tf_op jit(solution)/shard_map/ppermute | solution.py:364
  373.5 24.6 %collective-permute-start.52 = (f32[48,768]{1,0:T(8,128)}, f32[48,768]{1,0:T(8,128)}, u32[]{:S(2)}, u32[]{:S(2)}) collective-permute-start(f32[48,768]{1,0:T(8,128)} %bitcast_add_fusion.18), channel_id=1, source_target_pairs={{0,16},{4,0},{12,4},{8,12},{24,8},{28,24},{20,28},{16,20},{1,17},{... | collective-permute-start | bytes 442376 | tf_op jit(solution)/shard_map/ppermute | solution.py:368
  393.0 235.9 %reduce-scatter.11.cloned.1.call-start = ((), (), s32[]{:S(2)}) async-start(), calls=%async_computation.10 | async-start | bytes 2949120 | tf_op jit(solution)/shard_map/reduce_scatter | solution.py:315
  503.9 25.8 %collective-permute-start.35 = (f32[48,192]{1,0:T(8,128)}, f32[48,192]{1,0:T(8,128)}, u32[]{:S(2)}, u32[]{:S(2)}) collective-permute-start(f32[48,192]{1,0:T(8,128)} %dynamic-slice_bitcast_fusion.6), channel_id=1, source_target_pairs={{0,16},{4,0},{12,4},{8,12},{24,8},{28,24},{20,28},{16,20},{1,17},{... | collective-permute-start | bytes 110600 | tf_op jit(solution)/shard_map/ppermute | solution.py:368
  505.4 26.1 %collective-permute-start.28 = (f32[48,192]{1,0:T(8,128)}, f32[48,192]{1,0:T(8,128)}, u32[]{:S(2)}, u32[]{:S(2)}) collective-permute-start(f32[48,192]{1,0:T(8,128)} %dynamic-slice_bitcast_fusion.7), channel_id=1, source_target_pairs={{0,4},{4,12},{12,8},{8,24},{24,28},{28,20},{20,16},{16,0},{1,5},{5... | collective-permute-start | bytes 110600 | tf_op jit(solution)/shard_map/ppermute | solution.py:364
  511.9 37.5 %collective-permute-start.14 = (f32[52,768]{1,0:T(8,128)}, f32[52,768]{1,0:T(8,128)}, u32[]{:S(2)}, u32[]{:S(2)}) collective-permute-start(f32[52,768]{1,0:T(8,128)} %get-tuple-element.115), channel_id=1, source_target_pairs={{0,4},{4,12},{12,8},{8,24},{24,28},{28,20},{20,16},{16,0},{1,5},{5... | collective-permute-start | bytes 479240 | tf_op jit(solution)/shard_map/ppermute | solution.py:364
  511.9 76.9 %collective-permute-start.21 = (f32[52,768]{1,0:T(8,128)}, f32[52,768]{1,0:T(8,128)}, u32[]{:S(2)}, u32[]{:S(2)}) collective-permute-start(f32[52,768]{1,0:T(8,128)} %get-tuple-element.116), channel_id=1, source_target_pairs={{0,16},{4,0},{12,4},{8,12},{24,8},{28,24},{20,28},{16,20},{1,17},{... | collective-permute-start | bytes 479240 | tf_op jit(solution)/shard_map/ppermute | solution.py:368
  525.7 19.3 %collective-permute-start.7 = (f32[48,576]{1,0:T(8,128)}, f32[48,576]{1,0:T(8,128)S(1)}, u32[]{:S(2)}, u32[]{:S(2)}) collective-permute-start(f32[48,576]{1,0:T(8,128)} %dynamic-slice_bitcast_fusion.4), channel_id=1, source_target_pairs={{0,16},{4,0},{12,4},{8,12},{24,8},{28,24},{20,28},{16,20},{1,17},{... | collective-permute-start | bytes 331784 | tf_op jit(solution)/shard_map/ppermute | solution.py:368
  529.7 15.9 %collective-permute-start = (f32[48,576]{1,0:T(8,128)S(1)}, f32[48,576]{1,0:T(8,128)S(1)}, u32[]{:S(2)}, u32[]{:S(2)}) collective-permute-start(f32[48,576]{1,0:T(8,128)S(1)} %dynamic-slice_bitcast_fusion.5), channel_id=1, source_target_pairs={{0,4},{4,12},{12,8},{8,24},{24,28},{28,20},{20,16},{16,0},{1,5},{5... | collective-permute-start | bytes 331784 | tf_op jit(solution)/shard_map/ppermute | solution.py:364
  545.6 14.1 %collective-permute-start.8 = (f32[48,576]{1,0:T(8,128)S(1)}, f32[48,576]{1,0:T(8,128)S(1)}, u32[]{:S(2)}, u32[]{:S(2)}) collective-permute-start(f32[48,576]{1,0:T(8,128)S(1)} %bitcast_add_fusion.34), channel_id=1, source_target_pairs={{0,16},{4,0},{12,4},{8,12},{24,8},{28,24},{20,28},{16,20},{1,17},{... | collective-permute-start | bytes 331784 | tf_op jit(solution)/shard_map/ppermute | solution.py:368
  547.2 13.8 %collective-permute-start.1 = (f32[48,576]{1,0:T(8,128)S(1)}, f32[48,576]{1,0:T(8,128)S(1)}, u32[]{:S(2)}, u32[]{:S(2)}) collective-permute-start(f32[48,576]{1,0:T(8,128)S(1)} %bitcast_add_fusion.41), channel_id=1, source_target_pairs={{0,4},{4,12},{12,8},{8,24},{24,28},{28,20},{20,16},{16,0},{1,5},{5... | collective-permute-start | bytes 331784 | tf_op jit(solution)/shard_map/ppermute | solution.py:364
  551.2 13.5 %collective-permute-start.15 = (f32[52,768]{1,0:T(8,128)S(1)}, f32[52,768]{1,0:T(8,128)S(1)}, u32[]{:S(2)}, u32[]{:S(2)}) collective-permute-start(f32[52,768]{1,0:T(8,128)S(1)} %fusion.142), channel_id=1, source_target_pairs={{0,4},{4,12},{12,8},{8,24},{24,28},{28,20},{20,16},{16,0},{1,5},{5... | collective-permute-start | bytes 479240 | tf_op jit(solution)/shard_map/ppermute | solution.py:364
  581.3 11.9 %collective-permute-start.4 = (f32[48,576]{1,0:T(8,128)S(1)}, f32[48,576]{1,0:T(8,128)S(1)}, u32[]{:S(2)}, u32[]{:S(2)}) collective-permute-start(f32[48,576]{1,0:T(8,128)S(1)} %bitcast_add_fusion.38), channel_id=1, source_target_pairs={{0,4},{4,12},{12,8},{8,24},{24,28},{28,20},{20,16},{16,0},{1,5},{5... | collective-permute-start | bytes 331784 | tf_op jit(solution)/shard_map/ppermute | solution.py:364
  586.8 11.9 %collective-permute-start.12 = (f32[48,576]{1,0:T(8,128)S(1)}, f32[48,576]{1,0:T(8,128)S(1)}, u32[]{:S(2)}, u32[]{:S(2)}) collective-permute-start(f32[48,576]{1,0:T(8,128)S(1)} %bitcast_add_fusion.30), channel_id=1, source_target_pairs={{0,16},{4,0},{12,4},{8,12},{24,8},{28,24},{20,28},{16,20},{1,17},{... | collective-permute-start | bytes 331784 | tf_op jit(solution)/shard_map/ppermute | solution.py:368
  (131 other events, 1356.0 us)
Sparse Core Ops, SparseCore 0:
  9.6 52.6 all-gather.5
  88.6 46.4 reduce-scatter.4
  139.3 49.3 all-gather.7
  208.1 46.4 reduce-scatter.6
  263.7 49.3 all-gather.9
  330.9 47.0 reduce-scatter.8
  393.1 54.6 all-gather.11
  529.8 45.5 reduce-scatter.10

commit v6 on v4

--- a/solution.py
+++ b/solution.py
@@ -133,16 +133,17 @@
     queries = (projected[0] + qv_bias[0]).astype(jnp.bfloat16)
     key_rows = projected[1].astype(jnp.bfloat16)
     value_rows = (projected[2] + qv_bias[1]).astype(jnp.bfloat16)
-
+    local_width = queries.shape[1]
+
+    out_weight_all = lax.all_gather(out_weight, "tensor", axis=0, tiled=False)
     context, log_totals = attend_forward(queries, key_rows, value_rows, segments)
+    context_own = lax.all_to_all(
+        context.reshape(tensor_count, share_rows, local_width), "tensor", 0, 0, tiled=False
+    )
     attended = (
-        lax.psum_scatter(
-            jnp.dot(context, out_weight, preferred_element_type=jnp.float32).astype(jnp.bfloat16),
-            "tensor",
-            scatter_dimension=0,
-            tiled=True,
+        jnp.einsum(
+            "itc,icd->td", context_own, out_weight_all, preferred_element_type=jnp.float32
         )
-        .astype(jnp.float32)
         + out_bias
     )
     first_norm, normed_one, inverse_one = norm_forward(
@@ -313,18 +314,20 @@
     ).astype(jnp.bfloat16)
 
     def stacked_sum(parts, dtype):
-        flat = jnp.concatenate([part.astype(dtype) for part in parts], axis=1)
+        padded = [
+            jnp.pad(part.astype(dtype), ((0, 0), (0, (-part.shape[1]) % 16), (0, 0)))
+            for part in parts
+        ]
+        flat = jnp.concatenate(padded, axis=1)
         lanes = flat.shape[2]
-        pad = (-flat.shape[1]) % 16
-        flat = jnp.pad(flat, ((0, 0), (0, pad), (0, 0)))
         summed = lax.psum_scatter(
             flat.reshape(-1, lanes), "dp", scatter_dimension=0, tiled=True
         )
         pieces = []
         begin = 0
-        for part in parts:
+        for part, held in zip(parts, padded):
             pieces.append(summed[begin : begin + part.shape[1]])
-            begin += part.shape[1]
+            begin += held.shape[1]
         return pieces
 
     def in_blocks(grad):
@@ -337,7 +340,13 @@
 
     copied_rows = dp_count * dp_count * rows_group.size <= (1 << 20)
     out_blocks = in_blocks(out_weight_grad_t).reshape(dp_count, -1, model_width)
-    early_parts = [in_blocks(up_weight_grad), in_blocks(down_weight_grad_t), out_blocks]
+    early_shared = [token_sum, up_bias_grad]
+    early_parts = [
+        in_blocks(up_weight_grad),
+        in_blocks(down_weight_grad_t),
+        out_blocks,
+        copied(joined(early_shared), model_width),
+    ]
     if copied_rows:
         rows_slotted = lax.dynamic_update_slice(
             jnp.zeros((dp_count,) + rows_group.shape, rows_group.dtype),
@@ -351,19 +360,20 @@
     up_sum = early_sums[0].astype(jnp.float32)
     down_sum = early_sums[1].astype(jnp.float32).T
     out_sum = early_sums[2].reshape(-1, out_weight_grad_t.shape[1]).astype(jnp.float32).T
+    token_grads, up_bias_total = parted(
+        early_sums[3].reshape(-1).astype(jnp.float32), early_shared
+    )
     if copied_rows:
-        rows_each = early_sums[3].reshape(-1)[: rows_slotted.size]
-    late_shared = [token_sum, up_bias_grad, qv_bias_grad]
+        rows_each = early_sums[4].reshape(-1)[: rows_slotted.size]
+    late_shared = [qv_bias_grad]
     qkv_lanes = qkv_weight_grad.shape[1]
     late_sums = stacked_sum(
-        [in_blocks(qkv_weight_grad), copied(joined(late_shared), qkv_lanes)], jnp.float32
+        [in_blocks(qkv_weight_grad), copied(joined(late_shared), qkv_lanes)], jnp.bfloat16
     )
     qkv_sum = jnp.transpose(
         late_sums[0].reshape(late_sums[0].shape[0], 3, qkv_lanes // 3), (1, 0, 2)
-    )
-    token_grads, up_bias_total, qv_bias_total = parted(
-        late_sums[1].reshape(-1), late_shared
-    )
+    ).astype(jnp.float32)
+    (qv_bias_total,) = parted(late_sums[1].reshape(-1).astype(jnp.float32), late_shared)
     rows_all = rows_each.reshape(dp_count * seq_count, 4, model_width).astype(jnp.bfloat16)
     leading_all = rows_all[:, 0]
     grad_pre_all = rows_all[:, 1]

time: 668 us -> 637 us (0.954)
  waiting for transfers between devices: 448 us -> 402 us
  local copies, waits for them, and re-layouts: 48.8 us -> 66.2 us
    reduce_scatter x1 -> x0, waiting for transfers between devices: 46.4 us -> none  [body(): lax.psum_scatter(jnp.dot(context, out_weight, preferred_element_type=jnp....]
    unnamed x11, waiting for transfers between devices: 18.4 us -> 1.53 us
    all_to_all x0 -> x1, waiting for transfers between devices: none -> 13.3 us  [body(): lax.all_to_all(context.reshape(tensor_count, share_rows, local_width), 't...]
    unnamed x139 -> x126, local copies, waits for them, and re-layouts: 14.3 us -> 21.3 us
  transfers between devices with their start and end apart: 10 -> 11, of which waited for: 10 -> 10; matrix products, arithmetic and copies ran while one was open for 6% -> 11% of each run, Pallas kernels for 0% -> 0%
where the time goes in v6:
time: 637 us; the launch traced here: 628 us
  waiting for transfers between devices  402 us (63%)
  matrix products  110 us (17%)
  local copies, waits for them, and re-layouts  66.2 us (10%)
  other arithmetic  30 us (5%)
  between operations  15.4 us (2%)
    all_gather x1, waiting for transfers between devices, body(): lax.all_gather(jnp.concatenate([grad_att, riding], axis=0), 'tensor', axi...  54 us
    reduce_scatter x1, waiting for transfers between devices, stacked_sum(): lax.psum_scatter(flat.reshape(-1, lanes), 'dp', scatter_dimension=0, tile...  51.6 us
    all_gather x1, waiting for transfers between devices, body(): gathered = lax.all_gather(inputs, 'tensor', axis=0, tiled=True)  51.4 us
    all_gather x1, waiting for transfers between devices, body(): first_all = lax.all_gather(first_low, 'tensor', axis=0, tiled=True)  49.1 us
    all_gather x1, waiting for transfers between devices, body(): grad_fed_all = lax.all_gather(grad_fed, 'tensor', axis=0, tiled=True)  49.1 us
    reduce_scatter x1, waiting for transfers between devices, body(): lax.psum_scatter(jnp.einsum('kte,kde->td', stacked, qkv_weight, preferred...  45.7 us
    reduce_scatter x1, waiting for transfers between devices, body(): lax.psum_scatter(jnp.dot(active, down_weight, preferred_element_type=jnp....  45 us
    reduce_scatter x1, waiting for transfers between devices, body(): lax.psum_scatter(jnp.einsum('tf,df->td', grad_up, up_weight, preferred_el...  38.5 us
  transfers between devices with their start and end apart: 11, of which 10 were waited for; matrix products, arithmetic and copies ran while one was open for 11% of the time, Pallas kernels for 0%

profile of v6, /device:TPU:0, one launch (start us, length us, event | category | flops | bytes accessed | tf_op | source)
XLA Modules:
  0.0 628.0 jit_solution(2137516453148886722)
XLA Ops:
  10.9 51.4 %all-gather.8.cloned.1.call-done = bf16[1536,768]{1,0:T(8,128)(2,1)} async-done(((bf16[384,768]{1,0:T(8,128)(2,1)}), bf16[1536,768]{1,0:T(8,128)(2,1)}) %all-gather.8.cloned.1.call-update) | async-done | bytes 2359312 | tf_op jit(solution)/shard_map/all_gather | solution.py:130
  62.3 3.5 convolution_bitcast_fusion
  70.6 2.8 squeeze.26
  81.7 3.0 fusion.81
  86.8 3.5 all-to-all-start
  92.9 13.3 %all-to-all-done = bf16[4,384,192]{1,2,0:T(8,128)(2,1)S(1)} async-done(((bf16[4,384,192]{1,2,0:T(8,128)(2,1)}), bf16[4,384,192]{1,2,0:T(8,128)(2,1)S(1)}, u32[]{:S(2)}, u32[]{:S(2)}) %all-to-all-start) | async-done | bytes 589856 | tf_op jit(solution)/shard_map/all_to_all | solution.py:140
  110.8 49.1 %all-gather.10.cloned.1.call-done = bf16[1536,768]{1,0:T(8,128)(2,1)} async-done(((bf16[384,768]{1,0:T(8,128)(2,1)}), bf16[1536,768]{1,0:T(8,128)(2,1)}) %all-gather.10.cloned.1.call-update) | async-done | bytes 2359312 | tf_op jit(solution)/shard_map/all_gather | solution.py:153
  159.9 14.5 %multiply_convert_fusion = (bf16[1536,768]{1,0:T(8,128)(2,1)S(1)}, f32[1536,768]{1,0:T(8,128)}, f32[1536,768]{1,0:T(8,128)}) fusion(f32[768]{0:T(1024)} %param.30, bf16[1536,768]{1,0:T(8,128)(2,1)} %all-gather.10.cloned.1.call-done, bf16[768,768]{1,0:T(8,128)(2,1)S(1)} %copy-done), kind=kOutput, calls=%fused_computation.21 | convolution fusion | flops 1889796096 | bytes 15338496 | tf_op jit(solution)/shard_map/dot_general | solution.py:154
  175.8 3.4 convolution_convert_fusion.1
  180.9 45.0 %reduce-scatter.8.cloned.1.call-done = bf16[384,768]{1,0:T(8,128)(2,1)} async-done(((bf16[1536,768]{1,0:T(8,128)(2,1)}), bf16[384,768]{1,0:T(8,128)(2,1)}) %reduce-scatter.8.cloned.1.call-update) | async-done | bytes 589840 | tf_op jit(solution)/shard_map/reduce_scatter | solution.py:158
  236.3 49.1 %all-gather.12.cloned.1.call-done = bf16[1536,768]{1,0:T(8,128)(2,1)} async-done(((bf16[384,768]{1,0:T(8,128)(2,1)}), bf16[1536,768]{1,0:T(8,128)(2,1)}) %all-gather.12.cloned.1.call-update) | async-done | bytes 2359312 | tf_op jit(solution)/shard_map/all_gather | solution.py:200
  285.3 8.9 %fusion.137 = (bf16[768]{0:T(1024)(128)(2,1)}, bf16[1536,768]{1,0:T(8,128)(2,1)S(1)}) fusion(f32[1536,768]{1,0:T(8,128)} %get-tuple-element.118, f32[1536,768]{1,0:T(8,128)} %get-tuple-element.136, f32[768]{0:T(1024)} %param.30, bf16[1536,768]{1,0:T(8,128)(2,1)} %all-gather.12.cloned.1.call-done, bf16[768,768]{1,0:T(8,128)(2,1)} %param.31), kind=kOutput, calls=%fused_computation.213 | convolution fusion | flops 1830812928 | bytes 15340032 | tf_op jit(solution)/shard_map/td,fd->tf/dot_general | solution.py:204
  295.6 3.5 convolution_convert_fusion
  307.2 38.5 %reduce-scatter.10.cloned.1.call-done = bf16[384,768]{1,0:T(8,128)(2,1)} async-done(((bf16[1536,768]{1,0:T(8,128)(2,1)}), bf16[384,768]{1,0:T(8,128)(2,1)}) %reduce-scatter.10.cloned.1.call-update) | async-done | bytes 589840 | tf_op jit(solution)/shard_map/reduce_scatter | solution.py:211
  357.8 54.0 %all-gather.16.cloned.1.call-done = bf16[1728,768]{1,0:T(8,128)(2,1)} async-done(((bf16[432,768]{1,0:T(8,128)(2,1)}), bf16[1728,768]{1,0:T(8,128)(2,1)}) %all-gather.16.cloned.1.call-update) | async-done | bytes 2654224 | tf_op jit(solution)/shard_map/all_gather | solution.py:271
  416.5 5.1 fusion.92
  421.6 7.2 %fusion.145 = (bf16[3,64]{1,0:T(4,128)(2,1)S(1)}, bf16[3,3,64,512]{3,2,1,0:T(8,128)(2,1)}) fusion(f32[3,3,512,512]{2,3,1,0:T(8,128)} %copy-done.1, f32[3,3,512]{2,1,0:T(4,128)S(1)} %copy-done.31, pred[3,512,512]{1,2,0:T(8,128)(4,1)S(1)} %copy-done.8, bf16[3,512,3,64]{1,0,3,2:T(4,128)(2,1)S(1)} %reshape.278), kind=kOutput, calls=%fused_computation.220 | convolution fusion | flops 312016704 | bytes 11422080 | tf_op jit(solution)/shard_map/rhqk,rqhe->rkhe/dot_general | solution.py:72
  428.7 16.2 %fusion.78 = bf16[3,512,3,64]{1,3,2,0:T(8,128)(2,1)} fusion(f32[3,3,512,512]{2,3,1,0:T(8,128)} %fusion.92, f32[3,3,512,512]{2,3,1,0:T(8,128)} %copy-done.1, f32[3,3,512]{2,1,0:T(4,128)} %log_add_fusion, pred[3,512,512]{1,2,0:T(8,128)(4,1)S(1)} %copy-done.8, bf16[3,512,3,64]{1,0,3,2:T(4,128)(2,1)} %copy-done.16), kind=kOutput, calls=%fused_computation.79 | convolution fusion | flops 328537088 | bytes 20858880 | tf_op jit(solution)/shard_map/rhqk,rqhe->rkhe/dot_general | solution.py:89
  444.9 15.3 %fusion.146 = (bf16[3,64]{1,0:T(4,128)(2,1)S(1)}, bf16[3,3,64,512]{3,2,1,0:T(8,128)(2,1)S(1)}) fusion(f32[3,3,512,512]{2,3,1,0:T(8,128)} %fusion.92, f32[3,3,512,512]{2,3,1,0:T(8,128)} %copy-done.1, f32[3,3,512]{2,1,0:T(4,128)S(1)} %copy-done.32, pred[3,512,512]{1,2,0:T(8,128)(4,1)S(1)} %copy-done.8, bf16[3,512,3,64]{1,0,3,2:T(4,128)(2,1)S(1)} %copy-done.15), kind=kOutput, calls=%fused_computation.221 | convolution fusion | flops 328831808 | bytes 20859264 | tf_op jit(solution)/shard_map/rhqk,rkhe->rqhe/dot_general | solution.py:85
  465.7 2.5 fusion.72
  476.7 4.8 bitcast_convert_fusion
  483.6 4.6 convolution_convert_fusion.4
  512.3 45.7 %reduce-scatter.12.cloned.1.call-done = bf16[384,768]{1,0:T(8,128)(2,1)} async-done(((bf16[1536,768]{1,0:T(8,128)(2,1)}), bf16[384,768]{1,0:T(8,128)(2,1)}) %reduce-scatter.12.cloned.1.call-update) | async-done | bytes 589840 | tf_op jit(solution)/shard_map/reduce_scatter | solution.py:305
  560.1 51.6 %reduce-scatter.14.cloned.1.call-done = bf16[336,768]{1,0:T(8,128)(2,1)} async-done(((bf16[2688,768]{1,0:T(8,128)(2,1)}), bf16[336,768]{1,0:T(8,128)(2,1)}) %reduce-scatter.14.cloned.1.call-update) | async-done | bytes 516112 | tf_op jit(solution)/shard_map/reduce_scatter | solution.py:323
  (263 shorter events, 116.0 us)
Async XLA Ops:
  7.2 152.7 %copy-start = (bf16[768,768]{1,0:T(8,128)(2,1)S(1)}, bf16[768,768]{1,0:T(8,128)(2,1)}, u32[]{:S(2)}) copy-start(bf16[768,768]{1,0:T(8,128)(2,1)} %param.29) | copy-start | bytes 3538948
  7.2 55.1 %all-gather.8.cloned.1.call-start = ((), (), s32[]{:S(2)}) async-start(), calls=%async_computation.6 | async-start | bytes 2949120 | tf_op jit(solution)/shard_map/all_gather | solution.py:130
  7.9 85.0 %all-gather.14.cloned.1.call-start = ((), (), s32[]{:S(2)}) async-start(), calls=%async_computation.13 | async-start | bytes 1474560 | tf_op jit(solution)/shard_map/all_gather | solution.py:138
  10.9 68.6 %copy-start.7 = (pred[3,512,512]{1,2,0:T(8,128)(4,1)}, pred[3,512,512]{1,2,0:T(8,128)(4,1)S(1)}, u32[]{:S(2)}) copy-start(pred[3,512,512]{1,2,0:T(8,128)(4,1)S(1)} %broadcast_compare_fusion) | copy-start | bytes 2359300
  84.7 22.3 %copy-start.17 = (bf16[384,768]{1,0:T(8,128)(2,1)S(1)}, bf16[384,768]{1,0:T(8,128)(2,1)}, u32[]{:S(2)}) copy-start(bf16[384,768]{1,0:T(8,128)(2,1)} %param.20) | copy-start | bytes 1769476
  84.8 22.3 %copy-start.51 = (f32[768]{0:T(1024)S(1)}, f32[768]{0:T(1024)}, u32[]{:S(2)}) copy-start(f32[768]{0:T(1024)} %param.26) | copy-start | bytes 9220
  85.3 21.0 %copy-start.2 = (bf16[3,512,3,64]{1,0,3,2:T(4,128)(2,1)}, bf16[3,512,3,64]{1,0,3,2:T(4,128)(2,1)S(1)}, u32[]{:S(2)}) copy-start(bf16[3,512,3,64]{1,0,3,2:T(4,128)(2,1)S(1)} %copy.139) | copy-start | bytes 1769476
  86.8 19.4 %all-to-all-start = ((bf16[4,384,192]{1,2,0:T(8,128)(2,1)}), bf16[4,384,192]{1,2,0:T(8,128)(2,1)S(1)}, u32[]{:S(2)}, u32[]{:S(2)}) async-start(bf16[4,384,192]{1,2,0:T(8,128)(2,1)} %copy.140), calls=%async_computation | async-start | bytes 1179648 | tf_op jit(solution)/shard_map/all_to_all | solution.py:140
  90.3 69.6 %all-gather.10.cloned.1.call-start = ((), (), s32[]{:S(2)}) async-start(), calls=%async_computation.7 | async-start | bytes 2949120 | tf_op jit(solution)/shard_map/all_gather | solution.py:153
  109.6 116.3 %copy-start.30 = (f32[384]{0:T(512)}, f32[384]{0:T(512)S(1)}, u32[]{:S(2)}) copy-start(f32[384]{0:T(512)S(1)} %add_rsqrt_fusion.1) | copy-start | bytes 4612
  110.7 65.1 %copy-start.49 = (bf16[768,768]{1,0:T(8,128)(2,1)S(1)}, bf16[768,768]{1,0:T(8,128)(2,1)}, u32[]{:S(2)}) copy-start(bf16[768,768]{1,0:T(8,128)(2,1)} %param.31) | copy-start | bytes 3538948
  110.7 115.2 %reduce-scatter.8.cloned.1.call-start = ((), (), s32[]{:S(2)}) async-start(), calls=%async_computation.8 | async-start | bytes 2949120 | tf_op jit(solution)/shard_map/reduce_scatter | solution.py:158
  179.3 106.0 %all-gather.12.cloned.1.call-start = ((), (), s32[]{:S(2)}) async-start(), calls=%async_computation.9 | async-start | bytes 2949120 | tf_op jit(solution)/shard_map/all_gather | solution.py:200
  179.4 48.4 %copy-start.33 = (s32[384]{0:T(512)}, s32[384]{0:T(512)S(1)}, u32[]{:S(2)}) copy-start(s32[384]{0:T(512)S(1)} %iota_add_fusion) | copy-start | bytes 4612
  180.9 49.0 %copy-start.5 = (bf16[768,768]{1,0:T(8,128)(2,1)S(1)}, bf16[768,768]{1,0:T(8,128)(2,1)}, u32[]{:S(2)}) copy-start(bf16[768,768]{1,0:T(8,128)(2,1)} %param.35) | copy-start | bytes 3538948
  235.8 109.9 %reduce-scatter.10.cloned.1.call-start = ((), (), s32[]{:S(2)}) async-start(), calls=%async_computation.10 | async-start | bytes 2949120 | tf_op jit(solution)/shard_map/reduce_scatter | solution.py:211
  299.1 112.7 %all-gather.16.cloned.1.call-start = ((), (), s32[]{:S(2)}) async-start(), calls=%async_computation.14 | async-start | bytes 3317760 | tf_op jit(solution)/shard_map/all_gather | solution.py:271
  300.6 47.5 %copy-start.28 = (f32[768]{0:T(1024)S(1)}, f32[768]{0:T(1024)}, u32[]{:S(2)}) copy-start(f32[768]{0:T(1024)} %param.27) | copy-start | bytes 9220
  357.0 151.6 %reduce-scatter.16.cloned.1.call-start = ((), (), s32[]{:S(2)}) async-start(), calls=%async_computation.15 | async-start | bytes 1290240
  428.7 16.2 %copy-start.15 = (bf16[3,512,3,64]{1,0,3,2:T(4,128)(2,1)S(1)}, bf16[3,512,3,64]{1,0,3,2:T(4,128)(2,1)}, u32[]{:S(2)}) copy-start(bf16[3,512,3,64]{1,0,3,2:T(4,128)(2,1)} %convert_element_type.292) | copy-start | bytes 1769476
  428.7 16.2 %copy-start.32 = (f32[3,3,512]{2,1,0:T(4,128)S(1)}, f32[3,3,512]{2,1,0:T(4,128)}, u32[]{:S(2)}) copy-start(f32[3,3,512]{2,1,0:T(4,128)} %log_add_fusion) | copy-start | bytes 55300
  472.8 85.3 %reduce-scatter.12.cloned.1.call-start = ((), (), s32[]{:S(2)}) async-start(), calls=%async_computation.11 | async-start | bytes 2949120 | tf_op jit(solution)/shard_map/reduce_scatter | solution.py:305
  481.5 130.1 %reduce-scatter.14.cloned.1.call-start = ((), (), s32[]{:S(2)}) async-start(), calls=%async_computation.12 | async-start | bytes 4644864 | tf_op jit(solution)/shard_map/reduce_scatter | solution.py:323
  508.5 49.5 %copy-start.6 = (f32[384,768]{1,0:T(8,128)S(1)}, f32[384,768]{1,0:T(8,128)}, u32[]{:S(2)}) copy-start(f32[384,768]{1,0:T(8,128)} %get-tuple-element.114) | copy-start | bytes 3538948
  (43 other events, 128.7 us)
Sparse Core Ops, SparseCore 0:
  9.6 52.6 all-gather.7
  63.9 29.0 all-gather.13
  110.8 49.0 all-gather.9
  179.4 46.4 reduce-scatter.7
  235.9 49.3 all-gather.11
  299.3 46.4 reduce-scatter.9
  357.1 54.6 all-gather.15
  472.9 34.5 reduce-scatter.15
  510.3 47.6 reduce-scatter.11
  561.3 50.2 reduce-scatter.13

commit v7 on v6

--- a/solution.py
+++ b/solution.py
@@ -262,29 +262,40 @@
     small_round = lax.reduce_precision(small_flat, exponent_bits=8, mantissa_bits=7)
     small_high = small_round.astype(jnp.bfloat16)
     small_low = (small_flat - small_round).astype(jnp.bfloat16)
-    small_rows = -(-2 * small_flat.size // model_width)
+    small_lanes = local_width
+    small_rows = -(-2 * small_flat.size // small_lanes)
     small_rows += (-(share_rows + small_rows)) % 16
-    small_pad = small_rows * model_width - 2 * small_flat.size
+    small_pad = small_rows * small_lanes - 2 * small_flat.size
     riding = jnp.concatenate(
         [small_high, small_low, jnp.zeros((small_pad,), jnp.bfloat16)]
-    ).reshape(small_rows, model_width)
-    att_gathered = lax.all_gather(
-        jnp.concatenate([grad_att, riding], axis=0), "tensor", axis=0, tiled=False
-    )
-    grad_att_all = att_gathered[:, :share_rows].reshape(group_rows, model_width)
-    small_back = att_gathered[:, share_rows:].reshape(tensor_count, -1)
+    ).reshape(1, small_rows, small_lanes)
+    context_heads = jnp.einsum(
+        "td,jcd->jtc", grad_att, out_weight_all, preferred_element_type=jnp.float32
+    ).astype(jnp.bfloat16)
+    heads_back = lax.all_to_all(
+        jnp.concatenate(
+            [context_heads, jnp.broadcast_to(riding, (tensor_count, small_rows, small_lanes))],
+            axis=1,
+        ),
+        "tensor",
+        0,
+        0,
+        tiled=False,
+    )
+    grad_context = heads_back[:, :share_rows].reshape(group_rows, local_width)
+    small_back = heads_back[:, share_rows:].reshape(tensor_count, -1)
     small_total = jnp.sum(
         small_back[:, : small_flat.size].astype(jnp.float32)
         + small_back[:, small_flat.size : 2 * small_flat.size].astype(jnp.float32),
         axis=0,
     )
     token_sum, rows_group = parted(small_total, token_parts)
-    out_weight_grad_t = jnp.einsum(
-        "td,te->de", grad_att_all, context, preferred_element_type=jnp.float32
-    )
-    grad_context = jnp.einsum(
-        "td,ed->te", grad_att_all, out_weight, preferred_element_type=jnp.float32
-    ).astype(jnp.bfloat16)
+    out_weight_full = jnp.einsum(
+        "itc,td->icd", context_own, grad_att, preferred_element_type=jnp.float32
+    ).reshape(tensor_count * local_width, model_width)
+    out_weight_grad_t = lax.psum_scatter(
+        out_weight_full.astype(jnp.bfloat16), "tensor", scatter_dimension=0, tiled=True
+    ).T
     grad_queries, grad_keys, grad_values = attend_backward(
         queries, key_rows, value_rows, segments, log_totals, grad_context
     )

time: 637 us -> 628 us (0.986)
  local copies, waits for them, and re-layouts: 66.2 us -> 56.2 us
  waiting for transfers between devices: 402 us -> 395 us
    all_gather x1 -> x0, waiting for transfers between devices: 54 us -> none  [body(): lax.all_gather(jnp.concatenate([grad_att, riding], axis=0), 'tensor', axi...]
    all_to_all x0 -> x1, waiting for transfers between devices: none -> 37.1 us  [body(): lax.all_to_all(jnp.concatenate([context_heads, jnp.broadcast_to(riding, (...]
    unnamed x11 -> x12, waiting for transfers between devices: 1.53 us -> 10.5 us
    unnamed x126 -> x107, local copies, waits for them, and re-layouts: 21.3 us -> 15.9 us
  transfers between devices with their start and end apart: 11 -> 12, of which waited for: 10 -> 11; matrix products, arithmetic and copies ran while one was open for 11% -> 21% of each run, Pallas kernels for 0% -> 0%
where the time goes in v7:
time: 628 us; the launch traced here: 618 us
  waiting for transfers between devices  395 us (63%)
  matrix products  114 us (18%)
  local copies, waits for them, and re-layouts  56.2 us (9%)
  other arithmetic  28.6 us (5%)
  between operations  15.5 us (2%)
  starting transfers between devices  8.44 us (1%)
    reduce_scatter x1, waiting for transfers between devices, stacked_sum(): lax.psum_scatter(flat.reshape(-1, lanes), 'dp', scatter_dimension=0, tile...  51.6 us
    all_gather x1, waiting for transfers between devices, body(): gathered = lax.all_gather(inputs, 'tensor', axis=0, tiled=True)  51.4 us
    all_gather x1, waiting for transfers between devices, body(): grad_fed_all = lax.all_gather(grad_fed, 'tensor', axis=0, tiled=True)  49.1 us
    all_gather x1, waiting for transfers between devices, body(): first_all = lax.all_gather(first_low, 'tensor', axis=0, tiled=True)  48.9 us
    reduce_scatter x1, waiting for transfers between devices, body(): lax.psum_scatter(jnp.einsum('kte,kde->td', stacked, qkv_weight, preferred...  47 us
    reduce_scatter x1, waiting for transfers between devices, body(): lax.psum_scatter(jnp.dot(active, down_weight, preferred_element_type=jnp....  45 us
    reduce_scatter x1, waiting for transfers between devices, body(): lax.psum_scatter(jnp.einsum('tf,df->td', grad_up, up_weight, preferred_el...  38.6 us
    all_to_all x1, waiting for transfers between devices, body(): lax.all_to_all(jnp.concatenate([context_heads, jnp.broadcast_to(riding, (...  37.1 us
  transfers between devices with their start and end apart: 12, of which 11 were waited for; matrix products, arithmetic and copies ran while one was open for 21% of the time, Pallas kernels for 0%

profile of v7, /device:TPU:0, one launch (start us, length us, event | category | flops | bytes accessed | tf_op | source)
XLA Modules:
  0.0 618.0 jit_solution(5154511767106498211)
XLA Ops:
  10.9 51.4 %all-gather.6.cloned.1.call-done = bf16[1536,768]{1,0:T(8,128)(2,1)} async-done(((bf16[384,768]{1,0:T(8,128)(2,1)}), bf16[1536,768]{1,0:T(8,128)(2,1)}) %all-gather.6.cloned.1.call-update) | async-done | bytes 2359312 | tf_op jit(solution)/shard_map/all_gather | solution.py:130
  62.4 3.5 convolution_bitcast_fusion
  81.5 3.0 fusion.82
  86.7 3.5 all-to-all-start
  93.0 13.1 %all-to-all-done = bf16[4,384,192]{1,2,0:T(8,128)(2,1)S(1)} async-done(((bf16[4,384,192]{1,2,0:T(8,128)(2,1)}), bf16[4,384,192]{1,2,0:T(8,128)(2,1)S(1)}, u32[]{:S(2)}, u32[]{:S(2)}) %all-to-all-start) | async-done | bytes 589856 | tf_op jit(solution)/shard_map/all_to_all | solution.py:140
  110.2 48.9 %all-gather.8.cloned.1.call-done = bf16[1536,768]{1,0:T(8,128)(2,1)} async-done(((bf16[384,768]{1,0:T(8,128)(2,1)}), bf16[1536,768]{1,0:T(8,128)(2,1)}) %all-gather.8.cloned.1.call-update) | async-done | bytes 2359312 | tf_op jit(solution)/shard_map/all_gather | solution.py:153
  159.1 14.5 %multiply_convert_fusion = (bf16[1536,768]{1,0:T(8,128)(2,1)S(1)}, f32[1536,768]{1,0:T(8,128)}, f32[1536,768]{1,0:T(8,128)}) fusion(f32[768]{0:T(1024)} %param.30, bf16[1536,768]{1,0:T(8,128)(2,1)} %all-gather.8.cloned.1.call-done, bf16[768,768]{1,0:T(8,128)(2,1)S(1)} %copy-done), kind=kOutput, calls=%fused_computation.21 | convolution fusion | flops 1889796096 | bytes 15338496 | tf_op jit(solution)/shard_map/dot_general | solution.py:154
  175.1 3.4 convolution_convert_fusion.1
  180.2 45.0 %reduce-scatter.11.cloned.1.call-done = bf16[384,768]{1,0:T(8,128)(2,1)} async-done(((bf16[1536,768]{1,0:T(8,128)(2,1)}), bf16[384,768]{1,0:T(8,128)(2,1)}) %reduce-scatter.11.cloned.1.call-update) | async-done | bytes 589840 | tf_op jit(solution)/shard_map/reduce_scatter | solution.py:158
  235.6 49.1 %all-gather.10.cloned.1.call-done = bf16[1536,768]{1,0:T(8,128)(2,1)} async-done(((bf16[384,768]{1,0:T(8,128)(2,1)}), bf16[1536,768]{1,0:T(8,128)(2,1)}) %all-gather.10.cloned.1.call-update) | async-done | bytes 2359312 | tf_op jit(solution)/shard_map/all_gather | solution.py:200
  284.6 8.7 %fusion.142 = (bf16[768]{0:T(1024)(128)(2,1)}, bf16[1536,768]{1,0:T(8,128)(2,1)S(1)}) fusion(f32[1536,768]{1,0:T(8,128)} %get-tuple-element.117, f32[1536,768]{1,0:T(8,128)} %get-tuple-element.135, f32[768]{0:T(1024)} %param.30, bf16[1536,768]{1,0:T(8,128)(2,1)} %all-gather.10.cloned.1.call-done, bf16[768,768]{1,0:T(8,128)(2,1)} %param.31), kind=kOutput, calls=%fused_computation.216 | convolution fusion | flops 1830812928 | bytes 15340032 | tf_op jit(solution)/shard_map/td,fd->tf/dot_general | solution.py:204
  294.9 3.5 convolution_convert_fusion
  306.4 38.6 %reduce-scatter.13.cloned.1.call-done = bf16[384,768]{1,0:T(8,128)(2,1)} async-done(((bf16[1536,768]{1,0:T(8,128)(2,1)}), bf16[384,768]{1,0:T(8,128)(2,1)}) %reduce-scatter.13.cloned.1.call-update) | async-done | bytes 589840 | tf_op jit(solution)/shard_map/reduce_scatter | solution.py:211
  353.5 3.5 all-to-all-start.1
  360.3 37.1 %all-to-all-done.1 = bf16[4,528,192]{1,2,0:T(8,128)(2,1)S(1)} async-done(((bf16[4,528,192]{1,2,0:T(8,128)(2,1)}), bf16[4,528,192]{1,2,0:T(8,128)(2,1)S(1)}, u32[]{:S(2)}, u32[]{:S(2)}) %all-to-all-start.1) | async-done | bytes 811040 | tf_op jit(solution)/shard_map/all_to_all | solution.py:275
  401.5 6.5 %fusion.95 = f32[3,3,512,512]{2,3,1,0:T(8,128)} fusion(bf16[3,512,3,64]{1,0,3,2:T(4,128)(2,1)} %reshape_reshape.9, bf16[3,512,3,64]{1,0,3,2:T(4,128)(2,1)} %copy-done.9), kind=kOutput, calls=%fused_computation.121 | convolution fusion | flops 301989888 | bytes 10616832 | tf_op jit(solution)/shard_map/rqhe,rkhe->rhqk/dot_general | solution.py:78
  407.9 16.5 %fusion.151 = (bf16[3,64]{1,0:T(4,128)(2,1)S(1)}, bf16[3,3,64,512]{3,2,1,0:T(8,128)(2,1)}) fusion(f32[3,3,512,512]{2,3,1,0:T(8,128)} %fusion.95, f32[3,3,512,512]{2,3,1,0:T(8,128)} %copy-done.2, f32[3,3,512]{2,1,0:T(4,128)S(1)} %log_add_fusion, pred[3,512,512]{1,2,0:T(8,128)(4,1)} %copy-done.7, bf16[3,512,3,64]{1,0,3,2:T(4,128)(2,1)} %convert_element_type.293), kind=kOutput, calls=%fused_computation.224 | convolution fusion | flops 328831808 | bytes 20859264 | tf_op jit(solution)/shard_map/rhqk,rkhe->rqhe/dot_general | solution.py:85
  427.0 16.9 %fusion.79 = bf16[3,512,3,64]{1,3,2,0:T(8,128)(2,1)} fusion(f32[3,3,512,512]{2,3,1,0:T(8,128)} %fusion.95, f32[3,3,512,512]{2,3,1,0:T(8,128)} %copy-done.2, f32[3,3,512]{2,1,0:T(4,128)S(1)} %log_add_fusion, pred[3,512,512]{1,2,0:T(8,128)(4,1)} %copy-done.7, bf16[3,512,3,64]{1,0,3,2:T(4,128)(2,1)} %copy-done.14), kind=kOutput, calls=%fused_computation.81 | convolution fusion | flops 328537088 | bytes 20858880 | tf_op jit(solution)/shard_map/rhqk,rqhe->rkhe/dot_general | solution.py:89
  446.7 6.6 %fusion.150 = (bf16[3,64]{1,0:T(4,128)(2,1)S(1)}, bf16[3,3,64,512]{3,2,1,0:T(8,128)(2,1)S(1)}) fusion(f32[3,3,512,512]{2,3,1,0:T(8,128)} %copy-done.2, f32[3,3,512]{2,1,0:T(4,128)S(1)} %log_add_fusion, pred[3,512,512]{1,2,0:T(8,128)(4,1)S(1)} %copy-done.8, bf16[3,512,3,64]{1,0,3,2:T(4,128)(2,1)S(1)} %copy-done.10), kind=kOutput, calls=%fused_computation.223 | convolution fusion | flops 312016704 | bytes 11422080 | tf_op jit(solution)/shard_map/rhqk,rqhe->rkhe/dot_general | solution.py:72
  468.2 4.9 bitcast_convert_fusion
  473.4 4.6 convolution_convert_fusion.4
  488.5 8.9 %reduce-scatter.19.cloned.1.call-done = bf16[112,576]{1,0:T(8,128)(2,1)} async-done(((bf16[896,576]{1,0:T(8,128)(2,1)}), bf16[112,576]{1,0:T(8,128)(2,1)}) %reduce-scatter.19.cloned.1.call-update) | async-done | bytes 129040
  501.0 47.0 %reduce-scatter.15.cloned.1.call-done = bf16[384,768]{1,0:T(8,128)(2,1)} async-done(((bf16[1536,768]{1,0:T(8,128)(2,1)}), bf16[384,768]{1,0:T(8,128)(2,1)}) %reduce-scatter.15.cloned.1.call-update) | async-done | bytes 589840 | tf_op jit(solution)/shard_map/reduce_scatter | solution.py:316
  550.0 51.6 %reduce-scatter.17.cloned.1.call-done = bf16[336,768]{1,0:T(8,128)(2,1)} async-done(((bf16[2688,768]{1,0:T(8,128)(2,1)}), bf16[336,768]{1,0:T(8,128)(2,1)}) %reduce-scatter.17.cloned.1.call-update) | async-done | bytes 516112 | tf_op jit(solution)/shard_map/reduce_scatter | solution.py:334
  (250 shorter events, 112.1 us)
Async XLA Ops:
  7.2 151.9 %copy-start = (bf16[768,768]{1,0:T(8,128)(2,1)S(1)}, bf16[768,768]{1,0:T(8,128)(2,1)}, u32[]{:S(2)}) copy-start(bf16[768,768]{1,0:T(8,128)(2,1)} %param.29) | copy-start | bytes 3538948
  7.2 55.2 %all-gather.6.cloned.1.call-start = ((), (), s32[]{:S(2)}) async-start(), calls=%async_computation.8 | async-start | bytes 2949120 | tf_op jit(solution)/shard_map/all_gather | solution.py:130
  7.9 85.1 %all-gather.12.cloned.1.call-start = ((), (), s32[]{:S(2)}) async-start(), calls=%async_computation.15 | async-start | bytes 1474560 | tf_op jit(solution)/shard_map/all_gather | solution.py:138
  10.8 69.5 %copy-start.7 = (pred[3,512,512]{1,2,0:T(8,128)(4,1)}, pred[3,512,512]{1,2,0:T(8,128)(4,1)S(1)}, u32[]{:S(2)}) copy-start(pred[3,512,512]{1,2,0:T(8,128)(4,1)S(1)} %broadcast_compare_fusion) | copy-start | bytes 2359300
  84.6 21.5 %copy-start.43 = (f32[768]{0:T(1024)S(1)}, f32[768]{0:T(1024)}, u32[]{:S(2)}) copy-start(f32[768]{0:T(1024)} %param.26) | copy-start | bytes 9220
  86.7 19.5 %all-to-all-start = ((bf16[4,384,192]{1,2,0:T(8,128)(2,1)}), bf16[4,384,192]{1,2,0:T(8,128)(2,1)S(1)}, u32[]{:S(2)}, u32[]{:S(2)}) async-start(bf16[4,384,192]{1,2,0:T(8,128)(2,1)} %copy.145), calls=%async_computation | async-start | bytes 1179648 | tf_op jit(solution)/shard_map/all_to_all | solution.py:140
  90.1 69.0 %all-gather.8.cloned.1.call-start = ((), (), s32[]{:S(2)}) async-start(), calls=%async_computation.9 | async-start | bytes 2949120 | tf_op jit(solution)/shard_map/all_gather | solution.py:153
  108.9 116.4 %copy-start.24 = (f32[384]{0:T(512)}, f32[384]{0:T(512)S(1)}, u32[]{:S(2)}) copy-start(f32[384]{0:T(512)S(1)} %add_rsqrt_fusion.1) | copy-start | bytes 4612
  110.0 65.2 %copy-start.41 = (bf16[768,768]{1,0:T(8,128)(2,1)S(1)}, bf16[768,768]{1,0:T(8,128)(2,1)}, u32[]{:S(2)}) copy-start(bf16[768,768]{1,0:T(8,128)(2,1)} %param.31) | copy-start | bytes 3538948
  110.0 115.3 %reduce-scatter.11.cloned.1.call-start = ((), (), s32[]{:S(2)}) async-start(), calls=%async_computation.10 | async-start | bytes 2949120 | tf_op jit(solution)/shard_map/reduce_scatter | solution.py:158
  178.6 106.0 %all-gather.10.cloned.1.call-start = ((), (), s32[]{:S(2)}) async-start(), calls=%async_computation.11 | async-start | bytes 2949120 | tf_op jit(solution)/shard_map/all_gather | solution.py:200
  178.7 48.4 %copy-start.25 = (s32[384]{0:T(512)}, s32[384]{0:T(512)S(1)}, u32[]{:S(2)}) copy-start(s32[384]{0:T(512)S(1)} %iota_add_fusion) | copy-start | bytes 4612
  180.2 49.0 %copy-start.5 = (bf16[768,768]{1,0:T(8,128)(2,1)S(1)}, bf16[768,768]{1,0:T(8,128)(2,1)}, u32[]{:S(2)}) copy-start(bf16[768,768]{1,0:T(8,128)(2,1)} %param.35) | copy-start | bytes 3538948
  235.1 109.9 %copy-start.1 = (f32[384,768]{1,0:T(8,128)}, f32[384,768]{1,0:T(8,128)S(1)}, u32[]{:S(2)}) copy-start(f32[384,768]{1,0:T(8,128)S(1)} %get-tuple-element.111) | copy-start | bytes 3538948
  235.1 109.9 %reduce-scatter.13.cloned.1.call-start = ((), (), s32[]{:S(2)}) async-start(), calls=%async_computation.12 | async-start | bytes 2949120 | tf_op jit(solution)/shard_map/reduce_scatter | solution.py:211
  303.7 43.1 %copy-start.22 = (f32[768]{0:T(1024)S(1)}, f32[768]{0:T(1024)}, u32[]{:S(2)}) copy-start(f32[768]{0:T(1024)} %param.27) | copy-start | bytes 9220
  353.5 43.8 %all-to-all-start.1 = ((bf16[4,528,192]{1,2,0:T(8,128)(2,1)}), bf16[4,528,192]{1,2,0:T(8,128)(2,1)S(1)}, u32[]{:S(2)}, u32[]{:S(2)}) async-start(bf16[4,528,192]{1,2,0:T(8,128)(2,1)} %pad_maximum_fusion), calls=%async_computation.3 | async-start | bytes 1966080 | tf_op jit(solution)/shard_map/all_to_all | solution.py:275
  357.1 127.2 %reduce-scatter.21.cloned.1.call-start = ((), (), s32[]{:S(2)}) async-start(), calls=%async_computation.17 | async-start | bytes 1474560
  360.0 137.4 %reduce-scatter.19.cloned.1.call-start = ((), (), s32[]{:S(2)}) async-start(), calls=%async_computation.16 | async-start | bytes 1290240
  397.4 10.6 %copy-start.6 = (bf16[4,528,192]{1,2,0:T(8,128)(2,1)}, bf16[4,528,192]{1,2,0:T(8,128)(2,1)S(1)}, u32[]{:S(2)}) copy-start(bf16[4,528,192]{1,2,0:T(8,128)(2,1)S(1)} %all-to-all-done.1) | copy-start | bytes 2433028
  446.6 8.2 %copy-start.39 = (bf16[1536,768]{1,0:T(8,128)(2,1)S(1)}, bf16[1536,768]{1,0:T(8,128)(2,1)}, u32[]{:S(2)}) copy-start(bf16[1536,768]{1,0:T(8,128)(2,1)} %all-gather.6.cloned.1.call-done) | copy-start | bytes 7077892
  462.2 85.9 %reduce-scatter.15.cloned.1.call-start = ((), (), s32[]{:S(2)}) async-start(), calls=%async_computation.13 | async-start | bytes 2949120 | tf_op jit(solution)/shard_map/reduce_scatter | solution.py:316
  473.1 128.6 %reduce-scatter.17.cloned.1.call-start = ((), (), s32[]{:S(2)}) async-start(), calls=%async_computation.14 | async-start | bytes 4644864 | tf_op jit(solution)/shard_map/reduce_scatter | solution.py:334
  473.4 5.7 copy-start.46
  (37 other events, 93.4 us)
Sparse Core Ops, SparseCore 0:
  9.6 52.7 all-gather.5
  63.9 29.0 all-gather.11
  110.1 48.9 all-gather.7
  178.7 46.4 reduce-scatter.10
  235.3 49.3 all-gather.9
  298.5 46.4 reduce-scatter.12
  360.2 40.3 reduce-scatter.20
  462.3 35.0 reduce-scatter.18
  500.3 47.6 reduce-scatter.14
  551.3 50.2 reduce-scatter.16

commit v8 on v6

--- a/solution.py
+++ b/solution.py
@@ -367,9 +367,12 @@
         rows_each = early_sums[4].reshape(-1)[: rows_slotted.size]
     late_shared = [qv_bias_grad]
     qkv_lanes = qkv_weight_grad.shape[1]
-    late_sums = stacked_sum(
-        [in_blocks(qkv_weight_grad), copied(joined(late_shared), qkv_lanes)], jnp.bfloat16
-    )
+    late_parts = [in_blocks(qkv_weight_grad), copied(joined(late_shared), qkv_lanes)]
+    late_received = lax.all_to_all(
+        jnp.concatenate(late_parts, axis=1), "dp", 0, 0, tiled=False
+    )
+    late_total = jnp.sum(late_received, axis=0)
+    late_sums = [late_total[: late_parts[0].shape[1]], late_total[late_parts[0].shape[1] :]]
     qkv_sum = jnp.transpose(
         late_sums[0].reshape(late_sums[0].shape[0], 3, qkv_lanes // 3), (1, 0, 2)
     ).astype(jnp.float32)

time: 637 us -> 600 us (0.942)
  waiting for transfers between devices: 402 us -> 336 us
  blocking collectives: 0 us -> 30.4 us
    reduce_scatter x1, waiting for transfers between devices: 45.7 us -> 0.01 us  [body(): lax.psum_scatter(jnp.einsum('kte,kde->td', stacked, qkv_weight, preferred...]
    all_to_all x0 -> x1, blocking collectives: none -> 30.4 us  [body(): lax.all_to_all(jnp.concatenate(late_parts, axis=1), 'dp', 0, 0, tiled=False)]
    reduce_scatter x1, waiting for transfers between devices: 51.6 us -> 31.7 us  [stacked_sum(): lax.psum_scatter(flat.reshape(-1, lanes), 'dp', scatter_dimension=0, tile...]
    unnamed x126 -> x124, local copies, waits for them, and re-layouts: 21.3 us -> 22.8 us
  transfers between devices with their start and end apart: 11 -> 10, of which waited for: 10 -> 9; matrix products, arithmetic and copies ran while one was open for 11% -> 11% of each run, Pallas kernels for 0% -> 0%
where the time goes in v8:
time: 600 us; the launch traced here: 591 us
  waiting for transfers between devices  336 us (56%)
  matrix products  113 us (19%)
  local copies, waits for them, and re-layouts  63.9 us (11%)
  blocking collectives  30.4 us (5%)
  other arithmetic  27.8 us (5%)
  between operations  15.1 us (3%)
    all_gather x1, waiting for transfers between devices, body(): lax.all_gather(jnp.concatenate([grad_att, riding], axis=0), 'tensor', axi...  54.1 us
    all_gather x1, waiting for transfers between devices, body(): gathered = lax.all_gather(inputs, 'tensor', axis=0, tiled=True)  51.4 us
    all_gather x1, waiting for transfers between devices, body(): first_all = lax.all_gather(first_low, 'tensor', axis=0, tiled=True)  49.1 us
    all_gather x1, waiting for transfers between devices, body(): grad_fed_all = lax.all_gather(grad_fed, 'tensor', axis=0, tiled=True)  49.1 us
    reduce_scatter x1, waiting for transfers between devices, body(): lax.psum_scatter(jnp.dot(active, down_weight, preferred_element_type=jnp....  45 us
    reduce_scatter x1, waiting for transfers between devices, body(): lax.psum_scatter(jnp.einsum('tf,df->td', grad_up, up_weight, preferred_el...  38.5 us
    reduce_scatter x1, waiting for transfers between devices, stacked_sum(): lax.psum_scatter(flat.reshape(-1, lanes), 'dp', scatter_dimension=0, tile...  31.7 us
    all_to_all x1, blocking collectives, body(): lax.all_to_all(jnp.concatenate(late_parts, axis=1), 'dp', 0, 0, tiled=False)  30.4 us
  transfers between devices with their start and end apart: 10, of which 9 were waited for; matrix products, arithmetic and copies ran while one was open for 11% of the time, Pallas kernels for 0%

profile of v8, /device:TPU:0, one launch (start us, length us, event | category | flops | bytes accessed | tf_op | source)
XLA Modules:
  0.0 590.9 jit_solution(4772669153601765406)
XLA Ops:
  10.9 51.4 %all-gather.8.cloned.1.call-done = bf16[1536,768]{1,0:T(8,128)(2,1)} async-done(((bf16[384,768]{1,0:T(8,128)(2,1)}), bf16[1536,768]{1,0:T(8,128)(2,1)}) %all-gather.8.cloned.1.call-update) | async-done | bytes 2359312 | tf_op jit(solution)/shard_map/all_gather | solution.py:130
  62.3 3.5 convolution_bitcast_fusion
  81.7 3.0 fusion.77
  86.8 3.5 all-to-all-start
  92.9 13.3 %all-to-all-done = bf16[4,384,192]{1,2,0:T(8,128)(2,1)S(1)} async-done(((bf16[4,384,192]{1,2,0:T(8,128)(2,1)}), bf16[4,384,192]{1,2,0:T(8,128)(2,1)S(1)}, u32[]{:S(2)}, u32[]{:S(2)}) %all-to-all-start) | async-done | bytes 589856 | tf_op jit(solution)/shard_map/all_to_all | solution.py:140
  110.8 49.1 %all-gather.10.cloned.1.call-done = bf16[1536,768]{1,0:T(8,128)(2,1)} async-done(((bf16[384,768]{1,0:T(8,128)(2,1)}), bf16[1536,768]{1,0:T(8,128)(2,1)}) %all-gather.10.cloned.1.call-update) | async-done | bytes 2359312 | tf_op jit(solution)/shard_map/all_gather | solution.py:153
  159.9 14.5 %multiply_convert_fusion = (bf16[1536,768]{1,0:T(8,128)(2,1)S(1)}, f32[1536,768]{1,0:T(8,128)}, f32[1536,768]{1,0:T(8,128)}) fusion(f32[768]{0:T(1024)} %param.30, bf16[1536,768]{1,0:T(8,128)(2,1)} %all-gather.10.cloned.1.call-done, bf16[768,768]{1,0:T(8,128)(2,1)S(1)} %copy-done), kind=kOutput, calls=%fused_computation.21 | convolution fusion | flops 1889796096 | bytes 15338496 | tf_op jit(solution)/shard_map/dot_general | solution.py:154
  175.8 3.4 convolution_convert_fusion.1
  180.9 45.0 %reduce-scatter.5.cloned.1.call-done = bf16[384,768]{1,0:T(8,128)(2,1)} async-done(((bf16[1536,768]{1,0:T(8,128)(2,1)}), bf16[384,768]{1,0:T(8,128)(2,1)}) %reduce-scatter.5.cloned.1.call-update) | async-done | bytes 589840 | tf_op jit(solution)/shard_map/reduce_scatter | solution.py:158
  236.3 49.1 %all-gather.12.cloned.1.call-done = bf16[1536,768]{1,0:T(8,128)(2,1)} async-done(((bf16[384,768]{1,0:T(8,128)(2,1)}), bf16[1536,768]{1,0:T(8,128)(2,1)}) %all-gather.12.cloned.1.call-update) | async-done | bytes 2359312 | tf_op jit(solution)/shard_map/all_gather | solution.py:200
  285.3 8.9 %fusion.132 = (bf16[768]{0:T(1024)(128)(2,1)}, bf16[1536,768]{1,0:T(8,128)(2,1)S(1)}) fusion(f32[1536,768]{1,0:T(8,128)} %get-tuple-element.118, f32[1536,768]{1,0:T(8,128)} %get-tuple-element.136, f32[768]{0:T(1024)} %param.30, bf16[1536,768]{1,0:T(8,128)(2,1)} %all-gather.12.cloned.1.call-done, bf16[768,768]{1,0:T(8,128)(2,1)} %param.31), kind=kOutput, calls=%fused_computation.211 | convolution fusion | flops 1830812928 | bytes 15340032 | tf_op jit(solution)/shard_map/td,fd->tf/dot_general | solution.py:204
  295.6 3.5 convolution_convert_fusion
  307.2 38.5 %reduce-scatter.7.cloned.1.call-done = bf16[384,768]{1,0:T(8,128)(2,1)} async-done(((bf16[1536,768]{1,0:T(8,128)(2,1)}), bf16[384,768]{1,0:T(8,128)(2,1)}) %reduce-scatter.7.cloned.1.call-update) | async-done | bytes 589840 | tf_op jit(solution)/shard_map/reduce_scatter | solution.py:211
  357.7 54.1 %all-gather.16.cloned.1.call-done = bf16[1728,768]{1,0:T(8,128)(2,1)} async-done(((bf16[432,768]{1,0:T(8,128)(2,1)}), bf16[1728,768]{1,0:T(8,128)(2,1)}) %all-gather.16.cloned.1.call-update) | async-done | bytes 2654224 | tf_op jit(solution)/shard_map/all_gather | solution.py:271
  416.6 5.1 fusion.87
  421.7 7.2 %convert_reduce_fusion = (f32[3,64]{1,0:T(4,128)S(1)}, bf16[3,3,64,512]{3,2,1,0:T(8,128)(2,1)}) fusion(f32[3,3,512,512]{2,3,1,0:T(8,128)} %copy-done.1, f32[3,3,512]{2,1,0:T(4,128)S(1)} %copy-done.32, pred[3,512,512]{1,2,0:T(8,128)(4,1)S(1)} %copy-done.10, bf16[3,512,3,64]{1,0,3,2:T(4,128)(2,1)S(1)} %reshape.270), kind=kOutput, calls=%fused_computation.81 | convolution fusion | flops 312311616 | bytes 11422464 | tf_op jit(solution)/shard_map/rhqk,rqhe->rkhe/dot_general | solution.py:72
  428.9 16.2 %fusion.74 = bf16[3,512,3,64]{1,3,2,0:T(8,128)(2,1)} fusion(f32[3,3,512,512]{2,3,1,0:T(8,128)} %fusion.87, f32[3,3,512,512]{2,3,1,0:T(8,128)} %copy-done.1, f32[3,3,512]{2,1,0:T(4,128)} %log_add_fusion, pred[3,512,512]{1,2,0:T(8,128)(4,1)S(1)} %copy-done.10, bf16[3,512,3,64]{1,0,3,2:T(4,128)(2,1)} %copy-done.17), kind=kOutput, calls=%fused_computation.77 | convolution fusion | flops 328537088 | bytes 20858880 | tf_op jit(solution)/shard_map/rhqk,rqhe->rkhe/dot_general | solution.py:89
  445.1 15.8 %convert_reduce_fusion.1 = (f32[3,64]{1,0:T(4,128)S(1)}, bf16[3,3,64,512]{3,2,1,0:T(8,128)(2,1)}) fusion(f32[3,3,512,512]{2,3,1,0:T(8,128)} %fusion.87, f32[3,3,512,512]{2,3,1,0:T(8,128)} %copy-done.1, f32[3,3,512]{2,1,0:T(4,128)S(1)} %copy-done.33, pred[3,512,512]{1,2,0:T(8,128)(4,1)S(1)} %copy-done.10, bf16[3,512,3,64]{1,0,3,2:T(4,128)(2,1)S(1)} %copy-done.16), kind=kOutput, calls=%fused_computation.82 | convolution fusion | flops 329126720 | bytes 20859648 | tf_op jit(solution)/shard_map/rhqk,rkhe->rqhe/dot_general | solution.py:85
  469.4 5.2 bitcast_convert_fusion
  476.7 4.6 convolution_convert_fusion.4
  488.8 3.0 convolution_convert_fusion.5
  500.1 4.4 fusion.53
  506.6 30.4 %all_to_all.10 = f32[8,97,576]{2,1,0:T(8,128)S(1)} all-to-all(f32[8,97,576]{2,1,0:T(8,128)S(1)} %pad_maximum_fusion), channel_id=1, replica_groups=mesh['dp'=8,'tensor'=4] {'dp'}, dimensions={0} | all-to-all | bytes 3575808 | tf_op jit(solution)/shard_map/all_to_all | solution.py:371
  543.3 31.7 %reduce-scatter.11.cloned.1.call-done = bf16[336,768]{1,0:T(8,128)(2,1)} async-done(((bf16[2688,768]{1,0:T(8,128)(2,1)}), bf16[336,768]{1,0:T(8,128)(2,1)}) %reduce-scatter.11.cloned.1.call-update) | async-done | bytes 516112 | tf_op jit(solution)/shard_map/reduce_scatter | solution.py:323
  (259 shorter events, 111.4 us)
Async XLA Ops:
  7.2 152.7 %copy-start = (bf16[768,768]{1,0:T(8,128)(2,1)S(1)}, bf16[768,768]{1,0:T(8,128)(2,1)}, u32[]{:S(2)}) copy-start(bf16[768,768]{1,0:T(8,128)(2,1)} %param.29) | copy-start | bytes 3538948
  7.2 55.1 %all-gather.8.cloned.1.call-start = ((), (), s32[]{:S(2)}) async-start(), calls=%async_computation.6 | async-start | bytes 2949120 | tf_op jit(solution)/shard_map/all_gather | solution.py:130
  7.9 85.0 %all-gather.14.cloned.1.call-start = ((), (), s32[]{:S(2)}) async-start(), calls=%async_computation.13 | async-start | bytes 1474560 | tf_op jit(solution)/shard_map/all_gather | solution.py:138
  10.9 68.6 %copy-start.9 = (pred[3,512,512]{1,2,0:T(8,128)(4,1)}, pred[3,512,512]{1,2,0:T(8,128)(4,1)S(1)}, u32[]{:S(2)}) copy-start(pred[3,512,512]{1,2,0:T(8,128)(4,1)S(1)} %broadcast_compare_fusion) | copy-start | bytes 2359300
  84.7 22.3 %copy-start.18 = (bf16[384,768]{1,0:T(8,128)(2,1)S(1)}, bf16[384,768]{1,0:T(8,128)(2,1)}, u32[]{:S(2)}) copy-start(bf16[384,768]{1,0:T(8,128)(2,1)} %param.20) | copy-start | bytes 1769476
  84.8 22.3 %copy-start.51 = (f32[768]{0:T(1024)S(1)}, f32[768]{0:T(1024)}, u32[]{:S(2)}) copy-start(f32[768]{0:T(1024)} %param.26) | copy-start | bytes 9220
  85.3 21.0 %copy-start.2 = (bf16[3,512,3,64]{1,0,3,2:T(4,128)(2,1)}, bf16[3,512,3,64]{1,0,3,2:T(4,128)(2,1)S(1)}, u32[]{:S(2)}) copy-start(bf16[3,512,3,64]{1,0,3,2:T(4,128)(2,1)S(1)} %copy.136) | copy-start | bytes 1769476
  86.8 19.4 %all-to-all-start = ((bf16[4,384,192]{1,2,0:T(8,128)(2,1)}), bf16[4,384,192]{1,2,0:T(8,128)(2,1)S(1)}, u32[]{:S(2)}, u32[]{:S(2)}) async-start(bf16[4,384,192]{1,2,0:T(8,128)(2,1)} %copy.137), calls=%async_computation | async-start | bytes 1179648 | tf_op jit(solution)/shard_map/all_to_all | solution.py:140
  90.3 69.6 %all-gather.10.cloned.1.call-start = ((), (), s32[]{:S(2)}) async-start(), calls=%async_computation.7 | async-start | bytes 2949120 | tf_op jit(solution)/shard_map/all_gather | solution.py:153
  109.6 116.3 %copy-start.31 = (f32[384]{0:T(512)}, f32[384]{0:T(512)S(1)}, u32[]{:S(2)}) copy-start(f32[384]{0:T(512)S(1)} %add_rsqrt_fusion.1) | copy-start | bytes 4612
  110.7 65.1 %copy-start.49 = (bf16[768,768]{1,0:T(8,128)(2,1)S(1)}, bf16[768,768]{1,0:T(8,128)(2,1)}, u32[]{:S(2)}) copy-start(bf16[768,768]{1,0:T(8,128)(2,1)} %param.31) | copy-start | bytes 3538948
  110.7 115.2 %reduce-scatter.5.cloned.1.call-start = ((), (), s32[]{:S(2)}) async-start(), calls=%async_computation.8 | async-start | bytes 2949120 | tf_op jit(solution)/shard_map/reduce_scatter | solution.py:158
  179.3 106.0 %all-gather.12.cloned.1.call-start = ((), (), s32[]{:S(2)}) async-start(), calls=%async_computation.9 | async-start | bytes 2949120 | tf_op jit(solution)/shard_map/all_gather | solution.py:200
  179.4 48.4 %copy-start.34 = (s32[384]{0:T(512)}, s32[384]{0:T(512)S(1)}, u32[]{:S(2)}) copy-start(s32[384]{0:T(512)S(1)} %iota_add_fusion) | copy-start | bytes 4612
  180.9 49.0 %copy-start.7 = (bf16[768,768]{1,0:T(8,128)(2,1)S(1)}, bf16[768,768]{1,0:T(8,128)(2,1)}, u32[]{:S(2)}) copy-start(bf16[768,768]{1,0:T(8,128)(2,1)} %param.35) | copy-start | bytes 3538948
  235.8 109.9 %reduce-scatter.7.cloned.1.call-start = ((), (), s32[]{:S(2)}) async-start(), calls=%async_computation.10 | async-start | bytes 2949120 | tf_op jit(solution)/shard_map/reduce_scatter | solution.py:211
  299.1 112.7 %all-gather.16.cloned.1.call-start = ((), (), s32[]{:S(2)}) async-start(), calls=%async_computation.14 | async-start | bytes 3317760 | tf_op jit(solution)/shard_map/all_gather | solution.py:271
  300.6 47.5 %copy-start.29 = (f32[768]{0:T(1024)S(1)}, f32[768]{0:T(1024)}, u32[]{:S(2)}) copy-start(f32[768]{0:T(1024)} %param.27) | copy-start | bytes 9220
  350.5 6.6 %copy-start.25 = (f32[3,3,512]{2,1,0:T(4,128)S(1)}, f32[3,3,512]{2,1,0:T(4,128)}, u32[]{:S(2)}) copy-start(f32[3,3,512]{2,1,0:T(4,128)} %copy-done.24) | copy-start | bytes 55300
  350.5 6.6 %copy-start.27 = (f32[3,3,512]{2,1,0:T(4,128)S(1)}, f32[3,3,512]{2,1,0:T(4,128)}, u32[]{:S(2)}) copy-start(f32[3,3,512]{2,1,0:T(4,128)} %copy-done.26) | copy-start | bytes 55300
  357.0 184.3 %reduce-scatter.9.cloned.1.call-start = ((), (), s32[]{:S(2)}) async-start(), calls=%async_computation.11 | async-start | bytes 2949120 | tf_op jit(solution)/shard_map/reduce_scatter | solution.py:305
  428.9 16.2 %copy-start.16 = (bf16[3,512,3,64]{1,0,3,2:T(4,128)(2,1)S(1)}, bf16[3,512,3,64]{1,0,3,2:T(4,128)(2,1)}, u32[]{:S(2)}) copy-start(bf16[3,512,3,64]{1,0,3,2:T(4,128)(2,1)} %convert_element_type.264) | copy-start | bytes 1769476
  428.9 16.2 %copy-start.33 = (f32[3,3,512]{2,1,0:T(4,128)S(1)}, f32[3,3,512]{2,1,0:T(4,128)}, u32[]{:S(2)}) copy-start(f32[3,3,512]{2,1,0:T(4,128)} %log_add_fusion) | copy-start | bytes 55300
  474.6 100.3 %reduce-scatter.11.cloned.1.call-start = ((), (), s32[]{:S(2)}) async-start(), calls=%async_computation.12 | async-start | bytes 4644864 | tf_op jit(solution)/shard_map/reduce_scatter | solution.py:323
  (42 other events, 109.4 us)
Sparse Core Ops, SparseCore 0:
  9.6 52.6 all-gather.7
  63.9 29.0 all-gather.13
  110.8 49.0 all-gather.9
  179.4 46.4 reduce-scatter.4
  235.9 49.3 all-gather.11
  299.3 46.4 reduce-scatter.6
  357.1 54.6 all-gather.15
  474.7 46.4 reduce-scatter.8
  524.7 50.2 reduce-scatter.10

commit v9 on v8

--- a/solution.py
+++ b/solution.py
@@ -79,7 +79,7 @@
         "rqhe,rkhe->rhqk", grad_heads, value_heads, preferred_element_type=jnp.float32
     )
     grad_scores = soft_probs * (grad_soft - jnp.sum(soft_probs * grad_soft, axis=-1, keepdims=True))
-    grad_low = jnp.where(allowed, grad_scores, 0.0).astype(jnp.bfloat16)
+    grad_low = lax.optimization_barrier(jnp.where(allowed, grad_scores, 0.0).astype(jnp.bfloat16))
     score_scale = HEAD ** (-0.5)
     grad_queries = (
         jnp.einsum("rhqk,rkhe->rqhe", grad_low, key_heads, preferred_element_type=jnp.float32)
@@ -129,10 +129,13 @@
 
     gathered = lax.all_gather(inputs, "tensor", axis=0, tiled=True)
     group_rows = gathered.shape[0]
-    projected = jnp.einsum("td,kde->kte", gathered, qkv_weight, preferred_element_type=jnp.float32)
-    queries = (projected[0] + qv_bias[0]).astype(jnp.bfloat16)
-    key_rows = projected[1].astype(jnp.bfloat16)
-    value_rows = (projected[2] + qv_bias[1]).astype(jnp.bfloat16)
+
+    def project(which):
+        return jnp.dot(gathered, qkv_weight[which], preferred_element_type=jnp.float32)
+
+    queries = (project(0) + qv_bias[0]).astype(jnp.bfloat16)
+    key_rows = project(1).astype(jnp.bfloat16)
+    value_rows = (project(2) + qv_bias[1]).astype(jnp.bfloat16)
     local_width = queries.shape[1]
 
     out_weight_all = lax.all_gather(out_weight, "tensor", axis=0, tiled=False)
@@ -258,27 +261,30 @@
         ),
         row_block,
     ]
-    small_flat = joined(token_parts)
+    small_flat = token_parts[0].reshape(-1)
     small_round = lax.reduce_precision(small_flat, exponent_bits=8, mantissa_bits=7)
     small_high = small_round.astype(jnp.bfloat16)
     small_low = (small_flat - small_round).astype(jnp.bfloat16)
-    small_rows = -(-2 * small_flat.size // model_width)
+    rows_low = row_block.reshape(-1).astype(jnp.bfloat16)
+    riding_size = 2 * small_flat.size + rows_low.size
+    small_rows = -(-riding_size // model_width)
     small_rows += (-(share_rows + small_rows)) % 16
-    small_pad = small_rows * model_width - 2 * small_flat.size
+    small_pad = small_rows * model_width - riding_size
     riding = jnp.concatenate(
-        [small_high, small_low, jnp.zeros((small_pad,), jnp.bfloat16)]
+        [small_high, small_low, rows_low, jnp.zeros((small_pad,), jnp.bfloat16)]
     ).reshape(small_rows, model_width)
     att_gathered = lax.all_gather(
         jnp.concatenate([grad_att, riding], axis=0), "tensor", axis=0, tiled=False
     )
     grad_att_all = att_gathered[:, :share_rows].reshape(group_rows, model_width)
-    small_back = att_gathered[:, share_rows:].reshape(tensor_count, -1)
-    small_total = jnp.sum(
-        small_back[:, : small_flat.size].astype(jnp.float32)
-        + small_back[:, small_flat.size : 2 * small_flat.size].astype(jnp.float32),
-        axis=0,
-    )
-    token_sum, rows_group = parted(small_total, token_parts)
+    small_back = att_gathered[:, share_rows:].reshape(tensor_count, -1).astype(jnp.float32)
+    token_size = small_flat.size
+    token_sum = jnp.sum(
+        small_back[:, :token_size] + small_back[:, token_size : 2 * token_size], axis=0
+    ).reshape(token_parts[0].shape)
+    rows_group = jnp.sum(
+        small_back[:, 2 * token_size : 2 * token_size + rows_low.size], axis=0
+    ).reshape(row_block.shape)
     out_weight_grad_t = jnp.einsum(
         "td,te->de", grad_att_all, context, preferred_element_type=jnp.float32
     )

time: 600 us -> 572 us (0.953)
  local copies, waits for them, and re-layouts: 63.9 us -> 44.2 us
  matrix products: 113 us -> 95.5 us
  waiting for transfers between devices: 336 us -> 350 us
    dot_general x1, matrix products: 16.2 us -> 1.54 us  [attend_backward(): jnp.einsum('rhqk,rqhe->rkhe', grad_low, query_heads, preferred_element_ty...]
    sub x0 -> x1, matrix products: none -> 13.8 us  [attend_backward(): grad_soft - jnp.sum(soft_probs * grad_soft, axis=-1, keepdims=True)]
    dot_general x1, matrix products: 15.8 us -> 3.47 us  [attend_backward(): jnp.einsum('rhqk,rkhe->rqhe', grad_low, key_heads, preferred_element_type...]
    reduce_scatter x1, waiting for transfers between devices: 31.7 us -> 41.6 us  [stacked_sum(): lax.psum_scatter(flat.reshape(-1, lanes), 'dp', scatter_dimension=0, tile...]
    unnamed x124 -> x132, local copies, waits for them, and re-layouts: 22.8 us -> 19.6 us
  transfers between devices with their start and end apart: 10 -> 10, of which waited for: 9 -> 9; matrix products, arithmetic and copies ran while one was open for 11% -> 9% of each run, Pallas kernels for 0% -> 0%
where the time goes in v9:
time: 572 us; the launch traced here: 563 us
  waiting for transfers between devices  350 us (61%)
  matrix products  95.5 us (17%)
  local copies, waits for them, and re-layouts  44.2 us (8%)
  blocking collectives  30.4 us (5%)
  other arithmetic  24.2 us (4%)
  between operations  15 us (3%)
    all_gather x1, waiting for transfers between devices, body(): lax.all_gather(jnp.concatenate([grad_att, riding], axis=0), 'tensor', axi...  52.4 us
    all_gather x1, waiting for transfers between devices, body(): gathered = lax.all_gather(inputs, 'tensor', axis=0, tiled=True)  51.6 us
    all_gather x1, waiting for transfers between devices, body(): grad_fed_all = lax.all_gather(grad_fed, 'tensor', axis=0, tiled=True)  49.3 us
    all_gather x1, waiting for transfers between devices, body(): first_all = lax.all_gather(first_low, 'tensor', axis=0, tiled=True)  48.9 us
    reduce_scatter x1, waiting for transfers between devices, body(): lax.psum_scatter(jnp.dot(active, down_weight, preferred_element_type=jnp....  44.9 us
    reduce_scatter x1, waiting for transfers between devices, body(): lax.psum_scatter(jnp.einsum('tf,df->td', grad_up, up_weight, preferred_el...  43.5 us
    reduce_scatter x1, waiting for transfers between devices, stacked_sum(): lax.psum_scatter(flat.reshape(-1, lanes), 'dp', scatter_dimension=0, tile...  41.6 us
    all_to_all x1, blocking collectives, body(): lax.all_to_all(jnp.concatenate(late_parts, axis=1), 'dp', 0, 0, tiled=False)  30.4 us
  transfers between devices with their start and end apart: 10, of which 9 were waited for; matrix products, arithmetic and copies ran while one was open for 9% of the time, Pallas kernels for 0%

profile of v9, /device:TPU:0, one launch (start us, length us, event | category | flops | bytes accessed | tf_op | source)
XLA Modules:
  0.0 563.4 jit_solution(4205286017027712571)
XLA Ops:
  10.7 51.6 %all-gather.8.cloned.1.call-done = bf16[1536,768]{1,0:T(8,128)(2,1)} async-done(((bf16[384,768]{1,0:T(8,128)(2,1)}), bf16[1536,768]{1,0:T(8,128)(2,1)}) %all-gather.8.cloned.1.call-update) | async-done | bytes 2359312 | tf_op jit(solution)/shard_map/all_gather | solution.py:130
  62.3 2.6 fusion.22
  65.4 3.7 convolution_convert_fusion.3
  70.5 3.7 fusion.21
  82.2 3.0 fusion.46
  87.3 3.5 all-to-all-start
  93.0 13.8 %all-to-all-done = bf16[4,384,192]{1,2,0:T(8,128)(2,1)S(1)} async-done(((bf16[4,384,192]{1,2,0:T(8,128)(2,1)}), bf16[4,384,192]{1,2,0:T(8,128)(2,1)S(1)}, u32[]{:S(2)}, u32[]{:S(2)}) %all-to-all-start) | async-done | bytes 589856 | tf_op jit(solution)/shard_map/all_to_all | solution.py:143
  111.6 48.9 %all-gather.10.cloned.1.call-done = bf16[1536,768]{1,0:T(8,128)(2,1)} async-done(((bf16[384,768]{1,0:T(8,128)(2,1)}), bf16[1536,768]{1,0:T(8,128)(2,1)}) %all-gather.10.cloned.1.call-update) | async-done | bytes 2359312 | tf_op jit(solution)/shard_map/all_gather | solution.py:156
  160.5 14.4 %multiply_convert_fusion = (bf16[1536,768]{1,0:T(8,128)(2,1)S(1)}, f32[1536,768]{1,0:T(8,128)}, f32[1536,768]{1,0:T(8,128)}) fusion(f32[768]{0:T(1024)} %param.30, bf16[1536,768]{1,0:T(8,128)(2,1)} %all-gather.10.cloned.1.call-done, bf16[768,768]{1,0:T(8,128)(2,1)S(1)} %copy-done), kind=kOutput, calls=%fused_computation.16 | convolution fusion | flops 1889796096 | bytes 15338496 | tf_op jit(solution)/shard_map/dot_general | solution.py:157
  176.4 3.4 convolution_convert_fusion.1
  181.6 44.9 %reduce-scatter.5.cloned.1.call-done = bf16[384,768]{1,0:T(8,128)(2,1)} async-done(((bf16[1536,768]{1,0:T(8,128)(2,1)}), bf16[384,768]{1,0:T(8,128)(2,1)}) %reduce-scatter.5.cloned.1.call-update) | async-done | bytes 589840 | tf_op jit(solution)/shard_map/reduce_scatter | solution.py:161
  236.6 49.3 %all-gather.12.cloned.1.call-done = bf16[1536,768]{1,0:T(8,128)(2,1)} async-done(((bf16[384,768]{1,0:T(8,128)(2,1)}), bf16[1536,768]{1,0:T(8,128)(2,1)}) %all-gather.12.cloned.1.call-update) | async-done | bytes 2359312 | tf_op jit(solution)/shard_map/all_gather | solution.py:203
  285.9 8.7 %fusion.112 = (bf16[768]{0:T(1024)(128)(2,1)}, bf16[1536,768]{1,0:T(8,128)(2,1)S(1)}) fusion(f32[1536,768]{1,0:T(8,128)} %get-tuple-element.116, f32[1536,768]{1,0:T(8,128)} %get-tuple-element.134, f32[768]{0:T(1024)} %param.30, bf16[1536,768]{1,0:T(8,128)(2,1)} %all-gather.12.cloned.1.call-done, bf16[768,768]{1,0:T(8,128)(2,1)} %param.31), kind=kOutput, calls=%fused_computation.206 | convolution fusion | flops 1830812928 | bytes 15340032 | tf_op jit(solution)/shard_map/td,fd->tf/dot_general | solution.py:207
  296.1 3.5 convolution_convert_fusion
  302.8 43.5 %reduce-scatter.7.cloned.1.call-done = bf16[384,768]{1,0:T(8,128)(2,1)} async-done(((bf16[1536,768]{1,0:T(8,128)(2,1)}), bf16[384,768]{1,0:T(8,128)(2,1)}) %reduce-scatter.7.cloned.1.call-update) | async-done | bytes 589840 | tf_op jit(solution)/shard_map/reduce_scatter | solution.py:214
  353.5 52.4 %all-gather.16.cloned.1.call-done = bf16[1664,768]{1,0:T(8,128)(2,1)} async-done(((bf16[416,768]{1,0:T(8,128)(2,1)}), bf16[1664,768]{1,0:T(8,128)(2,1)}) %all-gather.16.cloned.1.call-update) | async-done | bytes 2555920 | tf_op jit(solution)/shard_map/all_gather | solution.py:276
  411.0 13.8 %select_convert_fusion = bf16[3,3,512,512]{2,3,1,0:T(8,128)(2,1)} fusion(f32[3,3,512,512]{2,3,1,0:T(8,128)} %copy-done.3, f32[3,3,512]{2,1,0:T(4,128)S(1)} %log_add_fusion, pred[3,512,512]{1,2,0:T(8,128)(4,1)S(1)} %copy-done.9, bf16[3,512,3,64]{1,0,3,2:T(4,128)(2,1)S(1)} %reshape.263, bf16[3,512,3,64]{1,0,3,2:T(4,128)(2,1)S(1)} %copy-done.18), kind=kOutput, calls=%fused_computation.1 | convolution fusion | flops 629937152 | bytes 16140288 | tf_op jit(solution)/shard_map/sub | solution.py:81
  424.8 3.5 convert_reduce_fusion.1
  430.3 6.4 %convert_reduce_fusion = (f32[3,64]{1,0:T(4,128)S(1)}, bf16[3,3,64,512]{3,2,1,0:T(8,128)(2,1)S(1)}) fusion(f32[3,3,512,512]{2,3,1,0:T(8,128)} %copy-done.3, f32[3,3,512]{2,1,0:T(4,128)S(1)} %log_add_fusion, pred[3,512,512]{1,2,0:T(8,128)(4,1)S(1)} %copy-done.9, bf16[3,512,3,64]{1,0,3,2:T(4,128)(2,1)S(1)} %reshape.263), kind=kOutput, calls=%fused_computation.73 | convolution fusion | flops 312311616 | bytes 11422464 | tf_op jit(solution)/shard_map/rhqk,rqhe->rkhe/dot_general | solution.py:72
  442.2 5.0 bitcast_convert_fusion
  448.5 4.6 convolution_convert_fusion.5
  466.5 2.8 fusion.34
  471.6 30.4 %all_to_all.10 = f32[8,97,576]{2,1,0:T(8,128)S(1)} all-to-all(f32[8,97,576]{2,1,0:T(8,128)S(1)} %pad_maximum_fusion), channel_id=1, replica_groups=mesh['dp'=8,'tensor'=4] {'dp'}, dimensions={0} | all-to-all | bytes 3575808 | tf_op jit(solution)/shard_map/all_to_all | solution.py:377
  506.0 41.6 %reduce-scatter.11.cloned.1.call-done = bf16[336,768]{1,0:T(8,128)(2,1)} async-done(((bf16[2688,768]{1,0:T(8,128)(2,1)}), bf16[336,768]{1,0:T(8,128)(2,1)}) %reduce-scatter.11.cloned.1.call-update) | async-done | bytes 516112 | tf_op jit(solution)/shard_map/reduce_scatter | solution.py:329
  (261 shorter events, 89.5 us)
Async XLA Ops:
  7.2 153.3 %copy-start = (bf16[768,768]{1,0:T(8,128)(2,1)S(1)}, bf16[768,768]{1,0:T(8,128)(2,1)}, u32[]{:S(2)}) copy-start(bf16[768,768]{1,0:T(8,128)(2,1)} %param.29) | copy-start | bytes 3538948
  7.2 55.1 %all-gather.8.cloned.1.call-start = ((), (), s32[]{:S(2)}) async-start(), calls=%async_computation.6 | async-start | bytes 2949120 | tf_op jit(solution)/shard_map/all_gather | solution.py:130
  7.9 85.1 %all-gather.14.cloned.1.call-start = ((), (), s32[]{:S(2)}) async-start(), calls=%async_computation.13 | async-start | bytes 1474560 | tf_op jit(solution)/shard_map/all_gather | solution.py:141
  10.7 69.8 %copy-start.8 = (pred[3,512,512]{1,2,0:T(8,128)(4,1)}, pred[3,512,512]{1,2,0:T(8,128)(4,1)S(1)}, u32[]{:S(2)}) copy-start(pred[3,512,512]{1,2,0:T(8,128)(4,1)S(1)} %broadcast_compare_fusion) | copy-start | bytes 2359300
  65.4 10.9 %copy-start.10 = (bf16[3,512,3,64]{1,0,3,2:T(4,128)(2,1)}, bf16[3,512,3,64]{1,0,3,2:T(4,128)(2,1)S(1)}, u32[]{:S(2)}) copy-start(bf16[3,512,3,64]{1,0,3,2:T(4,128)(2,1)S(1)} %reshape.258) | copy-start | bytes 1769476
  70.5 5.8 %copy-start.12 = (bf16[3,512,3,64]{1,0,3,2:T(4,128)(2,1)}, bf16[3,512,3,64]{1,0,3,2:T(4,128)(2,1)S(1)}, u32[]{:S(2)}) copy-start(bf16[3,512,3,64]{1,0,3,2:T(4,128)(2,1)S(1)} %reshape.259) | copy-start | bytes 1769476
  85.2 22.5 %copy-start.19 = (bf16[384,768]{1,0:T(8,128)(2,1)S(1)}, bf16[384,768]{1,0:T(8,128)(2,1)}, u32[]{:S(2)}) copy-start(bf16[384,768]{1,0:T(8,128)(2,1)} %param.20) | copy-start | bytes 1769476
  85.2 22.5 %copy-start.56 = (f32[768]{0:T(1024)S(1)}, f32[768]{0:T(1024)}, u32[]{:S(2)}) copy-start(f32[768]{0:T(1024)} %param.26) | copy-start | bytes 9220
  85.8 21.1 %copy-start.4 = (bf16[3,512,3,64]{1,0,3,2:T(4,128)(2,1)}, bf16[3,512,3,64]{1,0,3,2:T(4,128)(2,1)S(1)}, u32[]{:S(2)}) copy-start(bf16[3,512,3,64]{1,0,3,2:T(4,128)(2,1)S(1)} %copy.138) | copy-start | bytes 1769476
  87.3 19.6 %all-to-all-start = ((bf16[4,384,192]{1,2,0:T(8,128)(2,1)}), bf16[4,384,192]{1,2,0:T(8,128)(2,1)S(1)}, u32[]{:S(2)}, u32[]{:S(2)}) async-start(bf16[4,384,192]{1,2,0:T(8,128)(2,1)} %copy.139), calls=%async_computation | async-start | bytes 1179648 | tf_op jit(solution)/shard_map/all_to_all | solution.py:143
  90.8 69.7 %all-gather.10.cloned.1.call-start = ((), (), s32[]{:S(2)}) async-start(), calls=%async_computation.7 | async-start | bytes 2949120 | tf_op jit(solution)/shard_map/all_gather | solution.py:156
  110.2 116.3 %copy-start.25 = (f32[384]{0:T(512)}, f32[384]{0:T(512)S(1)}, u32[]{:S(2)}) copy-start(f32[384]{0:T(512)S(1)} %add_rsqrt_fusion.1) | copy-start | bytes 4612
  111.3 65.1 %copy-start.53 = (bf16[768,768]{1,0:T(8,128)(2,1)S(1)}, bf16[768,768]{1,0:T(8,128)(2,1)}, u32[]{:S(2)}) copy-start(bf16[768,768]{1,0:T(8,128)(2,1)} %param.31) | copy-start | bytes 3538948
  111.3 115.2 %reduce-scatter.5.cloned.1.call-start = ((), (), s32[]{:S(2)}) async-start(), calls=%async_computation.8 | async-start | bytes 2949120 | tf_op jit(solution)/shard_map/reduce_scatter | solution.py:161
  179.9 106.0 %all-gather.12.cloned.1.call-start = ((), (), s32[]{:S(2)}) async-start(), calls=%async_computation.9 | async-start | bytes 2949120 | tf_op jit(solution)/shard_map/all_gather | solution.py:203
  181.6 48.3 %copy-start.6 = (bf16[768,768]{1,0:T(8,128)(2,1)S(1)}, bf16[768,768]{1,0:T(8,128)(2,1)}, u32[]{:S(2)}) copy-start(bf16[768,768]{1,0:T(8,128)(2,1)} %param.35) | copy-start | bytes 3538948
  236.4 109.9 %reduce-scatter.7.cloned.1.call-start = ((), (), s32[]{:S(2)}) async-start(), calls=%async_computation.10 | async-start | bytes 2949120 | tf_op jit(solution)/shard_map/reduce_scatter | solution.py:214
  299.6 46.7 %copy-start.26 = (f32[384]{0:T(512)S(1)}, f32[384]{0:T(512)}, u32[]{:S(2)}) copy-start(f32[384]{0:T(512)} %copy-done.25) | copy-start | bytes 4612
  299.6 106.3 %all-gather.16.cloned.1.call-start = ((), (), s32[]{:S(2)}) async-start(), calls=%async_computation.14 | async-start | bytes 3194880 | tf_op jit(solution)/shard_map/all_gather | solution.py:276
  352.7 151.1 %reduce-scatter.9.cloned.1.call-start = ((), (), s32[]{:S(2)}) async-start(), calls=%async_computation.11 | async-start | bytes 2949120 | tf_op jit(solution)/shard_map/reduce_scatter | solution.py:311
  411.0 13.8 %copy-start.13 = (bf16[3,512,3,64]{1,0,3,2:T(4,128)(2,1)S(1)}, bf16[3,512,3,64]{1,0,3,2:T(4,128)(2,1)}, u32[]{:S(2)}) copy-start(bf16[3,512,3,64]{1,0,3,2:T(4,128)(2,1)} %copy-done.12) | copy-start | bytes 1769476
  447.2 100.3 %reduce-scatter.11.cloned.1.call-start = ((), (), s32[]{:S(2)}) async-start(), calls=%async_computation.12 | async-start | bytes 4644864 | tf_op jit(solution)/shard_map/reduce_scatter | solution.py:329
  448.5 5.7 %copy-start.59 = (bf16[1536,768]{1,0:T(8,128)(2,1)S(1)}, bf16[1536,768]{1,0:T(8,128)(2,1)}, u32[]{:S(2)}) copy-start(bf16[1536,768]{1,0:T(8,128)(2,1)} %copy-done.58) | copy-start | bytes 7077892
  503.8 52.8 %copy-start.1 = (bf16[768,768]{1,0:T(8,128)(2,1)S(1)}, bf16[768,768]{1,0:T(8,128)(2,1)}, u32[]{:S(2)}) copy-start(bf16[768,768]{1,0:T(8,128)(2,1)} %param.29) | copy-start | bytes 3538948
  (47 other events, 101.6 us)
Sparse Core Ops, SparseCore 0:
  9.6 52.6 all-gather.7
  63.9 29.0 all-gather.13
  111.4 49.0 all-gather.9
  180.0 46.4 reduce-scatter.4
  236.5 49.3 all-gather.11
  299.7 46.4 reduce-scatter.6
  352.8 53.0 all-gather.15
  447.3 46.4 reduce-scatter.8
  497.3 50.2 reduce-scatter.10

commit v10 on v9

--- a/solution.py
+++ b/solution.py
@@ -122,7 +122,6 @@
     share_rows = inputs.shape[0]
     seq_count, seq_length = segments.shape
     tensor_index = lax.axis_index("tensor")
-    dp_index = lax.axis_index("dp")
     tensor_count = lax.axis_size("tensor")
     dp_count = lax.axis_size("dp")
     offset = tensor_index * share_rows
@@ -344,45 +343,37 @@
         flat = jnp.pad(flat, (0, rows * lanes - flat.size)).reshape(1, rows, lanes)
         return jnp.broadcast_to(flat, (dp_count, rows, lanes))
 
-    copied_rows = dp_count * dp_count * rows_group.size <= (1 << 20)
     out_blocks = in_blocks(out_weight_grad_t).reshape(dp_count, -1, model_width)
-    early_shared = [token_sum, up_bias_grad]
-    early_parts = [
-        in_blocks(up_weight_grad),
-        in_blocks(down_weight_grad_t),
-        out_blocks,
-        copied(joined(early_shared), model_width),
-    ]
-    if copied_rows:
-        rows_slotted = lax.dynamic_update_slice(
-            jnp.zeros((dp_count,) + rows_group.shape, rows_group.dtype),
-            rows_group[None],
-            (dp_index, 0, 0, 0),
-        )
-        early_parts.append(copied(rows_slotted.reshape(-1), model_width))
-    else:
-        rows_each = lax.all_gather(rows_group.astype(jnp.bfloat16), "dp", axis=0, tiled=False)
+    early_parts = [in_blocks(up_weight_grad), in_blocks(down_weight_grad_t), out_blocks]
     early_sums = stacked_sum(early_parts, jnp.bfloat16)
     up_sum = early_sums[0].astype(jnp.float32)
     down_sum = early_sums[1].astype(jnp.float32).T
     out_sum = early_sums[2].reshape(-1, out_weight_grad_t.shape[1]).astype(jnp.float32).T
-    token_grads, up_bias_total = parted(
-        early_sums[3].reshape(-1).astype(jnp.float32), early_shared
-    )
-    if copied_rows:
-        rows_each = early_sums[4].reshape(-1)[: rows_slotted.size]
-    late_shared = [qv_bias_grad]
+    late_shared = [qv_bias_grad, token_sum, up_bias_grad]
     qkv_lanes = qkv_weight_grad.shape[1]
-    late_parts = [in_blocks(qkv_weight_grad), copied(joined(late_shared), qkv_lanes)]
+
+    def aligned(part):
+        return jnp.pad(part, ((0, 0), (0, (-part.shape[1]) % 8), (0, 0)))
+
+    late_parts = [
+        aligned(in_blocks(qkv_weight_grad)),
+        aligned(copied(joined(late_shared), qkv_lanes)),
+        aligned(copied(rows_group.reshape(-1), qkv_lanes)),
+    ]
     late_received = lax.all_to_all(
         jnp.concatenate(late_parts, axis=1), "dp", 0, 0, tiled=False
     )
-    late_total = jnp.sum(late_received, axis=0)
-    late_sums = [late_total[: late_parts[0].shape[1]], late_total[late_parts[0].shape[1] :]]
+    qkv_rows = in_blocks(qkv_weight_grad).shape[1]
+    shared_begin = late_parts[0].shape[1]
+    rows_begin = shared_begin + late_parts[1].shape[1]
+    late_total = jnp.sum(late_received[:, :rows_begin], axis=0)
     qkv_sum = jnp.transpose(
-        late_sums[0].reshape(late_sums[0].shape[0], 3, qkv_lanes // 3), (1, 0, 2)
-    ).astype(jnp.float32)
-    (qv_bias_total,) = parted(late_sums[1].reshape(-1).astype(jnp.float32), late_shared)
+        late_total[:qkv_rows].reshape(qkv_rows, 3, qkv_lanes // 3), (1, 0, 2)
+    )
+    qv_bias_total, token_grads, up_bias_total = parted(
+        late_total[shared_begin:].reshape(-1), late_shared
+    )
+    rows_each = late_received[:, rows_begin:].reshape(dp_count, -1)[:, : rows_group.size]
     rows_all = rows_each.reshape(dp_count * seq_count, 4, model_width).astype(jnp.bfloat16)
     leading_all = rows_all[:, 0]
     grad_pre_all = rows_all[:, 1]

time: 572 us -> 532 us (0.930)
  waiting for transfers between devices: 350 us -> 303 us
    reduce_scatter x1, waiting for transfers between devices: 41.6 us -> 0.01 us  [stacked_sum(): lax.psum_scatter(flat.reshape(-1, lanes), 'dp', scatter_dimension=0, tile...]
    all_gather x1, waiting for transfers between devices: 52.4 us -> 44.6 us  [body(): lax.all_gather(jnp.concatenate([grad_att, riding], axis=0), 'tensor', axi...]
    unnamed x132 -> x139, local copies, waits for them, and re-layouts: 19.6 us -> 14.5 us
  transfers between devices with their start and end apart: 10 -> 10, of which waited for: 9 -> 8; matrix products, arithmetic and copies ran while one was open for 9% -> 19% of each run, Pallas kernels for 0% -> 0%
where the time goes in v10:
time: 532 us; the launch traced here: 523 us
  waiting for transfers between devices  303 us (57%)
  matrix products  99 us (19%)
  local copies, waits for them, and re-layouts  41.9 us (8%)
  blocking collectives  33.1 us (6%)
  other arithmetic  26.1 us (5%)
  between operations  15 us (3%)
    all_gather x1, waiting for transfers between devices, body(): gathered = lax.all_gather(inputs, 'tensor', axis=0, tiled=True)  51.6 us
    all_gather x1, waiting for transfers between devices, body(): grad_fed_all = lax.all_gather(grad_fed, 'tensor', axis=0, tiled=True)  49.3 us
    all_gather x1, waiting for transfers between devices, body(): first_all = lax.all_gather(first_low, 'tensor', axis=0, tiled=True)  48.7 us
    reduce_scatter x1, waiting for transfers between devices, body(): lax.psum_scatter(jnp.einsum('tf,df->td', grad_up, up_weight, preferred_el...  45.8 us
    reduce_scatter x1, waiting for transfers between devices, body(): lax.psum_scatter(jnp.dot(active, down_weight, preferred_element_type=jnp....  44.9 us
    all_gather x1, waiting for transfers between devices, body(): lax.all_gather(jnp.concatenate([grad_att, riding], axis=0), 'tensor', axi...  44.6 us
    all_to_all x1, blocking collectives, body(): lax.all_to_all(jnp.concatenate(late_parts, axis=1), 'dp', 0, 0, tiled=False)  33.1 us
    unnamed x139, local copies, waits for them, and re-layouts  14.5 us
  transfers between devices with their start and end apart: 10, of which 8 were waited for; matrix products, arithmetic and copies ran while one was open for 19% of the time, Pallas kernels for 0%

profile of v10, /device:TPU:0, one launch (start us, length us, event | category | flops | bytes accessed | tf_op | source)
XLA Modules:
  0.0 523.1 jit_solution(6113853195363155711)
XLA Ops:
  10.7 51.6 %all-gather.8.cloned.1.call-done = bf16[1536,768]{1,0:T(8,128)(2,1)} async-done(((bf16[384,768]{1,0:T(8,128)(2,1)}), bf16[1536,768]{1,0:T(8,128)(2,1)}) %all-gather.8.cloned.1.call-update) | async-done | bytes 2359312 | tf_op jit(solution)/shard_map/all_gather | solution.py:129
  65.4 2.9 fusion.25
  69.4 3.5 convolution_convert_fusion.3
  80.2 3.0 fusion.50
  85.3 3.5 all-to-all-start
  88.9 4.3 all-gather.14.cloned.1.call-done
  93.2 12.4 %all-to-all-done = bf16[4,384,192]{1,2,0:T(8,128)(2,1)S(1)} async-done(((bf16[4,384,192]{1,2,0:T(8,128)(2,1)}), bf16[4,384,192]{1,2,0:T(8,128)(2,1)S(1)}, u32[]{:S(2)}, u32[]{:S(2)}) %all-to-all-start) | async-done | bytes 589856 | tf_op jit(solution)/shard_map/all_to_all | solution.py:142
  110.3 48.7 %all-gather.10.cloned.1.call-done = bf16[1536,768]{1,0:T(8,128)(2,1)} async-done(((bf16[384,768]{1,0:T(8,128)(2,1)}), bf16[1536,768]{1,0:T(8,128)(2,1)}) %all-gather.10.cloned.1.call-update) | async-done | bytes 2359312 | tf_op jit(solution)/shard_map/all_gather | solution.py:155
  159.0 14.5 %multiply_convert_fusion = (bf16[1536,768]{1,0:T(8,128)(2,1)S(1)}, f32[1536,768]{1,0:T(8,128)}, f32[1536,768]{1,0:T(8,128)}) fusion(f32[768]{0:T(1024)} %param.30, bf16[1536,768]{1,0:T(8,128)(2,1)} %all-gather.10.cloned.1.call-done, bf16[768,768]{1,0:T(8,128)(2,1)S(1)} %copy-done), kind=kOutput, calls=%fused_computation.19 | convolution fusion | flops 1889796096 | bytes 15338496 | tf_op jit(solution)/shard_map/dot_general | solution.py:156
  174.9 3.4 convolution_convert_fusion.1
  180.1 44.9 %reduce-scatter.5.cloned.1.call-done = bf16[384,768]{1,0:T(8,128)(2,1)} async-done(((bf16[1536,768]{1,0:T(8,128)(2,1)}), bf16[384,768]{1,0:T(8,128)(2,1)}) %reduce-scatter.5.cloned.1.call-update) | async-done | bytes 589840 | tf_op jit(solution)/shard_map/reduce_scatter | solution.py:160
  235.1 49.3 %all-gather.12.cloned.1.call-done = bf16[1536,768]{1,0:T(8,128)(2,1)} async-done(((bf16[384,768]{1,0:T(8,128)(2,1)}), bf16[1536,768]{1,0:T(8,128)(2,1)}) %all-gather.12.cloned.1.call-update) | async-done | bytes 2359312 | tf_op jit(solution)/shard_map/all_gather | solution.py:202
  284.4 8.7 %convert_reduce_fusion = (f32[768]{0:T(1024)}, bf16[1536,768]{1,0:T(8,128)(2,1)S(1)}) fusion(f32[1536,768]{1,0:T(8,128)} %get-tuple-element.109, f32[1536,768]{1,0:T(8,128)} %get-tuple-element.133, f32[768]{0:T(1024)} %param.30, bf16[1536,768]{1,0:T(8,128)(2,1)} %all-gather.12.cloned.1.call-done, bf16[768,768]{1,0:T(8,128)(2,1)} %param.31), kind=kOutput, calls=%fused_computation.16 | convolution fusion | flops 1831992576 | bytes 15341568 | tf_op jit(solution)/shard_map/td,fd->tf/dot_general | solution.py:206
  294.6 3.5 convolution_convert_fusion
  299.0 45.8 %reduce-scatter.7.cloned.1.call-done = bf16[384,768]{1,0:T(8,128)(2,1)} async-done(((bf16[1536,768]{1,0:T(8,128)(2,1)}), bf16[384,768]{1,0:T(8,128)(2,1)}) %reduce-scatter.7.cloned.1.call-update) | async-done | bytes 589840 | tf_op jit(solution)/shard_map/reduce_scatter | solution.py:213
  352.3 4.6 convolution_convert_fusion.4
  359.0 44.6 %all-gather.16.cloned.1.call-done = bf16[1664,768]{1,0:T(8,128)(2,1)} async-done(((bf16[416,768]{1,0:T(8,128)(2,1)}), bf16[1664,768]{1,0:T(8,128)(2,1)}) %all-gather.16.cloned.1.call-update) | async-done | bytes 2555920 | tf_op jit(solution)/shard_map/all_gather | solution.py:275
  415.6 14.4 %select_convert_fusion = bf16[3,3,512,512]{2,3,1,0:T(8,128)(2,1)} fusion(f32[3,3,512,512]{2,3,1,0:T(8,128)} %copy-done.2, f32[3,3,512]{2,1,0:T(4,128)} %log_add_fusion, pred[3,512,512]{1,2,0:T(8,128)(4,1)S(1)} %copy-done.8, bf16[3,512,3,64]{1,0,3,2:T(4,128)(2,1)S(1)} %reshape.247, bf16[3,512,3,64]{1,0,3,2:T(4,128)(2,1)S(1)} %copy-done.16), kind=kOutput, calls=%fused_computation.1 | convolution fusion | flops 629937152 | bytes 16140288 | tf_op jit(solution)/shard_map/sub | solution.py:81
  430.0 3.4 convert_reduce_fusion.2
  433.5 6.4 %convert_reduce_fusion.1 = (f32[3,64]{1,0:T(4,128)S(1)}, bf16[3,3,64,512]{3,2,1,0:T(8,128)(2,1)S(1)}) fusion(f32[3,3,512,512]{2,3,1,0:T(8,128)} %copy-done.2, f32[3,3,512]{2,1,0:T(4,128)S(1)} %copy-done.37, pred[3,512,512]{1,2,0:T(8,128)(4,1)S(1)} %copy-done.8, bf16[3,512,3,64]{1,0,3,2:T(4,128)(2,1)S(1)} %copy-done.18), kind=kOutput, calls=%fused_computation.83 | convolution fusion | flops 312311616 | bytes 11422464 | tf_op jit(solution)/shard_map/rhqk,rqhe->rkhe/dot_general | solution.py:72
  441.1 3.9 fusion.49
  449.7 5.0 bitcast_convert_fusion
  463.5 3.5 copy.160
  467.0 33.1 %all_to_all.10 = f32[8,128,576]{1,2,0:T(8,128)S(1)} all-to-all(f32[8,128,576]{1,2,0:T(8,128)} %copy.160), channel_id=1, replica_groups=mesh['dp'=8,'tensor'=4] {'dp'}, dimensions={0} | all-to-all | bytes 4718592 | tf_op jit(solution)/shard_map/all_to_all | solution.py:363
  (266 shorter events, 89.3 us)
Async XLA Ops:
  7.2 151.8 %copy-start = (bf16[768,768]{1,0:T(8,128)(2,1)S(1)}, bf16[768,768]{1,0:T(8,128)(2,1)}, u32[]{:S(2)}) copy-start(bf16[768,768]{1,0:T(8,128)(2,1)} %param.29) | copy-start | bytes 3538948
  7.2 55.1 %all-gather.8.cloned.1.call-start = ((), (), s32[]{:S(2)}) async-start(), calls=%async_computation.6 | async-start | bytes 2949120 | tf_op jit(solution)/shard_map/all_gather | solution.py:129
  7.9 85.3 %all-gather.14.cloned.1.call-start = ((), (), s32[]{:S(2)}) async-start(), calls=%async_computation.13 | async-start | bytes 1474560 | tf_op jit(solution)/shard_map/all_gather | solution.py:140
  10.7 67.9 %copy-start.7 = (pred[3,512,512]{1,2,0:T(8,128)(4,1)}, pred[3,512,512]{1,2,0:T(8,128)(4,1)S(1)}, u32[]{:S(2)}) copy-start(pred[3,512,512]{1,2,0:T(8,128)(4,1)S(1)} %broadcast_compare_fusion) | copy-start | bytes 2359300
  65.4 8.9 %copy-start.9 = (bf16[3,512,3,64]{1,0,3,2:T(4,128)(2,1)}, bf16[3,512,3,64]{1,0,3,2:T(4,128)(2,1)S(1)}, u32[]{:S(2)}) copy-start(bf16[3,512,3,64]{1,0,3,2:T(4,128)(2,1)S(1)} %reshape.242) | copy-start | bytes 1769476
  83.3 23.2 %copy-start.19 = (bf16[384,768]{1,0:T(8,128)(2,1)S(1)}, bf16[384,768]{1,0:T(8,128)(2,1)}, u32[]{:S(2)}) copy-start(bf16[384,768]{1,0:T(8,128)(2,1)} %param.20) | copy-start | bytes 1769476
  83.3 23.1 %copy-start.61 = (f32[768]{0:T(1024)S(1)}, f32[768]{0:T(1024)}, u32[]{:S(2)}) copy-start(f32[768]{0:T(1024)} %param.26) | copy-start | bytes 9220
  83.8 21.8 %copy-start.3 = (bf16[3,512,3,64]{1,0,3,2:T(4,128)(2,1)}, bf16[3,512,3,64]{1,0,3,2:T(4,128)(2,1)S(1)}, u32[]{:S(2)}) copy-start(bf16[3,512,3,64]{1,0,3,2:T(4,128)(2,1)S(1)} %copy.142) | copy-start | bytes 1769476
  85.3 20.3 %all-to-all-start = ((bf16[4,384,192]{1,2,0:T(8,128)(2,1)}), bf16[4,384,192]{1,2,0:T(8,128)(2,1)S(1)}, u32[]{:S(2)}, u32[]{:S(2)}) async-start(bf16[4,384,192]{1,2,0:T(8,128)(2,1)} %copy.143), calls=%async_computation | async-start | bytes 1179648 | tf_op jit(solution)/shard_map/all_to_all | solution.py:142
  88.8 70.2 %all-gather.10.cloned.1.call-start = ((), (), s32[]{:S(2)}) async-start(), calls=%async_computation.7 | async-start | bytes 2949120 | tf_op jit(solution)/shard_map/all_gather | solution.py:155
  109.0 116.1 %copy-start.31 = (f32[384]{0:T(512)}, f32[384]{0:T(512)S(1)}, u32[]{:S(2)}) copy-start(f32[384]{0:T(512)S(1)} %add_rsqrt_fusion.1) | copy-start | bytes 4612
  110.1 64.9 %copy-start.58 = (bf16[768,768]{1,0:T(8,128)(2,1)S(1)}, bf16[768,768]{1,0:T(8,128)(2,1)}, u32[]{:S(2)}) copy-start(bf16[768,768]{1,0:T(8,128)(2,1)} %param.31) | copy-start | bytes 3538948
  110.1 115.0 %reduce-scatter.5.cloned.1.call-start = ((), (), s32[]{:S(2)}) async-start(), calls=%async_computation.8 | async-start | bytes 2949120 | tf_op jit(solution)/shard_map/reduce_scatter | solution.py:160
  178.4 106.0 %all-gather.12.cloned.1.call-start = ((), (), s32[]{:S(2)}) async-start(), calls=%async_computation.9 | async-start | bytes 2949120 | tf_op jit(solution)/shard_map/all_gather | solution.py:202
  180.1 48.3 %copy-start.5 = (bf16[768,768]{1,0:T(8,128)(2,1)S(1)}, bf16[768,768]{1,0:T(8,128)(2,1)}, u32[]{:S(2)}) copy-start(bf16[768,768]{1,0:T(8,128)(2,1)} %param.35) | copy-start | bytes 3538948
  234.9 109.9 %reduce-scatter.7.cloned.1.call-start = ((), (), s32[]{:S(2)}) async-start(), calls=%async_computation.10 | async-start | bytes 2949120 | tf_op jit(solution)/shard_map/reduce_scatter | solution.py:213
  298.1 46.7 %copy-start.32 = (f32[384]{0:T(512)S(1)}, f32[384]{0:T(512)}, u32[]{:S(2)}) copy-start(f32[384]{0:T(512)} %copy-done.31) | copy-start | bytes 4612
  298.2 105.5 %all-gather.16.cloned.1.call-start = ((), (), s32[]{:S(2)}) async-start(), calls=%async_computation.14 | async-start | bytes 3194880 | tf_op jit(solution)/shard_map/all_gather | solution.py:275
  350.4 160.6 %reduce-scatter.11.cloned.1.call-start = ((), (), s32[]{:S(2)}) async-start(), calls=%async_computation.12 | async-start | bytes 3096576 | tf_op jit(solution)/shard_map/reduce_scatter | solution.py:328
  413.0 101.4 %reduce-scatter.9.cloned.1.call-start = ((), (), s32[]{:S(2)}) async-start(), calls=%async_computation.11 | async-start | bytes 2949120 | tf_op jit(solution)/shard_map/reduce_scatter | solution.py:310
  415.6 14.4 %copy-start.13 = (bf16[3,512,3,64]{1,0,3,2:T(4,128)(2,1)S(1)}, bf16[3,512,3,64]{1,0,3,2:T(4,128)(2,1)}, u32[]{:S(2)}) copy-start(bf16[3,512,3,64]{1,0,3,2:T(4,128)(2,1)} %copy-done.12) | copy-start | bytes 1769476
  502.3 5.4 %copy-start.25 = (f32[9216]{0:T(1024)S(1)}, f32[9216]{0:T(1024)}, u32[]{:S(2)}) copy-start(f32[9216]{0:T(1024)} %reshape.252) | copy-start | bytes 110596
  505.0 9.5 %copy-start.6 = (f32[384,768]{1,0:T(8,128)S(1)}, f32[384,768]{1,0:T(8,128)}, u32[]{:S(2)}) copy-start(f32[384,768]{1,0:T(8,128)} %get-tuple-element.105) | copy-start | bytes 3538948
  509.1 7.3 %copy-start.1 = (bf16[768,768]{1,0:T(8,128)(2,1)S(1)}, bf16[768,768]{1,0:T(8,128)(2,1)}, u32[]{:S(2)}) copy-start(bf16[768,768]{1,0:T(8,128)(2,1)} %param.29) | copy-start | bytes 3538948
  (52 other events, 109.5 us)
Sparse Core Ops, SparseCore 0:
  9.6 52.6 all-gather.7
  63.9 29.2 all-gather.13
  110.2 48.7 all-gather.9
  178.5 46.4 reduce-scatter.4
  235.0 49.3 all-gather.11
  298.3 46.4 reduce-scatter.6
  350.5 53.0 all-gather.15
  413.1 42.8 reduce-scatter.10
  458.3 47.6 reduce-scatter.8

commit v11 on v10

--- a/solution.py
+++ b/solution.py
@@ -353,12 +353,15 @@
     qkv_lanes = qkv_weight_grad.shape[1]
 
     def aligned(part):
-        return jnp.pad(part, ((0, 0), (0, (-part.shape[1]) % 8), (0, 0)))
-
+        return jnp.pad(part, ((0, 0), (0, (-part.shape[1]) % 16), (0, 0)))
+
+    shared_flat = joined(late_shared)
+    shared_round = lax.reduce_precision(shared_flat, exponent_bits=8, mantissa_bits=7)
+    shared_pair = jnp.concatenate([shared_round, shared_flat - shared_round]).astype(jnp.bfloat16)
     late_parts = [
-        aligned(in_blocks(qkv_weight_grad)),
-        aligned(copied(joined(late_shared), qkv_lanes)),
-        aligned(copied(rows_group.reshape(-1), qkv_lanes)),
+        aligned(in_blocks(qkv_weight_grad).astype(jnp.bfloat16)),
+        aligned(copied(shared_pair, qkv_lanes)),
+        aligned(copied(rows_group.reshape(-1).astype(jnp.bfloat16), qkv_lanes)),
     ]
     late_received = lax.all_to_all(
         jnp.concatenate(late_parts, axis=1), "dp", 0, 0, tiled=False
@@ -366,13 +369,16 @@
     qkv_rows = in_blocks(qkv_weight_grad).shape[1]
     shared_begin = late_parts[0].shape[1]
     rows_begin = shared_begin + late_parts[1].shape[1]
-    late_total = jnp.sum(late_received[:, :rows_begin], axis=0)
-    qkv_sum = jnp.transpose(
-        late_total[:qkv_rows].reshape(qkv_rows, 3, qkv_lanes // 3), (1, 0, 2)
-    )
-    qv_bias_total, token_grads, up_bias_total = parted(
-        late_total[shared_begin:].reshape(-1), late_shared
-    )
+    qkv_total = jnp.sum(late_received[:, :qkv_rows].astype(jnp.float32), axis=0)
+    qkv_sum = jnp.transpose(qkv_total.reshape(qkv_rows, 3, qkv_lanes // 3), (1, 0, 2))
+    shared_back = late_received[:, shared_begin:rows_begin].reshape(dp_count, -1)
+    shared_back = shared_back.astype(jnp.float32)
+    shared_total = jnp.sum(
+        shared_back[:, : shared_flat.size]
+        + shared_back[:, shared_flat.size : 2 * shared_flat.size],
+        axis=0,
+    )
+    qv_bias_total, token_grads, up_bias_total = parted(shared_total, late_shared)
     rows_each = late_received[:, rows_begin:].reshape(dp_count, -1)[:, : rows_group.size]
     rows_all = rows_each.reshape(dp_count * seq_count, 4, model_width).astype(jnp.bfloat16)
     leading_all = rows_all[:, 0]

time: 532 us -> 521 us (0.979)
  waiting for transfers between devices: 303 us -> 316 us
  local copies, waits for them, and re-layouts: 41.9 us -> 31.5 us
  blocking collectives: 33.1 us -> 23.2 us
    reduce_scatter x1, waiting for transfers between devices: 0.01 us -> 14.1 us  [body(): lax.psum_scatter(jnp.einsum('kte,kde->td', stacked, qkv_weight, preferred...]
    all_to_all x1, blocking collectives: 33.1 us -> 23.2 us  [body(): lax.all_to_all(jnp.concatenate(late_parts, axis=1), 'dp', 0, 0, tiled=False)]
    unnamed x139 -> x126, local copies, waits for them, and re-layouts: 14.5 us -> 12.1 us
  transfers between devices with their start and end apart: 10 -> 10, of which waited for: 8 -> 9; matrix products, arithmetic and copies ran while one was open for 19% -> 17% of each run, Pallas kernels for 0% -> 0%
where the time goes in v11:
time: 521 us; the launch traced here: 513 us
  waiting for transfers between devices  316 us (61%)
  matrix products  96.2 us (18%)
  local copies, waits for them, and re-layouts  31.5 us (6%)
  other arithmetic  26.1 us (5%)
  blocking collectives  23.2 us (4%)
  between operations  15 us (3%)
    all_gather x1, waiting for transfers between devices, body(): gathered = lax.all_gather(inputs, 'tensor', axis=0, tiled=True)  51.6 us
    all_gather x1, waiting for transfers between devices, body(): grad_fed_all = lax.all_gather(grad_fed, 'tensor', axis=0, tiled=True)  49.3 us
    all_gather x1, waiting for transfers between devices, body(): first_all = lax.all_gather(first_low, 'tensor', axis=0, tiled=True)  48.7 us
    reduce_scatter x1, waiting for transfers between devices, body(): lax.psum_scatter(jnp.einsum('tf,df->td', grad_up, up_weight, preferred_el...  45.8 us
    reduce_scatter x1, waiting for transfers between devices, body(): lax.psum_scatter(jnp.dot(active, down_weight, preferred_element_type=jnp....  44.9 us
    all_gather x1, waiting for transfers between devices, body(): lax.all_gather(jnp.concatenate([grad_att, riding], axis=0), 'tensor', axi...  43.5 us
    all_to_all x1, blocking collectives, body(): lax.all_to_all(jnp.concatenate(late_parts, axis=1), 'dp', 0, 0, tiled=False)  23.2 us
    sub x1, matrix products, attend_backward(): grad_soft - jnp.sum(soft_probs * grad_soft, axis=-1, keepdims=True)  15.6 us
  transfers between devices with their start and end apart: 10, of which 9 were waited for; matrix products, arithmetic and copies ran while one was open for 17% of the time, Pallas kernels for 0%

profile of v11, /device:TPU:0, one launch (start us, length us, event | category | flops | bytes accessed | tf_op | source)
XLA Modules:
  0.0 512.7 jit_solution(8799194248279848913)
XLA Ops:
  10.7 51.6 %all-gather.8.cloned.1.call-done = bf16[1536,768]{1,0:T(8,128)(2,1)} async-done(((bf16[384,768]{1,0:T(8,128)(2,1)}), bf16[1536,768]{1,0:T(8,128)(2,1)}) %all-gather.8.cloned.1.call-update) | async-done | bytes 2359312 | tf_op jit(solution)/shard_map/all_gather | solution.py:129
  65.4 2.9 fusion.25
  69.4 3.5 convolution_convert_fusion.3
  80.2 3.0 fusion.55
  85.3 3.5 all-to-all-start
  88.9 4.4 all-gather.14.cloned.1.call-done
  93.2 12.4 %all-to-all-done = bf16[4,384,192]{1,2,0:T(8,128)(2,1)S(1)} async-done(((bf16[4,384,192]{1,2,0:T(8,128)(2,1)}), bf16[4,384,192]{1,2,0:T(8,128)(2,1)S(1)}, u32[]{:S(2)}, u32[]{:S(2)}) %all-to-all-start) | async-done | bytes 589856 | tf_op jit(solution)/shard_map/all_to_all | solution.py:142
  110.3 48.7 %all-gather.10.cloned.1.call-done = bf16[1536,768]{1,0:T(8,128)(2,1)} async-done(((bf16[384,768]{1,0:T(8,128)(2,1)}), bf16[1536,768]{1,0:T(8,128)(2,1)}) %all-gather.10.cloned.1.call-update) | async-done | bytes 2359312 | tf_op jit(solution)/shard_map/all_gather | solution.py:155
  159.0 14.4 %multiply_convert_fusion = (bf16[1536,768]{1,0:T(8,128)(2,1)S(1)}, f32[1536,768]{1,0:T(8,128)}, f32[1536,768]{1,0:T(8,128)}) fusion(f32[768]{0:T(1024)} %param.30, bf16[1536,768]{1,0:T(8,128)(2,1)} %all-gather.10.cloned.1.call-done, bf16[768,768]{1,0:T(8,128)(2,1)S(1)} %copy-done), kind=kOutput, calls=%fused_computation.19 | convolution fusion | flops 1889796096 | bytes 15338496 | tf_op jit(solution)/shard_map/dot_general | solution.py:156
  174.9 3.4 convolution_convert_fusion.1
  180.1 44.9 %reduce-scatter.5.cloned.1.call-done = bf16[384,768]{1,0:T(8,128)(2,1)} async-done(((bf16[1536,768]{1,0:T(8,128)(2,1)}), bf16[384,768]{1,0:T(8,128)(2,1)}) %reduce-scatter.5.cloned.1.call-update) | async-done | bytes 589840 | tf_op jit(solution)/shard_map/reduce_scatter | solution.py:160
  235.1 49.3 %all-gather.12.cloned.1.call-done = bf16[1536,768]{1,0:T(8,128)(2,1)} async-done(((bf16[384,768]{1,0:T(8,128)(2,1)}), bf16[1536,768]{1,0:T(8,128)(2,1)}) %all-gather.12.cloned.1.call-update) | async-done | bytes 2359312 | tf_op jit(solution)/shard_map/all_gather | solution.py:202
  284.3 8.8 %convert_reduce_fusion = (f32[768]{0:T(1024)}, bf16[1536,768]{1,0:T(8,128)(2,1)S(1)}) fusion(f32[1536,768]{1,0:T(8,128)} %get-tuple-element.109, f32[1536,768]{1,0:T(8,128)} %get-tuple-element.135, f32[768]{0:T(1024)} %param.30, bf16[1536,768]{1,0:T(8,128)(2,1)} %all-gather.12.cloned.1.call-done, bf16[768,768]{1,0:T(8,128)(2,1)} %param.31), kind=kOutput, calls=%fused_computation.16 | convolution fusion | flops 1831992576 | bytes 15341568 | tf_op jit(solution)/shard_map/td,fd->tf/dot_general | solution.py:206
  294.6 3.5 convolution_convert_fusion
  299.0 45.8 %reduce-scatter.7.cloned.1.call-done = bf16[384,768]{1,0:T(8,128)(2,1)} async-done(((bf16[1536,768]{1,0:T(8,128)(2,1)}), bf16[384,768]{1,0:T(8,128)(2,1)}) %reduce-scatter.7.cloned.1.call-update) | async-done | bytes 589840 | tf_op jit(solution)/shard_map/reduce_scatter | solution.py:213
  352.2 4.9 convolution_convert_fusion.4
  357.1 3.2 convolution_convert_fusion.5
  360.3 43.5 %all-gather.16.cloned.1.call-done = bf16[1664,768]{1,0:T(8,128)(2,1)} async-done(((bf16[416,768]{1,0:T(8,128)(2,1)}), bf16[1664,768]{1,0:T(8,128)(2,1)}) %all-gather.16.cloned.1.call-update) | async-done | bytes 2555920 | tf_op jit(solution)/shard_map/all_gather | solution.py:275
  408.1 2.8 fusion.24
  415.5 15.6 %select_convert_fusion = bf16[3,3,512,512]{2,3,1,0:T(8,128)(2,1)} fusion(f32[3,3,512,512]{2,3,1,0:T(8,128)} %copy-done.3, f32[3,3,512]{2,1,0:T(4,128)} %log_add_fusion, pred[3,512,512]{1,2,0:T(8,128)(4,1)S(1)} %copy-done.9, bf16[3,512,3,64]{1,0,3,2:T(4,128)(2,1)S(1)} %reshape.270, bf16[3,512,3,64]{1,0,3,2:T(4,128)(2,1)} %reshape.264), kind=kOutput, calls=%fused_computation.1 | convolution fusion | flops 629937152 | bytes 16140288 | tf_op jit(solution)/shard_map/sub | solution.py:81
  431.1 6.6 %convert_reduce_fusion.2 = (f32[3,64]{1,0:T(4,128)S(1)}, bf16[3,3,64,512]{3,2,1,0:T(8,128)(2,1)S(1)}) fusion(f32[3,3,512,512]{2,3,1,0:T(8,128)} %copy-done.3, f32[3,3,512]{2,1,0:T(4,128)S(1)} %copy-done.30, pred[3,512,512]{1,2,0:T(8,128)(4,1)S(1)} %copy-done.9, bf16[3,512,3,64]{1,0,3,2:T(4,128)(2,1)S(1)} %reshape.270), kind=kOutput, calls=%fused_computation.84 | convolution fusion | flops 312311616 | bytes 11422464 | tf_op jit(solution)/shard_map/rhqk,rqhe->rkhe/dot_general | solution.py:72
  445.9 5.2 %bitcast_convert_fusion = bf16[1536,768]{1,0:T(8,128)(2,1)} fusion(bf16[3,768,192]{1,2,0:T(8,128)(2,1)} %param.23, bf16[1,1536,192]{1,2,0:T(8,128)(2,1)} %convert_element_type.319, bf16[1,1536,192]{1,2,0:T(8,128)(2,1)S(1)} %convert_element_type.315, bf16[1,1536,192]{1,2,0:T(8,128)(2,1)} %convert_element_type.312), kind=kOutput, calls=%fused_computation.15 | convolution fusion | flops 1361903616 | bytes 5013504 | tf_op jit(solution)/shard_map/kte,kde->td/dot_general | solution.py:311
  456.0 23.2 %all_to_all.10 = bf16[8,144,576]{2,1,0:T(8,128)(2,1)S(1)} all-to-all(bf16[8,144,576]{2,1,0:T(8,128)(2,1)S(1)} %fusion.39), channel_id=1, replica_groups=mesh['dp'=8,'tensor'=4] {'dp'}, dimensions={0} | all-to-all | bytes 2654208 | tf_op jit(solution)/shard_map/all_to_all | solution.py:366
  489.9 14.1 %reduce-scatter.9.cloned.1.call-done = bf16[384,768]{1,0:T(8,128)(2,1)} async-done(((bf16[1536,768]{1,0:T(8,128)(2,1)}), bf16[384,768]{1,0:T(8,128)(2,1)}) %reduce-scatter.9.cloned.1.call-update) | async-done | bytes 589840 | tf_op jit(solution)/shard_map/reduce_scatter | solution.py:310
  (255 shorter events, 78.7 us)
Async XLA Ops:
  7.2 151.8 %copy-start = (bf16[768,768]{1,0:T(8,128)(2,1)S(1)}, bf16[768,768]{1,0:T(8,128)(2,1)}, u32[]{:S(2)}) copy-start(bf16[768,768]{1,0:T(8,128)(2,1)} %param.29) | copy-start | bytes 3538948
  7.2 55.1 %all-gather.8.cloned.1.call-start = ((), (), s32[]{:S(2)}) async-start(), calls=%async_computation.6 | async-start | bytes 2949120 | tf_op jit(solution)/shard_map/all_gather | solution.py:129
  7.9 85.3 %all-gather.14.cloned.1.call-start = ((), (), s32[]{:S(2)}) async-start(), calls=%async_computation.13 | async-start | bytes 1474560 | tf_op jit(solution)/shard_map/all_gather | solution.py:140
  10.7 67.9 %copy-start.8 = (pred[3,512,512]{1,2,0:T(8,128)(4,1)}, pred[3,512,512]{1,2,0:T(8,128)(4,1)S(1)}, u32[]{:S(2)}) copy-start(pred[3,512,512]{1,2,0:T(8,128)(4,1)S(1)} %broadcast_compare_fusion) | copy-start | bytes 2359300
  65.4 8.9 %copy-start.10 = (bf16[3,512,3,64]{1,0,3,2:T(4,128)(2,1)}, bf16[3,512,3,64]{1,0,3,2:T(4,128)(2,1)S(1)}, u32[]{:S(2)}) copy-start(bf16[3,512,3,64]{1,0,3,2:T(4,128)(2,1)S(1)} %reshape.265) | copy-start | bytes 1769476
  83.3 23.2 %copy-start.16 = (bf16[384,768]{1,0:T(8,128)(2,1)S(1)}, bf16[384,768]{1,0:T(8,128)(2,1)}, u32[]{:S(2)}) copy-start(bf16[384,768]{1,0:T(8,128)(2,1)} %param.20) | copy-start | bytes 1769476
  83.3 23.2 %copy-start.55 = (f32[768]{0:T(1024)S(1)}, f32[768]{0:T(1024)}, u32[]{:S(2)}) copy-start(f32[768]{0:T(1024)} %param.26) | copy-start | bytes 9220
  83.8 21.8 %copy-start.4 = (bf16[3,512,3,64]{1,0,3,2:T(4,128)(2,1)}, bf16[3,512,3,64]{1,0,3,2:T(4,128)(2,1)S(1)}, u32[]{:S(2)}) copy-start(bf16[3,512,3,64]{1,0,3,2:T(4,128)(2,1)S(1)} %copy.137) | copy-start | bytes 1769476
  85.3 20.3 %all-to-all-start = ((bf16[4,384,192]{1,2,0:T(8,128)(2,1)}), bf16[4,384,192]{1,2,0:T(8,128)(2,1)S(1)}, u32[]{:S(2)}, u32[]{:S(2)}) async-start(bf16[4,384,192]{1,2,0:T(8,128)(2,1)} %copy.138), calls=%async_computation | async-start | bytes 1179648 | tf_op jit(solution)/shard_map/all_to_all | solution.py:142
  88.8 70.2 %all-gather.10.cloned.1.call-start = ((), (), s32[]{:S(2)}) async-start(), calls=%async_computation.7 | async-start | bytes 2949120 | tf_op jit(solution)/shard_map/all_gather | solution.py:155
  109.0 116.0 %copy-start.24 = (f32[384]{0:T(512)}, f32[384]{0:T(512)S(1)}, u32[]{:S(2)}) copy-start(f32[384]{0:T(512)S(1)} %add_rsqrt_fusion.1) | copy-start | bytes 4612
  110.1 64.8 %copy-start.52 = (bf16[768,768]{1,0:T(8,128)(2,1)S(1)}, bf16[768,768]{1,0:T(8,128)(2,1)}, u32[]{:S(2)}) copy-start(bf16[768,768]{1,0:T(8,128)(2,1)} %param.31) | copy-start | bytes 3538948
  110.1 114.9 %reduce-scatter.5.cloned.1.call-start = ((), (), s32[]{:S(2)}) async-start(), calls=%async_computation.8 | async-start | bytes 2949120 | tf_op jit(solution)/shard_map/reduce_scatter | solution.py:160
  178.4 106.0 %all-gather.12.cloned.1.call-start = ((), (), s32[]{:S(2)}) async-start(), calls=%async_computation.9 | async-start | bytes 2949120 | tf_op jit(solution)/shard_map/all_gather | solution.py:202
  180.1 48.3 %copy-start.6 = (bf16[768,768]{1,0:T(8,128)(2,1)S(1)}, bf16[768,768]{1,0:T(8,128)(2,1)}, u32[]{:S(2)}) copy-start(bf16[768,768]{1,0:T(8,128)(2,1)} %param.35) | copy-start | bytes 3538948
  234.8 109.9 %reduce-scatter.7.cloned.1.call-start = ((), (), s32[]{:S(2)}) async-start(), calls=%async_computation.10 | async-start | bytes 2949120 | tf_op jit(solution)/shard_map/reduce_scatter | solution.py:213
  298.1 46.7 %copy-start.25 = (f32[384]{0:T(512)S(1)}, f32[384]{0:T(512)}, u32[]{:S(2)}) copy-start(f32[384]{0:T(512)} %copy-done.24) | copy-start | bytes 4612
  298.1 105.6 %all-gather.16.cloned.1.call-start = ((), (), s32[]{:S(2)}) async-start(), calls=%async_computation.14 | async-start | bytes 3194880 | tf_op jit(solution)/shard_map/all_gather | solution.py:275
  350.5 135.9 %reduce-scatter.11.cloned.1.call-start = ((), (), s32[]{:S(2)}) async-start(), calls=%async_computation.12 | async-start | bytes 3096576 | tf_op jit(solution)/shard_map/reduce_scatter | solution.py:328
  410.9 93.1 %reduce-scatter.9.cloned.1.call-start = ((), (), s32[]{:S(2)}) async-start(), calls=%async_computation.11 | async-start | bytes 2949120 | tf_op jit(solution)/shard_map/reduce_scatter | solution.py:310
  415.5 15.6 %copy-start.30 = (f32[3,3,512]{2,1,0:T(4,128)S(1)}, f32[3,3,512]{2,1,0:T(4,128)}, u32[]{:S(2)}) copy-start(f32[3,3,512]{2,1,0:T(4,128)} %log_add_fusion) | copy-start | bytes 55300
  431.1 7.1 %copy-start.13 = (bf16[3,512,3,64]{1,0,3,2:T(4,128)(2,1)S(1)}, bf16[3,512,3,64]{1,0,3,2:T(4,128)(2,1)}, u32[]{:S(2)}) copy-start(bf16[3,512,3,64]{1,0,3,2:T(4,128)(2,1)} %copy-done.12) | copy-start | bytes 1769476
  481.8 22.2 %copy-start.7 = (f32[384,768]{1,0:T(8,128)S(1)}, f32[384,768]{1,0:T(8,128)}, u32[]{:S(2)}) copy-start(f32[384,768]{1,0:T(8,128)} %get-tuple-element.105) | copy-start | bytes 3538948
  484.6 21.5 %copy-start.1 = (bf16[768,768]{1,0:T(8,128)(2,1)S(1)}, bf16[768,768]{1,0:T(8,128)(2,1)}, u32[]{:S(2)}) copy-start(bf16[768,768]{1,0:T(8,128)(2,1)} %param.29) | copy-start | bytes 3538948
  (46 other events, 106.9 us)
Sparse Core Ops, SparseCore 0:
  9.6 52.6 all-gather.7
  63.9 29.2 all-gather.13
  110.2 48.7 all-gather.9
  178.5 46.4 reduce-scatter.4
  234.9 49.3 all-gather.11
  298.2 46.4 reduce-scatter.6
  350.7 53.0 all-gather.15
  411.0 42.8 reduce-scatter.10
  456.3 47.7 reduce-scatter.8

commit v12 on v11

--- a/solution.py
+++ b/solution.py
@@ -306,17 +306,24 @@
             jnp.sum(grad_values.astype(jnp.float32), axis=0),
         ]
     )
-    input_grad = (
-        lax.psum_scatter(
-            jnp.einsum(
-                "kte,kde->td", stacked, qkv_weight, preferred_element_type=jnp.float32
-            ).astype(jnp.bfloat16),
-            "tensor",
-            scatter_dimension=0,
-            tiled=True,
-        ).astype(jnp.float32)
-        + grad_res
+    input_part = jnp.einsum(
+        "kte,kde->td", stacked, qkv_weight, preferred_element_type=jnp.float32
     ).astype(jnp.bfloat16)
+    split_width = (input_part.shape[1] * 3 // 512) * 128
+    summed_half = lax.psum_scatter(
+        input_part[:, :split_width], "tensor", scatter_dimension=0, tiled=True
+    ).astype(jnp.float32)
+    swapped_half = lax.all_to_all(
+        input_part[:, split_width:].reshape(tensor_count, share_rows, -1),
+        "tensor",
+        0,
+        0,
+        tiled=False,
+    )
+    input_sum = jnp.concatenate(
+        [summed_half, jnp.sum(swapped_half.astype(jnp.float32), axis=0)], axis=1
+    )
+    input_grad = (input_sum + grad_res).astype(jnp.bfloat16)
 
     def stacked_sum(parts, dtype):
         padded = [
@@ -343,12 +350,10 @@
         flat = jnp.pad(flat, (0, rows * lanes - flat.size)).reshape(1, rows, lanes)
         return jnp.broadcast_to(flat, (dp_count, rows, lanes))
 
-    out_blocks = in_blocks(out_weight_grad_t).reshape(dp_count, -1, model_width)
-    early_parts = [in_blocks(up_weight_grad), in_blocks(down_weight_grad_t), out_blocks]
+    early_parts = [in_blocks(up_weight_grad), in_blocks(down_weight_grad_t)]
     early_sums = stacked_sum(early_parts, jnp.bfloat16)
     up_sum = early_sums[0].astype(jnp.float32)
     down_sum = early_sums[1].astype(jnp.float32).T
-    out_sum = early_sums[2].reshape(-1, out_weight_grad_t.shape[1]).astype(jnp.float32).T
     late_shared = [qv_bias_grad, token_sum, up_bias_grad]
     qkv_lanes = qkv_weight_grad.shape[1]
 
@@ -358,8 +363,13 @@
     shared_flat = joined(late_shared)
     shared_round = lax.reduce_precision(shared_flat, exponent_bits=8, mantissa_bits=7)
     shared_pair = jnp.concatenate([shared_round, shared_flat - shared_round]).astype(jnp.bfloat16)
+    qkv_lanes = qkv_weight_grad.shape[1]
+    out_flat = in_blocks(out_weight_grad_t).astype(jnp.bfloat16).reshape(dp_count, -1)
+    out_rows = -(-out_flat.shape[1] // qkv_lanes)
+    out_blocks = jnp.pad(out_flat, ((0, 0), (0, out_rows * qkv_lanes - out_flat.shape[1])))
     late_parts = [
         aligned(in_blocks(qkv_weight_grad).astype(jnp.bfloat16)),
+        aligned(out_blocks.reshape(dp_count, out_rows, qkv_lanes)),
         aligned(copied(shared_pair, qkv_lanes)),
         aligned(copied(rows_group.reshape(-1).astype(jnp.bfloat16), qkv_lanes)),
     ]
@@ -367,9 +377,15 @@
         jnp.concatenate(late_parts, axis=1), "dp", 0, 0, tiled=False
     )
     qkv_rows = in_blocks(qkv_weight_grad).shape[1]
-    shared_begin = late_parts[0].shape[1]
-    rows_begin = shared_begin + late_parts[1].shape[1]
+    out_begin = late_parts[0].shape[1]
+    shared_begin = out_begin + late_parts[1].shape[1]
+    rows_begin = shared_begin + late_parts[2].shape[1]
     qkv_total = jnp.sum(late_received[:, :qkv_rows].astype(jnp.float32), axis=0)
+    out_total = jnp.sum(
+        late_received[:, out_begin:shared_begin].reshape(dp_count, -1).astype(jnp.float32),
+        axis=0,
+    )
+    out_sum = out_total[: out_flat.shape[1]].reshape(-1, out_weight_grad_t.shape[1]).T
     qkv_sum = jnp.transpose(qkv_total.reshape(qkv_rows, 3, qkv_lanes // 3), (1, 0, 2))
     shared_back = late_received[:, shared_begin:rows_begin].reshape(dp_count, -1)
     shared_back = shared_back.astype(jnp.float32)

time: 521 us -> 540 us (1.036)
  blocking collectives: 23.2 us -> 0 us
  waiting for transfers between devices: 316 us -> 333 us
  local copies, waits for them, and re-layouts: 31.5 us -> 43.7 us
  starting transfers between devices: 4.64 us -> 12.1 us
    all_to_all x0 -> x2, waiting for transfers between devices: none -> 26.6 us  [the longest x1 18.7 us: body(): lax.all_to_all(jnp.concatenate(late_parts, axis=1), 'dp', 0, 0, tiled=False)]
    all_to_all x1 -> x0, blocking collectives: 23.2 us -> none  [body(): lax.all_to_all(jnp.concatenate(late_parts, axis=1), 'dp', 0, 0, tiled=False)]
    reduce_scatter x1, waiting for transfers between devices: 14.1 us -> 4.67 us  [body(): lax.psum_scatter(input_part[:, :split_width], 'tensor', scatter_dimension...]
    all_to_all x0 -> x2, starting transfers between devices: none -> 7.49 us  [the longest x1 3.75 us: body(): lax.all_to_all(jnp.concatenate(late_parts, axis=1), 'dp', 0, 0, tiled=False)]
    unnamed x126 -> x138, local copies, waits for them, and re-layouts: 12.1 us -> 14.7 us
  transfers between devices with their start and end apart: 10 -> 12, of which waited for: 9 -> 11; matrix products, arithmetic and copies ran while one was open for 17% -> 21% of each run, Pallas kernels for 0% -> 0%
where the time goes in v12:
time: 540 us; the launch traced here: 531 us
  waiting for transfers between devices  333 us (62%)
  matrix products  99.6 us (18%)
  local copies, waits for them, and re-layouts  43.7 us (8%)
  other arithmetic  27.7 us (5%)
  between operations  15.3 us (3%)
  starting transfers between devices  12.1 us (2%)
    all_gather x1, waiting for transfers between devices, body(): gathered = lax.all_gather(inputs, 'tensor', axis=0, tiled=True)  51.6 us
    all_gather x1, waiting for transfers between devices, body(): grad_fed_all = lax.all_gather(grad_fed, 'tensor', axis=0, tiled=True)  49.1 us
    all_gather x1, waiting for transfers between devices, body(): first_all = lax.all_gather(first_low, 'tensor', axis=0, tiled=True)  48.7 us
    reduce_scatter x1, waiting for transfers between devices, body(): lax.psum_scatter(jnp.einsum('tf,df->td', grad_up, up_weight, preferred_el...  45.8 us
    reduce_scatter x1, waiting for transfers between devices, body(): lax.psum_scatter(jnp.dot(active, down_weight, preferred_element_type=jnp....  44.9 us
    all_gather x1, waiting for transfers between devices, body(): lax.all_gather(jnp.concatenate([grad_att, riding], axis=0), 'tensor', axi...  43.2 us
    all_to_all x1, waiting for transfers between devices, body(): lax.all_to_all(jnp.concatenate(late_parts, axis=1), 'dp', 0, 0, tiled=False)  18.7 us
    sub x1, matrix products, attend_backward(): grad_soft - jnp.sum(soft_probs * grad_soft, axis=-1, keepdims=True)  15.8 us
  transfers between devices with their start and end apart: 12, of which 11 were waited for; matrix products, arithmetic and copies ran while one was open for 21% of the time, Pallas kernels for 0%

profile of v12, /device:TPU:0, one launch (start us, length us, event | category | flops | bytes accessed | tf_op | source)
XLA Modules:
  0.0 531.1 jit_solution(7838471547616164172)
XLA Ops:
  10.7 51.6 %all-gather.8.cloned.1.call-done = bf16[1536,768]{1,0:T(8,128)(2,1)} async-done(((bf16[384,768]{1,0:T(8,128)(2,1)}), bf16[1536,768]{1,0:T(8,128)(2,1)}) %all-gather.8.cloned.1.call-update) | async-done | bytes 2359312 | tf_op jit(solution)/shard_map/all_gather | solution.py:129
  69.4 3.5 convolution_convert_fusion.3
  85.3 3.5 all-to-all-start
  88.9 4.4 all-gather.14.cloned.1.call-done
  93.3 12.4 %all-to-all-done = bf16[4,384,192]{1,2,0:T(8,128)(2,1)S(1)} async-done(((bf16[4,384,192]{1,2,0:T(8,128)(2,1)}), bf16[4,384,192]{1,2,0:T(8,128)(2,1)S(1)}, u32[]{:S(2)}, u32[]{:S(2)}) %all-to-all-start) | async-done | bytes 589856 | tf_op jit(solution)/shard_map/all_to_all | solution.py:142
  110.3 48.7 %all-gather.10.cloned.1.call-done = bf16[1536,768]{1,0:T(8,128)(2,1)} async-done(((bf16[384,768]{1,0:T(8,128)(2,1)}), bf16[1536,768]{1,0:T(8,128)(2,1)}) %all-gather.10.cloned.1.call-update) | async-done | bytes 2359312 | tf_op jit(solution)/shard_map/all_gather | solution.py:155
  159.0 14.4 %multiply_convert_fusion = (bf16[1536,768]{1,0:T(8,128)(2,1)S(1)}, f32[1536,768]{1,0:T(8,128)}, f32[1536,768]{1,0:T(8,128)}) fusion(f32[768]{0:T(1024)} %param.30, bf16[1536,768]{1,0:T(8,128)(2,1)} %all-gather.10.cloned.1.call-done, bf16[768,768]{1,0:T(8,128)(2,1)S(1)} %copy-done), kind=kOutput, calls=%fused_computation.19 | convolution fusion | flops 1889796096 | bytes 15338496 | tf_op jit(solution)/shard_map/dot_general | solution.py:156
  174.9 3.4 convolution_convert_fusion.1
  180.1 44.9 %reduce-scatter.5.cloned.1.call-done = bf16[384,768]{1,0:T(8,128)(2,1)} async-done(((bf16[1536,768]{1,0:T(8,128)(2,1)}), bf16[384,768]{1,0:T(8,128)(2,1)}) %reduce-scatter.5.cloned.1.call-update) | async-done | bytes 589840 | tf_op jit(solution)/shard_map/reduce_scatter | solution.py:160
  235.3 49.1 %all-gather.12.cloned.1.call-done = bf16[1536,768]{1,0:T(8,128)(2,1)} async-done(((bf16[384,768]{1,0:T(8,128)(2,1)}), bf16[1536,768]{1,0:T(8,128)(2,1)}) %all-gather.12.cloned.1.call-update) | async-done | bytes 2359312 | tf_op jit(solution)/shard_map/all_gather | solution.py:202
  284.4 8.8 %convert_reduce_fusion = (f32[768]{0:T(1024)}, bf16[1536,768]{1,0:T(8,128)(2,1)S(1)}) fusion(f32[1536,768]{1,0:T(8,128)} %get-tuple-element.109, f32[1536,768]{1,0:T(8,128)} %get-tuple-element.135, f32[768]{0:T(1024)} %param.30, bf16[1536,768]{1,0:T(8,128)(2,1)} %all-gather.12.cloned.1.call-done, bf16[768,768]{1,0:T(8,128)(2,1)} %param.31), kind=kOutput, calls=%fused_computation.16 | convolution fusion | flops 1831992576 | bytes 15341568 | tf_op jit(solution)/shard_map/td,fd->tf/dot_general | solution.py:206
  294.6 3.5 convolution_convert_fusion
  299.0 45.8 %reduce-scatter.7.cloned.1.call-done = bf16[384,768]{1,0:T(8,128)(2,1)} async-done(((bf16[1536,768]{1,0:T(8,128)(2,1)}), bf16[384,768]{1,0:T(8,128)(2,1)}) %reduce-scatter.7.cloned.1.call-update) | async-done | bytes 589840 | tf_op jit(solution)/shard_map/reduce_scatter | solution.py:213
  352.9 3.9 convolution_convert_fusion.4
  360.5 43.2 %all-gather.16.cloned.1.call-done = bf16[1664,768]{1,0:T(8,128)(2,1)} async-done(((bf16[416,768]{1,0:T(8,128)(2,1)}), bf16[1664,768]{1,0:T(8,128)(2,1)}) %all-gather.16.cloned.1.call-update) | async-done | bytes 2555920 | tf_op jit(solution)/shard_map/all_gather | solution.py:275
  413.2 15.8 %select_convert_fusion = bf16[3,3,512,512]{2,3,1,0:T(8,128)(2,1)} fusion(f32[3,3,512,512]{2,3,1,0:T(8,128)} %copy-done.2, f32[3,3,512]{2,1,0:T(4,128)} %log_add_fusion, pred[3,512,512]{1,2,0:T(8,128)(4,1)S(1)} %copy-done.8, bf16[3,512,3,64]{1,0,3,2:T(4,128)(2,1)S(1)} %reshape.282, bf16[3,512,3,64]{1,0,3,2:T(4,128)(2,1)} %reshape.276), kind=kOutput, calls=%fused_computation.1 | convolution fusion | flops 629937152 | bytes 16140288 | tf_op jit(solution)/shard_map/sub | solution.py:81
  432.4 7.3 %convert_reduce_fusion.3 = (f32[3,64]{1,0:T(4,128)S(1)}, bf16[3,3,64,512]{3,2,1,0:T(8,128)(2,1)}) fusion(f32[3,3,512,512]{2,3,1,0:T(8,128)} %copy-done.2, f32[3,3,512]{2,1,0:T(4,128)S(1)} %copy-done.36, pred[3,512,512]{1,2,0:T(8,128)(4,1)S(1)} %copy-done.8, bf16[3,512,3,64]{1,0,3,2:T(4,128)(2,1)S(1)} %reshape.282), kind=kOutput, calls=%fused_computation.85 | convolution fusion | flops 312311616 | bytes 11422464 | tf_op jit(solution)/shard_map/rhqk,rqhe->rkhe/dot_general | solution.py:72
  441.9 3.9 fusion.52
  449.5 3.4 bitcast_convert_fusion
  455.3 3.7 all-to-all-start.1
  471.4 7.9 %all-to-all-done.1 = bf16[4,384,256]{2,1,0:T(8,128)(2,1)S(1)} async-done(((bf16[4,384,256]{2,1,0:T(8,128)(2,1)}), bf16[4,384,256]{2,1,0:T(8,128)(2,1)S(1)}, u32[]{:S(2)}, u32[]{:S(2)}) %all-to-all-start.1) | async-done | bytes 786464 | tf_op jit(solution)/shard_map/all_to_all | solution.py:316
  480.2 3.7 all-to-all-start.2
  488.7 18.7 %all-to-all-done.2 = bf16[8,176,576]{2,1,0:T(8,128)(2,1)S(1)} async-done(((bf16[8,176,576]{2,1,0:T(8,128)(2,1)}), bf16[8,176,576]{2,1,0:T(8,128)(2,1)S(1)}, u32[]{:S(2)}, u32[]{:S(2)}) %all-to-all-start.2) | async-done | bytes 1622048 | tf_op jit(solution)/shard_map/all_to_all | solution.py:376
  517.4 4.7 reduce-scatter.9.cloned.1.call-done
  (274 shorter events, 105.8 us)
Async XLA Ops:
  7.2 151.8 %copy-start = (bf16[768,768]{1,0:T(8,128)(2,1)S(1)}, bf16[768,768]{1,0:T(8,128)(2,1)}, u32[]{:S(2)}) copy-start(bf16[768,768]{1,0:T(8,128)(2,1)} %param.29) | copy-start | bytes 3538948
  7.2 55.1 %all-gather.8.cloned.1.call-start = ((), (), s32[]{:S(2)}) async-start(), calls=%async_computation.7 | async-start | bytes 2949120 | tf_op jit(solution)/shard_map/all_gather | solution.py:129
  7.9 85.3 %all-gather.14.cloned.1.call-start = ((), (), s32[]{:S(2)}) async-start(), calls=%async_computation.14 | async-start | bytes 1474560 | tf_op jit(solution)/shard_map/all_gather | solution.py:140
  10.7 67.9 %copy-start.7 = (pred[3,512,512]{1,2,0:T(8,128)(4,1)}, pred[3,512,512]{1,2,0:T(8,128)(4,1)S(1)}, u32[]{:S(2)}) copy-start(pred[3,512,512]{1,2,0:T(8,128)(4,1)S(1)} %broadcast_compare_fusion) | copy-start | bytes 2359300
  65.4 8.9 %copy-start.11 = (bf16[3,512,3,64]{1,0,3,2:T(4,128)(2,1)}, bf16[3,512,3,64]{1,0,3,2:T(4,128)(2,1)S(1)}, u32[]{:S(2)}) copy-start(bf16[3,512,3,64]{1,0,3,2:T(4,128)(2,1)S(1)} %reshape.277) | copy-start | bytes 1769476
  83.3 23.2 %copy-start.19 = (bf16[384,768]{1,0:T(8,128)(2,1)S(1)}, bf16[384,768]{1,0:T(8,128)(2,1)}, u32[]{:S(2)}) copy-start(bf16[384,768]{1,0:T(8,128)(2,1)} %param.20) | copy-start | bytes 1769476
  83.3 23.2 %copy-start.61 = (f32[768]{0:T(1024)S(1)}, f32[768]{0:T(1024)}, u32[]{:S(2)}) copy-start(f32[768]{0:T(1024)} %param.26) | copy-start | bytes 9220
  83.8 21.8 %copy-start.3 = (bf16[3,512,3,64]{1,0,3,2:T(4,128)(2,1)}, bf16[3,512,3,64]{1,0,3,2:T(4,128)(2,1)S(1)}, u32[]{:S(2)}) copy-start(bf16[3,512,3,64]{1,0,3,2:T(4,128)(2,1)S(1)} %copy.138) | copy-start | bytes 1769476
  85.3 20.3 %all-to-all-start = ((bf16[4,384,192]{1,2,0:T(8,128)(2,1)}), bf16[4,384,192]{1,2,0:T(8,128)(2,1)S(1)}, u32[]{:S(2)}, u32[]{:S(2)}) async-start(bf16[4,384,192]{1,2,0:T(8,128)(2,1)} %copy.139), calls=%async_computation | async-start | bytes 1179648 | tf_op jit(solution)/shard_map/all_to_all | solution.py:142
  88.8 70.2 %all-gather.10.cloned.1.call-start = ((), (), s32[]{:S(2)}) async-start(), calls=%async_computation.8 | async-start | bytes 2949120 | tf_op jit(solution)/shard_map/all_gather | solution.py:155
  109.0 116.0 %copy-start.30 = (f32[384]{0:T(512)}, f32[384]{0:T(512)S(1)}, u32[]{:S(2)}) copy-start(f32[384]{0:T(512)S(1)} %add_rsqrt_fusion.1) | copy-start | bytes 4612
  110.1 64.8 %copy-start.58 = (bf16[768,768]{1,0:T(8,128)(2,1)S(1)}, bf16[768,768]{1,0:T(8,128)(2,1)}, u32[]{:S(2)}) copy-start(bf16[768,768]{1,0:T(8,128)(2,1)} %param.31) | copy-start | bytes 3538948
  110.1 114.9 %reduce-scatter.5.cloned.1.call-start = ((), (), s32[]{:S(2)}) async-start(), calls=%async_computation.9 | async-start | bytes 2949120 | tf_op jit(solution)/shard_map/reduce_scatter | solution.py:160
  178.4 106.0 %all-gather.12.cloned.1.call-start = ((), (), s32[]{:S(2)}) async-start(), calls=%async_computation.10 | async-start | bytes 2949120 | tf_op jit(solution)/shard_map/all_gather | solution.py:202
  180.1 48.3 %copy-start.5 = (bf16[768,768]{1,0:T(8,128)(2,1)S(1)}, bf16[768,768]{1,0:T(8,128)(2,1)}, u32[]{:S(2)}) copy-start(bf16[768,768]{1,0:T(8,128)(2,1)} %param.35) | copy-start | bytes 3538948
  234.8 109.9 %reduce-scatter.7.cloned.1.call-start = ((), (), s32[]{:S(2)}) async-start(), calls=%async_computation.11 | async-start | bytes 2949120 | tf_op jit(solution)/shard_map/reduce_scatter | solution.py:213
  298.1 46.7 %copy-start.31 = (f32[384]{0:T(512)S(1)}, f32[384]{0:T(512)}, u32[]{:S(2)}) copy-start(f32[384]{0:T(512)} %copy-done.30) | copy-start | bytes 4612
  298.1 105.6 %all-gather.16.cloned.1.call-start = ((), (), s32[]{:S(2)}) async-start(), calls=%async_computation.15 | async-start | bytes 3194880 | tf_op jit(solution)/shard_map/all_gather | solution.py:275
  350.5 136.3 %reduce-scatter.11.cloned.1.call-start = ((), (), s32[]{:S(2)}) async-start(), calls=%async_computation.13 | async-start | bytes 2654208 | tf_op jit(solution)/shard_map/reduce_scatter | solution.py:335
  413.2 15.8 %copy-start.14 = (bf16[3,512,3,64]{1,0,3,2:T(4,128)(2,1)S(1)}, bf16[3,512,3,64]{1,0,3,2:T(4,128)(2,1)}, u32[]{:S(2)}) copy-start(bf16[3,512,3,64]{1,0,3,2:T(4,128)(2,1)} %copy-done.13) | copy-start | bytes 1769476
  455.3 24.0 %all-to-all-start.1 = ((bf16[4,384,256]{2,1,0:T(8,128)(2,1)}), bf16[4,384,256]{2,1,0:T(8,128)(2,1)S(1)}, u32[]{:S(2)}, u32[]{:S(2)}) async-start(bf16[4,384,256]{2,1,0:T(8,128)(2,1)} %bitcast.141), calls=%async_computation.4 | async-start | bytes 1572864 | tf_op jit(solution)/shard_map/all_to_all | solution.py:316
  480.2 27.2 %all-to-all-start.2 = ((bf16[8,176,576]{2,1,0:T(8,128)(2,1)}), bf16[8,176,576]{2,1,0:T(8,128)(2,1)S(1)}, u32[]{:S(2)}, u32[]{:S(2)}) async-start(bf16[8,176,576]{2,1,0:T(8,128)(2,1)} %fusion.26), calls=%async_computation.5 | async-start | bytes 3604480 | tf_op jit(solution)/shard_map/all_to_all | solution.py:376
  484.0 38.1 %reduce-scatter.9.cloned.1.call-start = ((), (), s32[]{:S(2)}) async-start(), calls=%async_computation.12 | async-start | bytes 1966080 | tf_op jit(solution)/shard_map/reduce_scatter | solution.py:313
  511.9 11.3 %copy-start.6 = (f32[384,768]{1,0:T(8,128)S(1)}, f32[384,768]{1,0:T(8,128)}, u32[]{:S(2)}) copy-start(f32[384,768]{1,0:T(8,128)} %get-tuple-element.105) | copy-start | bytes 3538948
  (54 other events, 140.6 us)
Sparse Core Ops, SparseCore 0:
  9.6 52.6 all-gather.7
  63.9 29.3 all-gather.13
  110.2 48.7 all-gather.9
  178.5 46.4 reduce-scatter.4
  235.0 49.3 all-gather.11
  298.2 46.4 reduce-scatter.6
  350.6 53.0 all-gather.15
  407.1 41.0 reduce-scatter.10
  487.1 34.9 reduce-scatter.8

commit v13 on v11

--- a/solution.py
+++ b/solution.py
@@ -267,7 +267,7 @@
     rows_low = row_block.reshape(-1).astype(jnp.bfloat16)
     riding_size = 2 * small_flat.size + rows_low.size
     small_rows = -(-riding_size // model_width)
-    small_rows += (-(share_rows + small_rows)) % 16
+    small_rows += (-(share_rows + small_rows)) % 8
     small_pad = small_rows * model_width - riding_size
     riding = jnp.concatenate(
         [small_high, small_low, rows_low, jnp.zeros((small_pad,), jnp.bfloat16)]
@@ -343,12 +343,10 @@
         flat = jnp.pad(flat, (0, rows * lanes - flat.size)).reshape(1, rows, lanes)
         return jnp.broadcast_to(flat, (dp_count, rows, lanes))
 
-    out_blocks = in_blocks(out_weight_grad_t).reshape(dp_count, -1, model_width)
-    early_parts = [in_blocks(up_weight_grad), in_blocks(down_weight_grad_t), out_blocks]
+    early_parts = [in_blocks(up_weight_grad), in_blocks(down_weight_grad_t)]
     early_sums = stacked_sum(early_parts, jnp.bfloat16)
     up_sum = early_sums[0].astype(jnp.float32)
     down_sum = early_sums[1].astype(jnp.float32).T
-    out_sum = early_sums[2].reshape(-1, out_weight_grad_t.shape[1]).astype(jnp.float32).T
     late_shared = [qv_bias_grad, token_sum, up_bias_grad]
     qkv_lanes = qkv_weight_grad.shape[1]
 
@@ -358,8 +356,13 @@
     shared_flat = joined(late_shared)
     shared_round = lax.reduce_precision(shared_flat, exponent_bits=8, mantissa_bits=7)
     shared_pair = jnp.concatenate([shared_round, shared_flat - shared_round]).astype(jnp.bfloat16)
+    qkv_lanes = qkv_weight_grad.shape[1]
+    out_flat = in_blocks(out_weight_grad_t).astype(jnp.bfloat16).reshape(dp_count, -1)
+    out_rows = -(-out_flat.shape[1] // qkv_lanes)
+    out_blocks = jnp.pad(out_flat, ((0, 0), (0, out_rows * qkv_lanes - out_flat.shape[1])))
     late_parts = [
         aligned(in_blocks(qkv_weight_grad).astype(jnp.bfloat16)),
+        aligned(out_blocks.reshape(dp_count, out_rows, qkv_lanes)),
         aligned(copied(shared_pair, qkv_lanes)),
         aligned(copied(rows_group.reshape(-1).astype(jnp.bfloat16), qkv_lanes)),
     ]
@@ -367,9 +370,15 @@
         jnp.concatenate(late_parts, axis=1), "dp", 0, 0, tiled=False
     )
     qkv_rows = in_blocks(qkv_weight_grad).shape[1]
-    shared_begin = late_parts[0].shape[1]
-    rows_begin = shared_begin + late_parts[1].shape[1]
+    out_begin = late_parts[0].shape[1]
+    shared_begin = out_begin + late_parts[1].shape[1]
+    rows_begin = shared_begin + late_parts[2].shape[1]
     qkv_total = jnp.sum(late_received[:, :qkv_rows].astype(jnp.float32), axis=0)
+    out_total = jnp.sum(
+        late_received[:, out_begin:shared_begin].reshape(dp_count, -1).astype(jnp.float32),
+        axis=0,
+    )
+    out_sum = out_total[: out_flat.shape[1]].reshape(-1, out_weight_grad_t.shape[1]).T
     qkv_sum = jnp.transpose(qkv_total.reshape(qkv_rows, 3, qkv_lanes // 3), (1, 0, 2))
     shared_back = late_received[:, shared_begin:rows_begin].reshape(dp_count, -1)
     shared_back = shared_back.astype(jnp.float32)

time: 521 us -> 515 us (0.988)
  blocking collectives: 23.2 us -> 0 us
  waiting for transfers between devices: 316 us -> 324 us
  local copies, waits for them, and re-layouts: 31.5 us -> 37.3 us
    all_to_all x1 -> x0, blocking collectives: 23.2 us -> none  [body(): lax.all_to_all(jnp.concatenate(late_parts, axis=1), 'dp', 0, 0, tiled=False)]
    all_to_all x0 -> x1, waiting for transfers between devices: none -> 21.6 us  [body(): lax.all_to_all(jnp.concatenate(late_parts, axis=1), 'dp', 0, 0, tiled=False)]
    reduce_scatter x1, waiting for transfers between devices: 14.1 us -> 2.12 us  [body(): lax.psum_scatter(jnp.einsum('kte,kde->td', stacked, qkv_weight, preferred...]
    unnamed x126 -> x138, local copies, waits for them, and re-layouts: 12.1 us -> 13.3 us
  transfers between devices with their start and end apart: 10 -> 11, of which waited for: 9 -> 10; matrix products, arithmetic and copies ran while one was open for 17% -> 19% of each run, Pallas kernels for 0% -> 0%
where the time goes in v13:
time: 515 us; the launch traced here: 506 us
  waiting for transfers between devices  324 us (63%)
  matrix products  94.2 us (18%)
  local copies, waits for them, and re-layouts  37.3 us (7%)
  other arithmetic  27 us (5%)
  between operations  15 us (3%)
  starting transfers between devices  8.36 us (2%)
    all_gather x1, waiting for transfers between devices, body(): gathered = lax.all_gather(inputs, 'tensor', axis=0, tiled=True)  51.6 us
    all_gather x1, waiting for transfers between devices, body(): grad_fed_all = lax.all_gather(grad_fed, 'tensor', axis=0, tiled=True)  49.3 us
    all_gather x1, waiting for transfers between devices, body(): first_all = lax.all_gather(first_low, 'tensor', axis=0, tiled=True)  48.7 us
    reduce_scatter x1, waiting for transfers between devices, body(): lax.psum_scatter(jnp.einsum('tf,df->td', grad_up, up_weight, preferred_el...  45.8 us
    reduce_scatter x1, waiting for transfers between devices, body(): lax.psum_scatter(jnp.dot(active, down_weight, preferred_element_type=jnp....  44.9 us
    all_gather x1, waiting for transfers between devices, body(): lax.all_gather(jnp.concatenate([grad_att, riding], axis=0), 'tensor', axi...  42.1 us
    all_to_all x1, waiting for transfers between devices, body(): lax.all_to_all(jnp.concatenate(late_parts, axis=1), 'dp', 0, 0, tiled=False)  21.6 us
    sub x1, matrix products, attend_backward(): grad_soft - jnp.sum(soft_probs * grad_soft, axis=-1, keepdims=True)  15.6 us
  transfers between devices with their start and end apart: 11, of which 10 were waited for; matrix products, arithmetic and copies ran while one was open for 19% of the time, Pallas kernels for 0%

profile of v13, /device:TPU:0, one launch (start us, length us, event | category | flops | bytes accessed | tf_op | source)
XLA Modules:
  0.0 506.3 jit_solution(16779986411135076500)
XLA Ops:
  10.7 51.6 %all-gather.8.cloned.1.call-done = bf16[1536,768]{1,0:T(8,128)(2,1)} async-done(((bf16[384,768]{1,0:T(8,128)(2,1)}), bf16[1536,768]{1,0:T(8,128)(2,1)}) %all-gather.8.cloned.1.call-update) | async-done | bytes 2359312 | tf_op jit(solution)/shard_map/all_gather | solution.py:129
  62.3 2.6 fusion.24
  65.4 2.9 fusion.23
  69.4 3.5 convolution_convert_fusion.3
  80.2 3.0 fusion.53
  85.3 3.5 all-to-all-start
  88.9 4.4 all-gather.14.cloned.1.call-done
  93.2 12.4 %all-to-all-done = bf16[4,384,192]{1,2,0:T(8,128)(2,1)S(1)} async-done(((bf16[4,384,192]{1,2,0:T(8,128)(2,1)}), bf16[4,384,192]{1,2,0:T(8,128)(2,1)S(1)}, u32[]{:S(2)}, u32[]{:S(2)}) %all-to-all-start) | async-done | bytes 589856 | tf_op jit(solution)/shard_map/all_to_all | solution.py:142
  110.3 48.7 %all-gather.10.cloned.1.call-done = bf16[1536,768]{1,0:T(8,128)(2,1)} async-done(((bf16[384,768]{1,0:T(8,128)(2,1)}), bf16[1536,768]{1,0:T(8,128)(2,1)}) %all-gather.10.cloned.1.call-update) | async-done | bytes 2359312 | tf_op jit(solution)/shard_map/all_gather | solution.py:155
  159.0 14.4 %multiply_convert_fusion = (bf16[1536,768]{1,0:T(8,128)(2,1)S(1)}, f32[1536,768]{1,0:T(8,128)}, f32[1536,768]{1,0:T(8,128)}) fusion(f32[768]{0:T(1024)} %param.30, bf16[1536,768]{1,0:T(8,128)(2,1)} %all-gather.10.cloned.1.call-done, bf16[768,768]{1,0:T(8,128)(2,1)S(1)} %copy-done), kind=kOutput, calls=%fused_computation.19 | convolution fusion | flops 1889796096 | bytes 15338496 | tf_op jit(solution)/shard_map/dot_general | solution.py:156
  174.9 3.4 convolution_convert_fusion.1
  180.1 44.9 %reduce-scatter.5.cloned.1.call-done = bf16[384,768]{1,0:T(8,128)(2,1)} async-done(((bf16[1536,768]{1,0:T(8,128)(2,1)}), bf16[384,768]{1,0:T(8,128)(2,1)}) %reduce-scatter.5.cloned.1.call-update) | async-done | bytes 589840 | tf_op jit(solution)/shard_map/reduce_scatter | solution.py:160
  235.1 49.3 %all-gather.12.cloned.1.call-done = bf16[1536,768]{1,0:T(8,128)(2,1)} async-done(((bf16[384,768]{1,0:T(8,128)(2,1)}), bf16[1536,768]{1,0:T(8,128)(2,1)}) %all-gather.12.cloned.1.call-update) | async-done | bytes 2359312 | tf_op jit(solution)/shard_map/all_gather | solution.py:202
  284.4 8.8 %convert_reduce_fusion = (f32[768]{0:T(1024)}, bf16[1536,768]{1,0:T(8,128)(2,1)S(1)}) fusion(f32[1536,768]{1,0:T(8,128)} %get-tuple-element.109, f32[1536,768]{1,0:T(8,128)} %get-tuple-element.135, f32[768]{0:T(1024)} %param.30, bf16[1536,768]{1,0:T(8,128)(2,1)} %all-gather.12.cloned.1.call-done, bf16[768,768]{1,0:T(8,128)(2,1)} %param.31), kind=kOutput, calls=%fused_computation.16 | convolution fusion | flops 1831992576 | bytes 15341568 | tf_op jit(solution)/shard_map/td,fd->tf/dot_general | solution.py:206
  294.6 3.5 convolution_convert_fusion
  299.0 45.8 %reduce-scatter.7.cloned.1.call-done = bf16[384,768]{1,0:T(8,128)(2,1)} async-done(((bf16[1536,768]{1,0:T(8,128)(2,1)}), bf16[384,768]{1,0:T(8,128)(2,1)}) %reduce-scatter.7.cloned.1.call-update) | async-done | bytes 589840 | tf_op jit(solution)/shard_map/reduce_scatter | solution.py:213
  352.7 3.9 convolution_convert_fusion.4
  360.7 42.1 %all-gather.16.cloned.1.call-done = bf16[1632,768]{1,0:T(8,128)(2,1)} async-done(((bf16[408,768]{1,0:T(8,128)(2,1)}), bf16[1632,768]{1,0:T(8,128)(2,1)}) %all-gather.16.cloned.1.call-update) | async-done | bytes 2506768 | tf_op jit(solution)/shard_map/all_gather | solution.py:275
  413.1 15.6 %select_convert_fusion = bf16[3,3,512,512]{2,3,1,0:T(8,128)(2,1)} fusion(f32[3,3,512,512]{2,3,1,0:T(8,128)} %copy-done.3, f32[3,3,512]{2,1,0:T(4,128)S(1)} %copy-done.35, pred[3,512,512]{1,2,0:T(8,128)(4,1)S(1)} %copy-done.9, bf16[3,512,3,64]{1,0,3,2:T(4,128)(2,1)S(1)} %reshape.279, bf16[3,512,3,64]{1,0,3,2:T(4,128)(2,1)} %reshape.273), kind=kOutput, calls=%fused_computation.1 | convolution fusion | flops 629937152 | bytes 16140288 | tf_op jit(solution)/shard_map/sub | solution.py:81
  428.7 6.6 %convert_reduce_fusion.2 = (f32[3,64]{1,0:T(4,128)S(1)}, bf16[3,3,64,512]{3,2,1,0:T(8,128)(2,1)S(1)}) fusion(f32[3,3,512,512]{2,3,1,0:T(8,128)} %copy-done.3, f32[3,3,512]{2,1,0:T(4,128)S(1)} %copy-done.35, pred[3,512,512]{1,2,0:T(8,128)(4,1)S(1)} %copy-done.9, bf16[3,512,3,64]{1,0,3,2:T(4,128)(2,1)S(1)} %reshape.279), kind=kOutput, calls=%fused_computation.82 | convolution fusion | flops 312311616 | bytes 11422464 | tf_op jit(solution)/shard_map/rhqk,rqhe->rkhe/dot_general | solution.py:72
  444.2 3.4 convolution_convert_fusion.6
  447.6 3.5 bitcast_convert_fusion
  458.2 3.7 all-to-all-start.1
  463.8 21.6 %all-to-all-done.1 = bf16[8,176,576]{2,1,0:T(8,128)(2,1)S(1)} async-done(((bf16[8,176,576]{2,1,0:T(8,128)(2,1)}), bf16[8,176,576]{2,1,0:T(8,128)(2,1)S(1)}, u32[]{:S(2)}, u32[]{:S(2)}) %all-to-all-start.1) | async-done | bytes 1622048 | tf_op jit(solution)/shard_map/all_to_all | solution.py:369
  (267 shorter events, 88.3 us)
Async XLA Ops:
  7.2 151.8 %copy-start = (bf16[768,768]{1,0:T(8,128)(2,1)S(1)}, bf16[768,768]{1,0:T(8,128)(2,1)}, u32[]{:S(2)}) copy-start(bf16[768,768]{1,0:T(8,128)(2,1)} %param.29) | copy-start | bytes 3538948
  7.2 55.1 %all-gather.8.cloned.1.call-start = ((), (), s32[]{:S(2)}) async-start(), calls=%async_computation.6 | async-start | bytes 2949120 | tf_op jit(solution)/shard_map/all_gather | solution.py:129
  7.9 85.3 %all-gather.14.cloned.1.call-start = ((), (), s32[]{:S(2)}) async-start(), calls=%async_computation.13 | async-start | bytes 1474560 | tf_op jit(solution)/shard_map/all_gather | solution.py:140
  10.7 67.9 %copy-start.8 = (pred[3,512,512]{1,2,0:T(8,128)(4,1)}, pred[3,512,512]{1,2,0:T(8,128)(4,1)S(1)}, u32[]{:S(2)}) copy-start(pred[3,512,512]{1,2,0:T(8,128)(4,1)S(1)} %broadcast_compare_fusion) | copy-start | bytes 2359300
  65.4 8.9 %copy-start.10 = (bf16[3,512,3,64]{1,0,3,2:T(4,128)(2,1)}, bf16[3,512,3,64]{1,0,3,2:T(4,128)(2,1)S(1)}, u32[]{:S(2)}) copy-start(bf16[3,512,3,64]{1,0,3,2:T(4,128)(2,1)S(1)} %reshape.274) | copy-start | bytes 1769476
  83.3 23.2 %copy-start.16 = (bf16[384,768]{1,0:T(8,128)(2,1)S(1)}, bf16[384,768]{1,0:T(8,128)(2,1)}, u32[]{:S(2)}) copy-start(bf16[384,768]{1,0:T(8,128)(2,1)} %param.20) | copy-start | bytes 1769476
  83.3 23.2 %copy-start.61 = (f32[768]{0:T(1024)S(1)}, f32[768]{0:T(1024)}, u32[]{:S(2)}) copy-start(f32[768]{0:T(1024)} %param.26) | copy-start | bytes 9220
  83.8 21.8 %copy-start.4 = (bf16[3,512,3,64]{1,0,3,2:T(4,128)(2,1)}, bf16[3,512,3,64]{1,0,3,2:T(4,128)(2,1)S(1)}, u32[]{:S(2)}) copy-start(bf16[3,512,3,64]{1,0,3,2:T(4,128)(2,1)S(1)} %copy.138) | copy-start | bytes 1769476
  85.3 20.3 %all-to-all-start = ((bf16[4,384,192]{1,2,0:T(8,128)(2,1)}), bf16[4,384,192]{1,2,0:T(8,128)(2,1)S(1)}, u32[]{:S(2)}, u32[]{:S(2)}) async-start(bf16[4,384,192]{1,2,0:T(8,128)(2,1)} %copy.139), calls=%async_computation | async-start | bytes 1179648 | tf_op jit(solution)/shard_map/all_to_all | solution.py:142
  88.8 70.2 %all-gather.10.cloned.1.call-start = ((), (), s32[]{:S(2)}) async-start(), calls=%async_computation.7 | async-start | bytes 2949120 | tf_op jit(solution)/shard_map/all_gather | solution.py:155
  109.0 116.0 %copy-start.29 = (f32[384]{0:T(512)}, f32[384]{0:T(512)S(1)}, u32[]{:S(2)}) copy-start(f32[384]{0:T(512)S(1)} %add_rsqrt_fusion.1) | copy-start | bytes 4612
  110.1 64.8 %copy-start.57 = (bf16[768,768]{1,0:T(8,128)(2,1)S(1)}, bf16[768,768]{1,0:T(8,128)(2,1)}, u32[]{:S(2)}) copy-start(bf16[768,768]{1,0:T(8,128)(2,1)} %param.31) | copy-start | bytes 3538948
  110.1 114.9 %reduce-scatter.5.cloned.1.call-start = ((), (), s32[]{:S(2)}) async-start(), calls=%async_computation.8 | async-start | bytes 2949120 | tf_op jit(solution)/shard_map/reduce_scatter | solution.py:160
  178.4 106.0 %all-gather.12.cloned.1.call-start = ((), (), s32[]{:S(2)}) async-start(), calls=%async_computation.9 | async-start | bytes 2949120 | tf_op jit(solution)/shard_map/all_gather | solution.py:202
  180.1 48.3 %copy-start.6 = (bf16[768,768]{1,0:T(8,128)(2,1)S(1)}, bf16[768,768]{1,0:T(8,128)(2,1)}, u32[]{:S(2)}) copy-start(bf16[768,768]{1,0:T(8,128)(2,1)} %param.35) | copy-start | bytes 3538948
  234.8 109.9 %reduce-scatter.7.cloned.1.call-start = ((), (), s32[]{:S(2)}) async-start(), calls=%async_computation.10 | async-start | bytes 2949120 | tf_op jit(solution)/shard_map/reduce_scatter | solution.py:213
  298.1 46.7 %copy-start.30 = (f32[384]{0:T(512)S(1)}, f32[384]{0:T(512)}, u32[]{:S(2)}) copy-start(f32[384]{0:T(512)} %copy-done.29) | copy-start | bytes 4612
  298.1 104.8 %all-gather.16.cloned.1.call-start = ((), (), s32[]{:S(2)}) async-start(), calls=%async_computation.14 | async-start | bytes 3133440 | tf_op jit(solution)/shard_map/all_gather | solution.py:275
  350.5 111.5 %reduce-scatter.11.cloned.1.call-start = ((), (), s32[]{:S(2)}) async-start(), calls=%async_computation.12 | async-start | bytes 2654208 | tf_op jit(solution)/shard_map/reduce_scatter | solution.py:328
  360.3 137.3 %reduce-scatter.9.cloned.1.call-start = ((), (), s32[]{:S(2)}) async-start(), calls=%async_computation.11 | async-start | bytes 2949120 | tf_op jit(solution)/shard_map/reduce_scatter | solution.py:310
  428.7 7.2 %copy-start.2 = (bf16[3,3,512,512]{2,3,1,0:T(8,128)(2,1)S(1)}, bf16[3,3,512,512]{2,3,1,0:T(8,128)(2,1)}, u32[]{:S(2)}) copy-start(bf16[3,3,512,512]{2,3,1,0:T(8,128)(2,1)} %select_convert_fusion) | copy-start | bytes 14155780
  428.7 7.2 %copy-start.13 = (bf16[3,512,3,64]{1,0,3,2:T(4,128)(2,1)S(1)}, bf16[3,512,3,64]{1,0,3,2:T(4,128)(2,1)}, u32[]{:S(2)}) copy-start(bf16[3,512,3,64]{1,0,3,2:T(4,128)(2,1)} %copy-done.12) | copy-start | bytes 1769476
  458.2 27.2 %all-to-all-start.1 = ((bf16[8,176,576]{2,1,0:T(8,128)(2,1)}), bf16[8,176,576]{2,1,0:T(8,128)(2,1)S(1)}, u32[]{:S(2)}, u32[]{:S(2)}) async-start(bf16[8,176,576]{2,1,0:T(8,128)(2,1)} %fusion.26), calls=%async_computation.4 | async-start | bytes 3604480 | tf_op jit(solution)/shard_map/all_to_all | solution.py:369
  489.7 7.8 %copy-start.7 = (f32[384,768]{1,0:T(8,128)S(1)}, f32[384,768]{1,0:T(8,128)}, u32[]{:S(2)}) copy-start(f32[384,768]{1,0:T(8,128)} %get-tuple-element.105) | copy-start | bytes 3538948
  (53 other events, 130.8 us)
Sparse Core Ops, SparseCore 0:
  9.6 52.6 all-gather.7
  63.9 29.2 all-gather.13
  110.2 48.7 all-gather.9
  178.5 46.4 reduce-scatter.4
  235.0 49.3 all-gather.11
  298.2 46.4 reduce-scatter.6
  350.6 52.2 all-gather.15
  406.2 41.0 reduce-scatter.10
  451.2 46.2 reduce-scatter.8

commit v14 on v13

--- a/solution.py
+++ b/solution.py
@@ -79,15 +79,15 @@
         "rqhe,rkhe->rhqk", grad_heads, value_heads, preferred_element_type=jnp.float32
     )
     grad_scores = soft_probs * (grad_soft - jnp.sum(soft_probs * grad_soft, axis=-1, keepdims=True))
-    grad_low = lax.optimization_barrier(jnp.where(allowed, grad_scores, 0.0).astype(jnp.bfloat16))
     score_scale = HEAD ** (-0.5)
-    grad_queries = (
-        jnp.einsum("rhqk,rkhe->rqhe", grad_low, key_heads, preferred_element_type=jnp.float32)
-        * score_scale
-    )
-    grad_keys = (
-        jnp.einsum("rhqk,rqhe->rkhe", grad_low, query_heads, preferred_element_type=jnp.float32)
-        * score_scale
+    grad_low = lax.optimization_barrier(
+        jnp.where(allowed, grad_scores, 0.0).astype(jnp.bfloat16) * jnp.bfloat16(score_scale)
+    )
+    grad_queries = jnp.einsum(
+        "rhqk,rkhe->rqhe", grad_low, key_heads, preferred_element_type=jnp.float32
+    )
+    grad_keys = jnp.einsum(
+        "rhqk,rqhe->rkhe", grad_low, query_heads, preferred_element_type=jnp.float32
     )
     full_shape = queries.shape
     return (

time: 515 us -> 539 us (1.047)
  other arithmetic: 27 us -> 51 us
  local copies, waits for them, and re-layouts: 37.3 us -> 50.3 us
  waiting for transfers between devices: 324 us -> 316 us
    sub x0 -> x1, other arithmetic: none -> 17.9 us  [attend_backward(): grad_soft - jnp.sum(soft_probs * grad_soft, axis=-1, keepdims=True)]
    sub x1 -> x0, matrix products: 15.6 us -> none  [attend_backward(): grad_soft - jnp.sum(soft_probs * grad_soft, axis=-1, keepdims=True)]
    reduce_scatter x1, waiting for transfers between devices: 45.8 us -> 39.8 us  [body(): lax.psum_scatter(jnp.einsum('tf,df->td', grad_up, up_weight, preferred_el...]
    unnamed x138 -> x120, local copies, waits for them, and re-layouts: 13.3 us -> 13.3 us
  transfers between devices with their start and end apart: 11 -> 11, of which waited for: 10 -> 9; matrix products, arithmetic and copies ran while one was open for 19% -> 25% of each run, Pallas kernels for 0% -> 0%
where the time goes in v14:
time: 539 us; the launch traced here: 530 us
  waiting for transfers between devices  316 us (59%)
  matrix products  90.1 us (17%)
  other arithmetic  51 us (9%)
  local copies, waits for them, and re-layouts  50.3 us (9%)
  between operations  14.8 us (3%)
  starting transfers between devices  7.82 us (1%)
    all_gather x1, waiting for transfers between devices, body(): gathered = lax.all_gather(inputs, 'tensor', axis=0, tiled=True)  51.6 us
    all_gather x1, waiting for transfers between devices, body(): grad_fed_all = lax.all_gather(grad_fed, 'tensor', axis=0, tiled=True)  49.3 us
    all_gather x1, waiting for transfers between devices, body(): first_all = lax.all_gather(first_low, 'tensor', axis=0, tiled=True)  48.7 us
    reduce_scatter x1, waiting for transfers between devices, body(): lax.psum_scatter(jnp.dot(active, down_weight, preferred_element_type=jnp....  44.9 us
    all_gather x1, waiting for transfers between devices, body(): lax.all_gather(jnp.concatenate([grad_att, riding], axis=0), 'tensor', axi...  41.8 us
    reduce_scatter x1, waiting for transfers between devices, body(): lax.psum_scatter(jnp.einsum('tf,df->td', grad_up, up_weight, preferred_el...  39.8 us
    all_to_all x1, waiting for transfers between devices, body(): lax.all_to_all(jnp.concatenate(late_parts, axis=1), 'dp', 0, 0, tiled=False)  21.6 us
    sub x1, other arithmetic, attend_backward(): grad_soft - jnp.sum(soft_probs * grad_soft, axis=-1, keepdims=True)  17.9 us
  transfers between devices with their start and end apart: 11, of which 9 were waited for; matrix products, arithmetic and copies ran while one was open for 25% of the time, Pallas kernels for 0%

profile of v14, /device:TPU:0, one launch (start us, length us, event | category | flops | bytes accessed | tf_op | source)
XLA Modules:
  0.0 529.8 jit_solution(17238730763566774295)
XLA Ops:
  10.7 51.6 %all-gather.8.cloned.1.call-done = bf16[1536,768]{1,0:T(8,128)(2,1)} async-done(((bf16[384,768]{1,0:T(8,128)(2,1)}), bf16[1536,768]{1,0:T(8,128)(2,1)}) %all-gather.8.cloned.1.call-update) | async-done | bytes 2359312 | tf_op jit(solution)/shard_map/all_gather | solution.py:129
  69.4 3.5 convolution_convert_fusion.3
  85.3 3.5 all-to-all-start
  88.9 4.3 all-gather.14.cloned.1.call-done
  93.2 12.4 %all-to-all-done = bf16[4,384,192]{1,2,0:T(8,128)(2,1)S(1)} async-done(((bf16[4,384,192]{1,2,0:T(8,128)(2,1)}), bf16[4,384,192]{1,2,0:T(8,128)(2,1)S(1)}, u32[]{:S(2)}, u32[]{:S(2)}) %all-to-all-start) | async-done | bytes 589856 | tf_op jit(solution)/shard_map/all_to_all | solution.py:142
  110.3 48.7 %all-gather.10.cloned.1.call-done = bf16[1536,768]{1,0:T(8,128)(2,1)} async-done(((bf16[384,768]{1,0:T(8,128)(2,1)}), bf16[1536,768]{1,0:T(8,128)(2,1)}) %all-gather.10.cloned.1.call-update) | async-done | bytes 2359312 | tf_op jit(solution)/shard_map/all_gather | solution.py:155
  159.0 14.5 %multiply_convert_fusion = (bf16[1536,768]{1,0:T(8,128)(2,1)S(1)}, f32[1536,768]{1,0:T(8,128)}, f32[1536,768]{1,0:T(8,128)}) fusion(f32[768]{0:T(1024)} %param.30, bf16[1536,768]{1,0:T(8,128)(2,1)} %all-gather.10.cloned.1.call-done, bf16[768,768]{1,0:T(8,128)(2,1)S(1)} %copy-done), kind=kOutput, calls=%fused_computation.19 | convolution fusion | flops 1889796096 | bytes 15338496 | tf_op jit(solution)/shard_map/dot_general | solution.py:156
  174.9 3.4 convolution_convert_fusion.1
  180.1 44.9 %reduce-scatter.5.cloned.1.call-done = bf16[384,768]{1,0:T(8,128)(2,1)} async-done(((bf16[1536,768]{1,0:T(8,128)(2,1)}), bf16[384,768]{1,0:T(8,128)(2,1)}) %reduce-scatter.5.cloned.1.call-update) | async-done | bytes 589840 | tf_op jit(solution)/shard_map/reduce_scatter | solution.py:160
  235.1 49.3 %all-gather.12.cloned.1.call-done = bf16[1536,768]{1,0:T(8,128)(2,1)} async-done(((bf16[384,768]{1,0:T(8,128)(2,1)}), bf16[1536,768]{1,0:T(8,128)(2,1)}) %all-gather.12.cloned.1.call-update) | async-done | bytes 2359312 | tf_op jit(solution)/shard_map/all_gather | solution.py:202
  284.4 8.7 %convert_reduce_fusion = (f32[768]{0:T(1024)}, bf16[1536,768]{1,0:T(8,128)(2,1)S(1)}) fusion(f32[1536,768]{1,0:T(8,128)} %get-tuple-element.109, f32[1536,768]{1,0:T(8,128)} %get-tuple-element.135, f32[768]{0:T(1024)} %param.30, bf16[1536,768]{1,0:T(8,128)(2,1)} %all-gather.12.cloned.1.call-done, bf16[768,768]{1,0:T(8,128)(2,1)} %param.31), kind=kOutput, calls=%fused_computation.16 | convolution fusion | flops 1831992576 | bytes 15341568 | tf_op jit(solution)/shard_map/td,fd->tf/dot_general | solution.py:206
  294.6 3.5 convolution_convert_fusion
  304.9 39.8 %reduce-scatter.7.cloned.1.call-done = bf16[384,768]{1,0:T(8,128)(2,1)} async-done(((bf16[1536,768]{1,0:T(8,128)(2,1)}), bf16[384,768]{1,0:T(8,128)(2,1)}) %reduce-scatter.7.cloned.1.call-update) | async-done | bytes 589840 | tf_op jit(solution)/shard_map/reduce_scatter | solution.py:213
  355.2 4.6 convolution_convert_fusion.4
  363.6 41.8 %all-gather.16.cloned.1.call-done = bf16[1632,768]{1,0:T(8,128)(2,1)} async-done(((bf16[408,768]{1,0:T(8,128)(2,1)}), bf16[1632,768]{1,0:T(8,128)(2,1)}) %all-gather.16.cloned.1.call-update) | async-done | bytes 2506768 | tf_op jit(solution)/shard_map/all_gather | solution.py:275
  411.5 8.1 %convert_reduce_fusion.2 = (f32[3,64]{1,0:T(4,128)S(1)}, bf16[3,3,64,512]{3,2,1,0:T(8,128)(2,1)}) fusion(f32[3,3,512,512]{2,3,1,0:T(8,128)} %copy-done.2, f32[3,3,512]{2,1,0:T(4,128)} %log_add_fusion, pred[3,512,512]{1,2,0:T(8,128)(4,1)} %copy-done.7, bf16[3,512,3,64]{1,0,3,2:T(4,128)(2,1)} %reshape.279), kind=kOutput, calls=%fused_computation.81 | convolution fusion | flops 312311616 | bytes 11422464 | tf_op jit(solution)/shard_map/rhqk,rqhe->rkhe/dot_general | solution.py:72
  428.7 5.1 fusion.63
  433.8 17.9 %broadcast_multiply_fusion = bf16[3,3,512,512]{2,3,1,0:T(8,128)(2,1)} fusion(f32[3,3,512,512]{2,3,1,0:T(8,128)} %fusion.63, f32[3,3,512,512]{2,3,1,0:T(8,128)} %copy-done.2, f32[3,3,512]{2,1,0:T(4,128)} %log_add_fusion, pred[3,512,512]{1,2,0:T(8,128)(4,1)S(1)} %copy-done.8), kind=kOutput, calls=%fused_computation.50 | output fusion | flops 35394560 | bytes 24397824 | tf_op jit(solution)/shard_map/sub | solution.py:81
  451.7 3.5 convert_reduce_fusion.3
  461.0 3.5 convolution_convert_fusion.8
  464.5 3.5 bitcast_convert_fusion
  476.5 3.2 fusion.46
  482.1 3.6 all-to-all-start.1
  487.6 21.6 %all-to-all-done.1 = bf16[8,176,576]{2,1,0:T(8,128)(2,1)S(1)} async-done(((bf16[8,176,576]{2,1,0:T(8,128)(2,1)}), bf16[8,176,576]{2,1,0:T(8,128)(2,1)S(1)}, u32[]{:S(2)}, u32[]{:S(2)}) %all-to-all-start.1) | async-done | bytes 1622048 | tf_op jit(solution)/shard_map/all_to_all | solution.py:369
  (250 shorter events, 110.7 us)
Async XLA Ops:
  7.2 151.8 %copy-start = (bf16[768,768]{1,0:T(8,128)(2,1)S(1)}, bf16[768,768]{1,0:T(8,128)(2,1)}, u32[]{:S(2)}) copy-start(bf16[768,768]{1,0:T(8,128)(2,1)} %param.29) | copy-start | bytes 3538948
  7.2 55.1 %all-gather.8.cloned.1.call-start = ((), (), s32[]{:S(2)}) async-start(), calls=%async_computation.6 | async-start | bytes 2949120 | tf_op jit(solution)/shard_map/all_gather | solution.py:129
  7.9 85.3 %all-gather.14.cloned.1.call-start = ((), (), s32[]{:S(2)}) async-start(), calls=%async_computation.13 | async-start | bytes 1474560 | tf_op jit(solution)/shard_map/all_gather | solution.py:140
  10.7 67.9 %copy-start.7 = (pred[3,512,512]{1,2,0:T(8,128)(4,1)}, pred[3,512,512]{1,2,0:T(8,128)(4,1)S(1)}, u32[]{:S(2)}) copy-start(pred[3,512,512]{1,2,0:T(8,128)(4,1)S(1)} %broadcast_compare_fusion) | copy-start | bytes 2359300
  65.4 8.9 %copy-start.9 = (bf16[3,512,3,64]{1,0,3,2:T(4,128)(2,1)}, bf16[3,512,3,64]{1,0,3,2:T(4,128)(2,1)S(1)}, u32[]{:S(2)}) copy-start(bf16[3,512,3,64]{1,0,3,2:T(4,128)(2,1)S(1)} %reshape.274) | copy-start | bytes 1769476
  83.3 23.2 %copy-start.18 = (bf16[384,768]{1,0:T(8,128)(2,1)S(1)}, bf16[384,768]{1,0:T(8,128)(2,1)}, u32[]{:S(2)}) copy-start(bf16[384,768]{1,0:T(8,128)(2,1)} %param.20) | copy-start | bytes 1769476
  83.3 23.1 %copy-start.52 = (f32[768]{0:T(1024)S(1)}, f32[768]{0:T(1024)}, u32[]{:S(2)}) copy-start(f32[768]{0:T(1024)} %param.26) | copy-start | bytes 9220
  83.8 21.8 %copy-start.3 = (bf16[3,512,3,64]{1,0,3,2:T(4,128)(2,1)}, bf16[3,512,3,64]{1,0,3,2:T(4,128)(2,1)S(1)}, u32[]{:S(2)}) copy-start(bf16[3,512,3,64]{1,0,3,2:T(4,128)(2,1)S(1)} %copy.138) | copy-start | bytes 1769476
  85.3 20.3 %all-to-all-start = ((bf16[4,384,192]{1,2,0:T(8,128)(2,1)}), bf16[4,384,192]{1,2,0:T(8,128)(2,1)S(1)}, u32[]{:S(2)}, u32[]{:S(2)}) async-start(bf16[4,384,192]{1,2,0:T(8,128)(2,1)} %copy.139), calls=%async_computation | async-start | bytes 1179648 | tf_op jit(solution)/shard_map/all_to_all | solution.py:142
  88.8 70.2 %all-gather.10.cloned.1.call-start = ((), (), s32[]{:S(2)}) async-start(), calls=%async_computation.7 | async-start | bytes 2949120 | tf_op jit(solution)/shard_map/all_gather | solution.py:155
  109.0 116.1 %copy-start.31 = (f32[384]{0:T(512)}, f32[384]{0:T(512)S(1)}, u32[]{:S(2)}) copy-start(f32[384]{0:T(512)S(1)} %add_rsqrt_fusion.1) | copy-start | bytes 4612
  110.1 64.8 %copy-start.48 = (bf16[768,768]{1,0:T(8,128)(2,1)S(1)}, bf16[768,768]{1,0:T(8,128)(2,1)}, u32[]{:S(2)}) copy-start(bf16[768,768]{1,0:T(8,128)(2,1)} %param.31) | copy-start | bytes 3538948
  110.1 114.9 %reduce-scatter.5.cloned.1.call-start = ((), (), s32[]{:S(2)}) async-start(), calls=%async_computation.8 | async-start | bytes 2949120 | tf_op jit(solution)/shard_map/reduce_scatter | solution.py:160
  178.4 106.0 %all-gather.12.cloned.1.call-start = ((), (), s32[]{:S(2)}) async-start(), calls=%async_computation.9 | async-start | bytes 2949120 | tf_op jit(solution)/shard_map/all_gather | solution.py:202
  180.1 48.3 %copy-start.5 = (bf16[768,768]{1,0:T(8,128)(2,1)S(1)}, bf16[768,768]{1,0:T(8,128)(2,1)}, u32[]{:S(2)}) copy-start(bf16[768,768]{1,0:T(8,128)(2,1)} %param.35) | copy-start | bytes 3538948
  234.9 109.8 %reduce-scatter.7.cloned.1.call-start = ((), (), s32[]{:S(2)}) async-start(), calls=%async_computation.10 | async-start | bytes 2949120 | tf_op jit(solution)/shard_map/reduce_scatter | solution.py:213
  298.1 107.3 %all-gather.16.cloned.1.call-start = ((), (), s32[]{:S(2)}) async-start(), calls=%async_computation.14 | async-start | bytes 3133440 | tf_op jit(solution)/shard_map/all_gather | solution.py:275
  349.4 5.2 copy-start.28
  353.0 132.7 %reduce-scatter.11.cloned.1.call-start = ((), (), s32[]{:S(2)}) async-start(), calls=%async_computation.12 | async-start | bytes 2654208 | tf_op jit(solution)/shard_map/reduce_scatter | solution.py:328
  363.5 157.6 %reduce-scatter.9.cloned.1.call-start = ((), (), s32[]{:S(2)}) async-start(), calls=%async_computation.11 | async-start | bytes 2949120 | tf_op jit(solution)/shard_map/reduce_scatter | solution.py:310
  433.8 18.0 %copy-start.12 = (bf16[3,512,3,64]{1,0,3,2:T(4,128)(2,1)S(1)}, bf16[3,512,3,64]{1,0,3,2:T(4,128)(2,1)}, u32[]{:S(2)}) copy-start(bf16[3,512,3,64]{1,0,3,2:T(4,128)(2,1)} %copy-done.11) | copy-start | bytes 1769476
  468.0 7.4 %copy-start.40 = (f32[768]{0:T(1024)S(1)}, f32[768]{0:T(1024)}, u32[]{:S(2)}) copy-start(f32[768]{0:T(1024)} %get-tuple-element.98) | copy-start | bytes 9220
  482.1 27.0 %all-to-all-start.1 = ((bf16[8,176,576]{2,1,0:T(8,128)(2,1)}), bf16[8,176,576]{2,1,0:T(8,128)(2,1)S(1)}, u32[]{:S(2)}, u32[]{:S(2)}) async-start(bf16[8,176,576]{2,1,0:T(8,128)(2,1)} %fusion.28), calls=%async_computation.4 | async-start | bytes 3604480 | tf_op jit(solution)/shard_map/all_to_all | solution.py:369
  515.4 5.7 %copy-start.6 = (f32[384,768]{1,0:T(8,128)S(1)}, f32[384,768]{1,0:T(8,128)}, u32[]{:S(2)}) copy-start(f32[384,768]{1,0:T(8,128)} %get-tuple-element.105) | copy-start | bytes 3538948
  (44 other events, 122.7 us)
Sparse Core Ops, SparseCore 0:
  9.6 52.6 all-gather.7
  63.9 29.3 all-gather.13
  110.2 48.7 all-gather.9
  178.5 46.4 reduce-scatter.4
  235.0 49.3 all-gather.11
  298.2 46.4 reduce-scatter.6
  353.1 52.2 all-gather.15
  408.7 41.0 reduce-scatter.10
  468.2 45.9 reduce-scatter.8
